TPU v7x, 32 devices: a whole 2x2x4 slice. The times are simulated.
32 devices in a mesh: dom: 8 (over z, y), sub: 4 (over x, core).
Axes of the slice: x: 2, y: 2, z: 4, core: 2. Of those that a mesh axis runs over, the one named last changes fastest.
Arguments:
- source: float32 [32, 7, 16, 1024], P('dom', None, 'sub'), may hold values from -6 to 6
- zone_ids: int32 [32, 1024], P('dom'), may hold values from 0 to 15
- kappa_table: float32 [16, 7], replicated, may hold values from 0.05 to 1
- mu_table: float32 [16, 8], replicated, may hold values from 0.2 to 2
- owner_dev: int32 [8, 32], P('dom'), may hold values from 0 to 7, as said below
- owner_group: int32 [8, 32], P('dom'), may hold values from 0 to 31, as said below
Outputs:
- edge_field: float32 [32, 7, 16, 1024], P('dom', None, 'sub')
- potential: float32 [32, 16, 1024], P('dom', 'sub')
Inputs may be any that keep to these rules, and one draw needn't show every extreme that they name: owner_dev[d, j] is the index along dom of the device that sums slot j of device d; one device sends at most 4 of its slots to one owner, and exactly 4 to some owner. At owner e, receive position d * 4 + c stands for the c-th slot, in slot order, that device d sends to e. owner_group[e, d * 4 + c] is a receive position held alike by all copies of one shared primitive; a primitive has at most four copies, all at one owner; positions that no slot reaches hold their own index.
All inputs are finite; a program needn't handle non-finite values.
Results may differ from a plain program's by a relative error of at most 0.0001.
Values sent between devices are 32-bit elements; how exact they have to be, the bound alone decides.
No kernel may reach another device: no remote copies, remote signals or barrier semaphores. Data moves between devices by JAX's collectives and lax.ppermute only.
A program may use at most 64 MiB of HBM per device.

v0:
```python
import jax
import jax.numpy as jnp
from jax import lax
from jax.sharding import PartitionSpec as P

LAT = 32
SWEEPS = 2


EDGE_OFFSETS = ((0, 0, 1), (0, 1, 0), (1, 0, 0), (0, 1, 1), (1, 0, 1), (1, 1, 0), (1, 1, 1))
FACE_EDGES = (
    (0, 1, 3),
    (1, 0, 3),
    (0, 2, 4),
    (2, 0, 4),
    (1, 2, 5),
    (2, 1, 5),
    (3, 2, 6),
    (2, 3, 6),
)
SHARED_TYPES = (1, 2, 5)
EDGE_DAMPING = 0.6
NODE_DAMPING = 0.8


def with_halo(block, sides, width):
    for axis, dim in sides:
        count = lax.axis_size(axis)
        forward = [(i, i + 1) for i in range(count - 1)]
        backward = [(target, source) for source, target in forward]
        low = lax.ppermute(
            lax.slice_in_dim(block, block.shape[dim] - width, None, axis=dim), axis, forward
        )
        high = lax.ppermute(lax.slice_in_dim(block, 0, width, axis=dim), axis, backward)
        block = jnp.concatenate([low, block, high], axis=dim)
    return block


def from_behind(block, axis, distance):
    devices = range(lax.axis_size(axis))
    route = [(i - distance, i) for i in devices if i - distance in devices]
    return lax.ppermute(block, axis, route)


def shift_ahead(values, rise_y, rise_x):
    offset = rise_y * LAT + rise_x
    if offset == 0:
        return values
    padding = jnp.zeros(values.shape[:-1] + (offset,), values.dtype)
    shifted = jnp.concatenate([values[..., offset:], padding], axis=-1)
    if rise_x:
        column = jnp.arange(values.shape[-1]) % LAT
        shifted = jnp.where(column < LAT - rise_x, shifted, jnp.zeros_like(shifted))
    return shifted


def shift_behind(values, rise_y, rise_x):
    offset = rise_y * LAT + rise_x
    if offset == 0:
        return values
    padding = jnp.zeros(values.shape[:-1] + (offset,), values.dtype)
    shifted = jnp.concatenate([padding, values[..., :-offset]], axis=-1)
    if rise_x:
        column = jnp.arange(values.shape[-1]) % LAT
        shifted = jnp.where(column >= rise_x, shifted, jnp.zeros_like(shifted))
    return shifted


def apply_operator(padded, halo_width, extra_planes, first_plane, mass_coef, curl_coef):
    planes = padded.shape[2] - 2 * halo_width
    face_count = planes + extra_planes + 1
    first_face = halo_width - extra_planes - 1
    face_planes = first_plane - extra_planes - 1 + jnp.arange(face_count)
    face_valid = (face_planes >= 0)[None, :, None]
    result = [
        mass_coef[edge_type][:, None, :]
        * padded[:, edge_type, halo_width - extra_planes : halo_width + planes]
        for edge_type in range(7)
    ]
    for face_index, (first_edge, second_edge, diagonal_edge) in enumerate(FACE_EDGES):
        rise_z, rise_y, rise_x = EDGE_OFFSETS[first_edge]
        far_values = shift_ahead(
            padded[:, second_edge, first_face + rise_z : first_face + rise_z + face_count],
            rise_y,
            rise_x,
        )
        circulation = (
            padded[:, first_edge, first_face : first_face + face_count]
            + far_values
            - padded[:, diagonal_edge, first_face : first_face + face_count]
        )
        weighted = jnp.where(face_valid, curl_coef[face_index][:, None, :] * circulation, 0.0)
        result[first_edge] = result[first_edge] + weighted[:, 1:]
        result[diagonal_edge] = result[diagonal_edge] - weighted[:, 1:]
        result[second_edge] = result[second_edge] + shift_behind(
            weighted[:, 1 - rise_z : 1 - rise_z + planes + extra_planes], rise_y, rise_x
        )
    return jnp.stack(result, axis=1)


def edge_diagonal(mass_coef, curl_coef, first_plane, planes):
    inside = (first_plane + jnp.arange(planes) >= 1)[None, :, None]
    flat_planes = jnp.zeros((1, planes, 1), mass_coef.dtype)
    diagonal = [mass_coef[edge_type][:, None, :] + flat_planes for edge_type in range(7)]
    for face_index, (first_edge, second_edge, diagonal_edge) in enumerate(FACE_EDGES):
        rise_z, rise_y, rise_x = EDGE_OFFSETS[first_edge]
        own_term = curl_coef[face_index][:, None, :]
        diagonal[first_edge] = diagonal[first_edge] + own_term
        diagonal[diagonal_edge] = diagonal[diagonal_edge] + own_term
        behind_term = shift_behind(curl_coef[face_index], rise_y, rise_x)[:, None, :] + flat_planes
        if rise_z:
            behind_term = jnp.where(inside, behind_term, 0.0)
        diagonal[second_edge] = diagonal[second_edge] + behind_term
    return jnp.stack(diagonal, axis=1)


def node_diagonal(mass_coef, first_plane, planes):
    inside = (first_plane + jnp.arange(planes) >= 1)[None, :, None]
    total = jnp.zeros((mass_coef.shape[1], planes, mass_coef.shape[2]), mass_coef.dtype)
    for edge_type in range(7):
        rise_z, rise_y, rise_x = EDGE_OFFSETS[edge_type]
        total = total + mass_coef[edge_type][:, None, :]
        behind_term = shift_behind(mass_coef[edge_type], rise_y, rise_x)[:, None, :] + jnp.zeros(
            (1, planes, 1), mass_coef.dtype
        )
        if rise_z:
            behind_term = jnp.where(inside, behind_term, 0.0)
        total = total + behind_term
    return total


def node_residual(lowered, planes):
    total = jnp.zeros((lowered.shape[0], planes, lowered.shape[3]), lowered.dtype)
    for edge_type in range(7):
        rise_z, rise_y, rise_x = EDGE_OFFSETS[edge_type]
        total = (
            total
            + shift_behind(lowered[:, edge_type, 1 - rise_z : 1 - rise_z + planes], rise_y, rise_x)
            - lowered[:, edge_type, 1:]
        )
    return total


def gradient(raised, planes):
    result = []
    for edge_type in range(7):
        rise_z, rise_y, rise_x = EDGE_OFFSETS[edge_type]
        result.append(
            shift_ahead(raised[:, rise_z : rise_z + planes], rise_y, rise_x) - raised[:, :planes]
        )
    return jnp.stack(result, axis=1)


def edge_sides(values):
    macro_count, type_count, plane_count, cell_count = values.shape
    lattice = values.reshape(macro_count, type_count, plane_count, LAT, LAT)
    chosen = jnp.stack([lattice[:, edge_type] for edge_type in SHARED_TYPES], axis=1)
    sides = jnp.stack([chosen[..., 0], chosen[..., LAT - 1]], axis=1)
    return jnp.transpose(sides, (0, 1, 3, 2, 4)).reshape(-1, 3 * LAT)


def insert_edges(values, blocks):
    macro_count, type_count, plane_count, cell_count = values.shape
    shaped = blocks.reshape(macro_count, 2, plane_count, 3, LAT)
    shaped = jnp.transpose(shaped, (0, 1, 3, 2, 4))
    lattice = values.reshape(macro_count, type_count, plane_count, LAT, LAT)
    for side_index, column in ((0, 0), (1, LAT - 1)):
        for slot_type, edge_type in enumerate(SHARED_TYPES):
            lattice = lattice.at[:, edge_type, :, :, column].set(shaped[:, side_index, slot_type])
    return lattice.reshape(values.shape)


def node_sides(values):
    macro_count, plane_count, cell_count = values.shape
    lattice = values.reshape(macro_count, plane_count, LAT, LAT)
    sides = jnp.stack([lattice[..., 0], lattice[..., LAT - 1]], axis=1)
    return sides.reshape(-1, LAT)


def insert_nodes(values, blocks):
    macro_count, plane_count, cell_count = values.shape
    shaped = blocks.reshape(macro_count, 2, plane_count, LAT)
    lattice = values.reshape(macro_count, plane_count, LAT, LAT)
    for side_index, column in ((0, 0), (1, LAT - 1)):
        lattice = lattice.at[:, :, :, column].set(shaped[:, side_index])
    return lattice.reshape(values.shape)


def local(source, zone_ids, kappa_table, mu_table, owner_dev, owner_group):
    macro_count, type_count, planes, cell_count = source.shape
    first_plane = lax.axis_index("sub") * planes
    onehot = (jnp.arange(kappa_table.shape[0])[:, None] == zone_ids.reshape(1, -1)).astype(
        jnp.float32
    )
    mass_coef = jnp.dot(kappa_table.T, onehot, precision=lax.Precision.HIGHEST).reshape(
        type_count, macro_count, cell_count
    )
    curl_coef = jnp.dot(mu_table.T, onehot, precision=lax.Precision.HIGHEST).reshape(
        mu_table.shape[1], macro_count, cell_count
    )
    peer_count = lax.axis_size("dom")
    recv_rows = owner_group.shape[1]
    capacity = recv_rows // peer_count
    slot_count = owner_dev.shape[1]
    owner_of = owner_dev[0]
    groups = owner_group[0]
    earlier = jnp.arange(slot_count)[None, :] < jnp.arange(slot_count)[:, None]
    position = jnp.sum((owner_of[:, None] == owner_of[None, :]) & earlier, axis=1)
    slot_place = owner_of * capacity + position
    spread = (jnp.arange(recv_rows)[:, None] == slot_place[None, :]).astype(jnp.float32)
    same_group = (groups[:, None] == groups[None, :]).astype(jnp.float32)

    def owner_sum(received):
        summed = jnp.dot(
            same_group, received.reshape(recv_rows, -1), precision=lax.Precision.HIGHEST
        )
        return lax.all_to_all(
            summed.reshape(peer_count, capacity, -1), "dom", split_axis=0, concat_axis=0, tiled=True
        )

    def assemble(blocks):
        outgoing = jnp.dot(spread, blocks, precision=lax.Precision.HIGHEST).reshape(
            peer_count, capacity, blocks.shape[1]
        )
        returned = owner_sum(
            lax.all_to_all(outgoing, "dom", split_axis=0, concat_axis=0, tiled=True)
        )
        return jnp.take(returned.reshape(recv_rows, -1), slot_place, axis=0)

    rim_width = 2

    def rimmed(values):
        return with_halo(values, (("sub", 2),), rim_width)

    edge_diag = edge_diagonal(mass_coef, curl_coef, first_plane, planes)
    node_diag = node_diagonal(mass_coef, first_plane, planes)
    edge_width = 3 * LAT
    first_blocks = [edge_sides(edge_diag), node_sides(node_diag)]
    diag_sums = assemble(jnp.concatenate(first_blocks, axis=1))
    full_edge_diag = insert_edges(edge_diag, diag_sums[:, :edge_width])
    full_node_diag = insert_nodes(node_diag, diag_sums[:, edge_width : edge_width + LAT])
    source_below = from_behind(source[:, :, planes - 1 :], "sub", 1)
    edge_field = jnp.zeros_like(source)
    potential = jnp.zeros((macro_count, planes, cell_count), jnp.float32)
    for sweep_index in range(SWEEPS):
        if sweep_index == 0:
            residual = source
            residual_sum = assemble(edge_sides(residual))
        else:
            residual = source - apply_operator(
                rimmed(edge_field), rim_width, 0, first_plane, mass_coef, curl_coef
            )
            residual_sum = assemble(edge_sides(residual))
        full_residual = insert_edges(residual, residual_sum)
        edge_field = edge_field + EDGE_DAMPING * full_residual / full_edge_diag
        padded = rimmed(edge_field)
        lowered = jnp.concatenate([source_below, source], axis=2) - apply_operator(
            padded, 2, 1, first_plane, mass_coef, curl_coef
        )
        node_values = node_residual(lowered, planes)
        node_sum = assemble(node_sides(node_values))
        correction = NODE_DAMPING * insert_nodes(node_values, node_sum) / full_node_diag
        plane_above = from_behind(correction[:, :1], "sub", -1)
        edge_field = edge_field + gradient(
            jnp.concatenate([correction, plane_above], axis=1), planes
        )
        potential = potential + correction
    return (edge_field, potential)


def solution(mesh):
    in_specs = (
        P("dom", None, "sub", None),
        P("dom", None),
        P(),
        P(),
        P("dom", None),
        P("dom", None),
    )
    out_specs = (P("dom", None, "sub", None), P("dom", "sub", None))
    return jax.shard_map(local, mesh=mesh, in_specs=in_specs, out_specs=out_specs, check_vma=False)
```

profile of v0, /device:TPU:1, one launch (start us, length us, event | category | flops | bytes accessed | tf_op | source)
XLA Modules:
  0.0 226.3 jit_solution(10753228744907448692)
XLA Ops:
  0.7 1.8 reshape.1406
  4.5 6.4 %all-to-all-start = ((f32[8,4,96]{2,1,0:T(4,128)}), f32[8,4,96]{2,1,0:T(4,128)S(1)}, u32[]{:S(2)}, u32[]{:S(2)}) async-start(f32[8,4,96]{2,1,0:T(4,128)} %fusion.293), calls=%async_computation | async-start | bytes 32768 | tf_op jit(solution)/shard_map/all_to_all | solution.py:226
  25.3 5.4 %all-to-all-start.2 = ((f32[8,4,128]{2,1,0:T(4,128)}), f32[8,4,128]{2,1,0:T(4,128)S(1)}, u32[]{:S(2)}, u32[]{:S(2)}) async-start(f32[8,4,128]{2,1,0:T(4,128)} %bitcast.19), calls=%async_computation.2 | async-start | bytes 32768 | tf_op jit(solution)/shard_map/all_to_all | solution.py:226
  31.5 4.7 %all-to-all-done.2 = f32[8,4,128]{2,1,0:T(4,128)S(1)} async-done(((f32[8,4,128]{2,1,0:T(4,128)}), f32[8,4,128]{2,1,0:T(4,128)S(1)}, u32[]{:S(2)}, u32[]{:S(2)}) %all-to-all-start.2) | async-done | bytes 16416 | tf_op jit(solution)/shard_map/all_to_all | solution.py:226
  36.2 3.3 %all-to-all-start.1 = ((f32[8,4,96]{2,1,0:T(4,128)}), f32[8,4,96]{2,1,0:T(4,128)S(1)}, u32[]{:S(2)}, u32[]{:S(2)}) async-start(f32[8,4,96]{2,1,0:T(4,128)} %fusion.303), calls=%async_computation.1 | async-start | bytes 32768 | tf_op jit(solution)/shard_map/all_to_all | solution.py:217
  40.3 4.6 %all-to-all-done.1 = f32[8,4,96]{2,1,0:T(4,128)S(1)} async-done(((f32[8,4,96]{2,1,0:T(4,128)}), f32[8,4,96]{2,1,0:T(4,128)S(1)}, u32[]{:S(2)}, u32[]{:S(2)}) %all-to-all-start.1) | async-done | bytes 12320 | tf_op jit(solution)/shard_map/all_to_all | solution.py:217
  44.9 3.3 %all-to-all-start.3 = ((f32[8,4,128]{2,1,0:T(4,128)}), f32[8,4,128]{2,1,0:T(4,128)S(1)}, u32[]{:S(2)}, u32[]{:S(2)}) async-start(f32[8,4,128]{2,1,0:T(4,128)} %fusion.301), calls=%async_computation.3 | async-start | bytes 32768 | tf_op jit(solution)/shard_map/all_to_all | solution.py:217
  53.6 1.4 scatter.85
  55.0 1.4 scatter.86
  56.4 1.4 scatter.89
  61.8 1.7 scatter.90
  63.4 1.8 scatter.91
  65.2 1.7 scatter.94
  66.9 2.9 %scatter.95 = f32[4,7,4,32,32]{4,3,2,1,0:T(8,128)} dynamic-update-slice(f32[4,7,4,32,32]{4,3,2,1,0:T(8,128)} %scatter.94, f32[4,1,4,32,1]{4,3,2,1,0:T(8,128)S(1)} %copy.1016, s32[]{:T(128)} %constant.775.clone.1, s32[]{:T(128)} %constant.776.clone.1, s32[]{:T(128)} %constant.775.clone.1, s32[]{:T(128)} %constant.775.clone.1, s32[]{:T(128)} %constant.779.clone.1) | dynamic-update-slice | bytes 4100 | tf_op jit(solution)/shard_map/scatter | solution.py:169
  69.8 2.9 %scatter.96 = f32[4,7,4,32,32]{4,3,2,1,0:T(8,128)} dynamic-update-slice(f32[4,7,4,32,32]{4,3,2,1,0:T(8,128)} %scatter.95, f32[4,1,4,32,1]{4,3,2,1,0:T(8,128)S(1)} %copy.1017, s32[]{:T(128)} %constant.775.clone.1, s32[]{:T(128)} %constant.777.clone.1, s32[]{:T(128)} %constant.775.clone.1, s32[]{:T(128)} %constant.775.clone.1, s32[]{:T(128)} %constant.779.clone.1) | dynamic-update-slice | bytes 4100 | tf_op jit(solution)/shard_map/scatter | solution.py:169
  72.7 3.0 %scatter.99 = f32[4,7,4,32,32]{4,3,2,1,0:T(8,128)} dynamic-update-slice(f32[4,7,4,32,32]{4,3,2,1,0:T(8,128)} %scatter.96, f32[4,1,4,32,1]{4,3,2,1,0:T(8,128)S(1)} %copy.1018, s32[]{:T(128)} %constant.775.clone.1, s32[]{:T(128)} %constant.778.clone.1, s32[]{:T(128)} %constant.775.clone.1, s32[]{:T(128)} %constant.775.clone.1, s32[]{:T(128)} %constant.779.clone.1) | dynamic-update-slice | bytes 4100 | tf_op jit(solution)/shard_map/scatter | solution.py:169
  75.7 3.2 %multiply_divide_fusion.1 = f32[4,7,4,32,32]{4,3,2,1,0:T(8,128)} fusion(f32[4,7,4,32,32]{4,3,2,1,0:T(8,128)} %scatter.99, f32[4,7,4,32,32]{4,3,2,1,0:T(8,128)S(1)} %scatter.89), kind=kLoop, calls=%fused_computation.66 | loop fusion | flops 229376 | bytes 1376256 | tf_op jit(solution)/shard_map/div | solution.py:255
  78.9 2.5 %div.25 = f32[4,7,4,1024]{3,2,1,0:T(4,128)S(1)} reshape(f32[4,7,4,32,32]{4,3,2,1,0:T(8,128)} %multiply_divide_fusion.1) | data formatting | bytes 917504 | tf_op jit(solution)/shard_map/div | solution.py:255
  81.5 6.8 %collective-permute-start.1 = (f32[4,7,2,1024]{3,2,0,1:T(2,128)S(1)}, f32[4,7,2,1024]{3,2,0,1:T(2,128)S(1)}, u32[]{:S(2)}, u32[]{:S(2)}) collective-permute-start(f32[4,7,2,1024]{3,2,0,1:T(2,128)S(1)} %get-tuple-element.376), channel_id=1, source_target_pairs={{0,1},{1,2},{2,3},{4,5},{5,6},{6,7},{8,9},{9,10},{10,11},{12,13},{... | collective-permute-start | bytes 688136 | tf_op jit(solution)/shard_map/ppermute | solution.py:31
  88.4 1.9 collective-permute-start.2
  90.4 3.6 %collective-permute-start = (f32[4,7,1,1024]{3,2,0,1:T(1,128)S(1)}, f32[4,7,1,1024]{3,2,0,1:T(1,128)S(1)}, u32[]{:S(2)}, u32[]{:S(2)}) collective-permute-start(f32[4,7,1,1024]{3,2,0,1:T(1,128)S(1)} %copy.1183), channel_id=1, source_target_pairs={{0,1},{1,2},{2,3},{4,5},{5,6},{6,7},{8,9},{9,10},{10,11},{12,13},{... | collective-permute-start | bytes 344072 | tf_op jit(solution)/shard_map/ppermute | solution.py:42
  94.2 1.4 collective-permute-done.2
  100.5 5.7 %all-to-all-start.4 = ((f32[8,1,128]{2,1,0:T(1,128)}), f32[8,1,128]{2,1,0:T(1,128)S(1)}, u32[]{:S(2)}, u32[]{:S(2)}) async-start(f32[8,1,128]{2,1,0:T(1,128)} %reshape.1657), calls=%async_computation.4 | async-start | bytes 8192 | tf_op jit(solution)/shard_map/all_to_all | solution.py:226
  106.2 5.2 %all-to-all-done.4 = f32[8,1,128]{2,1,0:T(1,128)S(1)} async-done(((f32[8,1,128]{2,1,0:T(1,128)}), f32[8,1,128]{2,1,0:T(1,128)S(1)}, u32[]{:S(2)}, u32[]{:S(2)}) %all-to-all-start.4) | async-done | bytes 4128 | tf_op jit(solution)/shard_map/all_to_all | solution.py:226
  113.5 3.3 %all-to-all-start.5 = ((f32[8,1,128]{2,1,0:T(1,128)}), f32[8,1,128]{2,1,0:T(1,128)S(1)}, u32[]{:S(2)}, u32[]{:S(2)}) async-start(f32[8,1,128]{2,1,0:T(1,128)} %reshape.1659), calls=%async_computation.5 | async-start | bytes 8192 | tf_op jit(solution)/shard_map/all_to_all | solution.py:217
  117.4 1.4 scatter.105
  118.7 3.2 %all-to-all-done.5 = f32[8,1,128]{2,1,0:T(1,128)S(1)} async-done(((f32[8,1,128]{2,1,0:T(1,128)}), f32[8,1,128]{2,1,0:T(1,128)S(1)}, u32[]{:S(2)}, u32[]{:S(2)}) %all-to-all-start.5) | async-done | bytes 4128 | tf_op jit(solution)/shard_map/all_to_all | solution.py:217
  124.0 1.4 scatter.101
  125.6 1.9 collective-permute-start.3
  127.7 3.7 %collective-permute-done.3 = f32[4,1,1024]{2,1,0:T(1,128)S(1)} collective-permute-done((f32[4,1,1024]{2,1,0:T(1,128)S(1)}, f32[4,1,1024]{2,1,0:T(1,128)S(1)}, u32[]{:S(2)}, u32[]{:S(2)}) %collective-permute-start.3) | collective-permute-done | bytes 16416 | tf_op jit(solution)/shard_map/ppermute | solution.py:42
  132.5 1.9 collective-permute-start.4
  134.4 2.6 %collective-permute-start.5 = (f32[4,7,2,1024]{3,2,0,1:T(2,128)S(1)}, f32[4,7,2,1024]{3,2,0,1:T(2,128)S(1)}, u32[]{:S(2)}, u32[]{:S(2)}) collective-permute-start(f32[4,7,2,1024]{3,2,0,1:T(2,128)S(1)} %get-tuple-element.374), channel_id=1, source_target_pairs={{1,0},{2,1},{3,2},{5,4},{6,5},{7,6},{9,8},{10,9},{11,10},{13,12},{... | collective-permute-start | bytes 688136 | tf_op jit(solution)/shard_map/ppermute | solution.py:34
  137.4 4.4 %collective-permute-done.5 = f32[4,7,2,1024]{3,2,0,1:T(2,128)S(1)} collective-permute-done((f32[4,7,2,1024]{3,2,0,1:T(2,128)S(1)}, f32[4,7,2,1024]{3,2,0,1:T(2,128)S(1)}, u32[]{:S(2)}, u32[]{:S(2)}) %collective-permute-start.5) | collective-permute-done | bytes 229408 | tf_op jit(solution)/shard_map/ppermute | solution.py:34
  144.7 1.8 reshape.1439
  147.6 7.8 %all_to_all.50 = f32[8,4,96]{2,1,0:T(4,128)S(1)} all-to-all(f32[8,4,96]{2,1,0:T(4,128)S(1)} %fusion.289), channel_id=1, replica_groups=mesh['dom'=8,'sub'=4] {'dom'}, dimensions={0} | all-to-all | bytes 24576 | tf_op jit(solution)/shard_map/all_to_all | solution.py:226
  155.6 7.8 %all_to_all.51 = f32[8,4,96]{2,1,0:T(4,128)S(1)} all-to-all(f32[8,4,96]{2,1,0:T(4,128)S(1)} %fusion.297), channel_id=1, replica_groups=mesh['dom'=8,'sub'=4] {'dom'}, dimensions={0} | all-to-all | bytes 24576 | tf_op jit(solution)/shard_map/all_to_all | solution.py:217
  170.6 2.3 %scatter.111 = f32[4,7,4,32,32]{4,3,2,1,0:T(8,128)S(1)} dynamic-update-slice(f32[4,7,4,32,32]{4,3,2,1,0:T(8,128)S(1)} %scatter.110, f32[4,1,4,32,1]{4,3,2,1,0:T(8,128)} %copy.1052, s32[]{:T(128)} %constant.775.clone.1, s32[]{:T(128)} %constant.776.clone.1, s32[]{:T(128)} %constant.775.clone.1, s32[]{:T(128)} %constant.775.clone.1, s32[]{:T(128)} %constant.779.clone.1) | dynamic-update-slice | bytes 4100 | tf_op jit(solution)/shard_map/scatter | solution.py:169
  172.9 2.3 %scatter.114 = f32[4,7,4,32,32]{4,3,2,1,0:T(8,128)S(1)} dynamic-update-slice(f32[4,7,4,32,32]{4,3,2,1,0:T(8,128)S(1)} %scatter.111, f32[4,1,4,32,1]{4,3,2,1,0:T(8,128)} %copy.1053, s32[]{:T(128)} %constant.775.clone.1, s32[]{:T(128)} %constant.777.clone.1, s32[]{:T(128)} %constant.775.clone.1, s32[]{:T(128)} %constant.775.clone.1, s32[]{:T(128)} %constant.779.clone.1) | dynamic-update-slice | bytes 4100 | tf_op jit(solution)/shard_map/scatter | solution.py:169
  175.2 1.4 scatter.115
  176.6 3.2 %multiply_divide_fusion = f32[4,7,4,32,32]{4,3,2,1,0:T(8,128)} fusion(f32[4,7,4,32,32]{4,3,2,1,0:T(8,128)} %scatter.99, f32[4,7,4,32,32]{4,3,2,1,0:T(8,128)S(1)} %scatter.115), kind=kLoop, calls=%fused_computation.65 | loop fusion | flops 229376 | bytes 1376256 | tf_op jit(solution)/shard_map/div | solution.py:255
  179.8 2.4 %div.29 = f32[4,7,4,1024]{3,2,1,0:T(4,128)S(1)} reshape(f32[4,7,4,32,32]{4,3,2,1,0:T(8,128)} %multiply_divide_fusion) | data formatting | bytes 917504 | tf_op jit(solution)/shard_map/div | solution.py:255
  182.6 4.2 %collective-permute-start.6 = (f32[4,7,2,1024]{3,2,0,1:T(2,128)S(1)}, f32[4,7,2,1024]{3,2,0,1:T(2,128)S(1)}, u32[]{:S(2)}, u32[]{:S(2)}) collective-permute-start(f32[4,7,2,1024]{3,2,0,1:T(2,128)S(1)} %get-tuple-element.372), channel_id=1, source_target_pairs={{0,1},{1,2},{2,3},{4,5},{5,6},{6,7},{8,9},{9,10},{10,11},{12,13},{... | collective-permute-start | bytes 688136 | tf_op jit(solution)/shard_map/ppermute | solution.py:31
  186.8 1.9 collective-permute-start.7
  189.7 4.4 %collective-permute-done.7 = f32[4,7,2,1024]{3,2,0,1:T(2,128)S(1)} collective-permute-done((f32[4,7,2,1024]{3,2,0,1:T(2,128)S(1)}, f32[4,7,2,1024]{3,2,0,1:T(2,128)S(1)}, u32[]{:S(2)}, u32[]{:S(2)}) %collective-permute-start.7) | collective-permute-done | bytes 229408 | tf_op jit(solution)/shard_map/ppermute | solution.py:34
  199.0 8.0 %all_to_all.52 = f32[8,1,128]{2,1,0:T(1,128)S(1)} all-to-all(f32[8,1,128]{2,1,0:T(1,128)S(1)} %reshape.1661), channel_id=1, replica_groups=mesh['dom'=8,'sub'=4] {'dom'}, dimensions={0} | all-to-all | bytes 8192 | tf_op jit(solution)/shard_map/all_to_all | solution.py:226
  207.9 7.7 %all_to_all.53 = f32[8,1,128]{2,1,0:T(1,128)S(1)} all-to-all(f32[8,1,128]{2,1,0:T(1,128)S(1)} %reshape.1663), channel_id=1, replica_groups=mesh['dom'=8,'sub'=4] {'dom'}, dimensions={0} | all-to-all | bytes 8192 | tf_op jit(solution)/shard_map/all_to_all | solution.py:217
  219.2 1.9 collective-permute-start.8
  221.9 2.8 %collective-permute-done.8 = f32[4,1,1024]{2,1,0:T(1,128)S(1)} collective-permute-done((f32[4,1,1024]{2,1,0:T(1,128)S(1)}, f32[4,1,1024]{2,1,0:T(1,128)S(1)}, u32[]{:S(2)}, u32[]{:S(2)}) %collective-permute-start.8) | collective-permute-done | bytes 16416 | tf_op jit(solution)/shard_map/ppermute | solution.py:42
  (409 shorter events, 62.2 us)
Async XLA Ops:
  0.6 10.3 %copy-start = (f32[16,8]{0,1:T(8,128)S(1)}, f32[16,8]{0,1:T(8,128)}, u32[]{:S(2)}) copy-start(f32[16,8]{0,1:T(8,128)} %param.61) | copy-start | bytes 1540
  0.6 1.9 copy-start.55
  2.4 8.5 %copy-start.52 = (s32[4,1024]{1,0:T(4,128)S(1)}, s32[4,1024]{1,0:T(4,128)}, u32[]{:S(2)}) copy-start(s32[4,1024]{1,0:T(4,128)} %param.59) | copy-start | bytes 49156
  2.5 9.6 %copy-start.54 = (f32[16,7]{0,1:T(8,128)S(1)}, f32[16,7]{0,1:T(8,128)}, u32[]{:S(2)}) copy-start(f32[16,7]{0,1:T(8,128)} %param.60) | copy-start | bytes 1348
  4.5 20.9 %all-to-all-start = ((f32[8,4,96]{2,1,0:T(4,128)}), f32[8,4,96]{2,1,0:T(4,128)S(1)}, u32[]{:S(2)}, u32[]{:S(2)}) async-start(f32[8,4,96]{2,1,0:T(4,128)} %fusion.293), calls=%async_computation | async-start | bytes 32768 | tf_op jit(solution)/shard_map/all_to_all | solution.py:226
  10.8 4.4 %copy-start.39 = (pred[1024]{0:T(1024)(128)(4,1)}, pred[1024]{0:T(1024)(128)(4,1)S(1)}, u32[]{:S(2)}) copy-start(pred[1024]{0:T(1024)(128)(4,1)S(1)} %fusion.282) | copy-start | bytes 3076
  10.9 37.9 %copy-start.47 = (pred[32]{0:T(512)(128)(4,1)}, pred[32]{0:T(512)(128)(4,1)S(1)}, u32[]{:S(2)}) copy-start(pred[32]{0:T(512)(128)(4,1)S(1)} %get-tuple-element.341) | copy-start | bytes 100
  12.0 130.4 %copy-start.6 = (f32[4,1024]{1,0:T(4,128)}, f32[4,1024]{1,0:T(4,128)S(1)}, u32[]{:S(2)}) copy-start(f32[4,1024]{1,0:T(4,128)S(1)} %add.1146) | copy-start | bytes 49156
  12.0 130.8 %copy-start.2 = (f32[4,1024]{1,0:T(4,128)}, f32[4,1024]{1,0:T(4,128)S(1)}, u32[]{:S(2)}) copy-start(f32[4,1024]{1,0:T(4,128)S(1)} %add.1149) | copy-start | bytes 49156
  12.0 130.2 %copy-start.8 = (f32[4,1024]{1,0:T(4,128)}, f32[4,1024]{1,0:T(4,128)S(1)}, u32[]{:S(2)}) copy-start(f32[4,1024]{1,0:T(4,128)S(1)} %add.1162) | copy-start | bytes 49156
  12.0 130.7 %copy-start.4 = (f32[4,1024]{1,0:T(4,128)}, f32[4,1024]{1,0:T(4,128)S(1)}, u32[]{:S(2)}) copy-start(f32[4,1024]{1,0:T(4,128)S(1)} %squeeze.154) | copy-start | bytes 49156
  12.1 130.7 %copy-start.16 = (f32[4,1024]{1,0:T(4,128)}, f32[4,1024]{1,0:T(4,128)S(1)}, u32[]{:S(2)}) copy-start(f32[4,1024]{1,0:T(4,128)S(1)} %squeeze.155) | copy-start | bytes 49156
  12.6 130.5 %copy-start.12 = (f32[4,1024]{1,0:T(4,128)}, f32[4,1024]{1,0:T(4,128)S(1)}, u32[]{:S(2)}) copy-start(f32[4,1024]{1,0:T(4,128)S(1)} %add.1145) | copy-start | bytes 49156
  12.7 130.6 %copy-start.10 = (f32[4,1024]{1,0:T(4,128)}, f32[4,1024]{1,0:T(4,128)S(1)}, u32[]{:S(2)}) copy-start(f32[4,1024]{1,0:T(4,128)S(1)} %add.1158) | copy-start | bytes 49156
  16.3 3.0 %copy-start.56 = (s32[1,32]{1,0:T(1,128)S(1)}, s32[1,32]{1,0:T(1,128)}, u32[]{:S(2)}) copy-start(s32[1,32]{1,0:T(1,128)} %param.63) | copy-start | bytes 388
  25.3 25.7 %copy-start.53 = (s32[1024]{0:T(1024)}, s32[1024]{0:T(1024)S(1)}, u32[]{:S(2)}) copy-start(s32[1024]{0:T(1024)S(1)} %pad_clamp_fusion.1) | copy-start | bytes 12292
  25.3 10.9 %all-to-all-start.2 = ((f32[8,4,128]{2,1,0:T(4,128)}), f32[8,4,128]{2,1,0:T(4,128)S(1)}, u32[]{:S(2)}, u32[]{:S(2)}) async-start(f32[8,4,128]{2,1,0:T(4,128)} %bitcast.19), calls=%async_computation.2 | async-start | bytes 32768 | tf_op jit(solution)/shard_map/all_to_all | solution.py:226
  36.2 8.7 %all-to-all-start.1 = ((f32[8,4,96]{2,1,0:T(4,128)}), f32[8,4,96]{2,1,0:T(4,128)S(1)}, u32[]{:S(2)}, u32[]{:S(2)}) async-start(f32[8,4,96]{2,1,0:T(4,128)} %fusion.303), calls=%async_computation.1 | async-start | bytes 32768 | tf_op jit(solution)/shard_map/all_to_all | solution.py:217
  44.9 12.9 %all-to-all-start.3 = ((f32[8,4,128]{2,1,0:T(4,128)}), f32[8,4,128]{2,1,0:T(4,128)S(1)}, u32[]{:S(2)}, u32[]{:S(2)}) async-start(f32[8,4,128]{2,1,0:T(4,128)} %fusion.301), calls=%async_computation.3 | async-start | bytes 32768 | tf_op jit(solution)/shard_map/all_to_all | solution.py:217
  51.2 7.3 %copy-start.48 = (pred[32]{0:T(512)(128)(4,1)S(1)}, pred[32]{0:T(512)(128)(4,1)}, u32[]{:S(2)}) copy-start(pred[32]{0:T(512)(128)(4,1)} %copy-done.47) | copy-start | bytes 100
  78.8 11.4 %copy-start.1 = (f32[4,7,4,1024]{3,2,1,0:T(4,128)S(1)}, f32[4,7,4,1024]{3,2,1,0:T(4,128)}, u32[]{:S(2)}) copy-start(f32[4,7,4,1024]{3,2,1,0:T(4,128)} %param.58) | copy-start | bytes 1376260
  78.8 15.2 %copy-start.44 = (f32[1,4096]{1,0:T(1,128)S(1)}, f32[1,4096]{1,0:T(1,128)}, u32[]{:S(2)}) copy-start(f32[1,4096]{1,0:T(1,128)} %get-tuple-element.381) | copy-start | bytes 49156
  78.8 15.3 %copy-start.43 = (f32[1,4096]{1,0:T(1,128)S(1)}, f32[1,4096]{1,0:T(1,128)}, u32[]{:S(2)}) copy-start(f32[1,4096]{1,0:T(1,128)} %get-tuple-element.380) | copy-start | bytes 49156
  78.8 15.3 %copy-start.42 = (f32[1,4096]{1,0:T(1,128)S(1)}, f32[1,4096]{1,0:T(1,128)}, u32[]{:S(2)}) copy-start(f32[1,4096]{1,0:T(1,128)} %get-tuple-element.379) | copy-start | bytes 49156
  81.5 12.7 %collective-permute-start.1 = (f32[4,7,2,1024]{3,2,0,1:T(2,128)S(1)}, f32[4,7,2,1024]{3,2,0,1:T(2,128)S(1)}, u32[]{:S(2)}, u32[]{:S(2)}) collective-permute-start(f32[4,7,2,1024]{3,2,0,1:T(2,128)S(1)} %get-tuple-element.376), channel_id=1, source_target_pairs={{0,1},{1,2},{2,3},{4,5},{5,6},{6,7},{8,9},{9,10},{10,11},{12,13},{... | collective-permute-start | bytes 688136 | tf_op jit(solution)/shard_map/ppermute | solution.py:31
  88.4 7.3 %collective-permute-start.2 = (f32[4,7,2,1024]{3,2,0,1:T(2,128)S(1)}, f32[4,7,2,1024]{3,2,0,1:T(2,128)S(1)}, u32[]{:S(2)}, u32[]{:S(2)}) collective-permute-start(f32[4,7,2,1024]{3,2,0,1:T(2,128)S(1)} %get-tuple-element.375), channel_id=1, source_target_pairs={{1,0},{2,1},{3,2},{5,4},{6,5},{7,6},{9,8},{10,9},{11,10},{13,12},{... | collective-permute-start | bytes 688136 | tf_op jit(solution)/shard_map/ppermute | solution.py:34
  90.4 8.1 %collective-permute-start = (f32[4,7,1,1024]{3,2,0,1:T(1,128)S(1)}, f32[4,7,1,1024]{3,2,0,1:T(1,128)S(1)}, u32[]{:S(2)}, u32[]{:S(2)}) collective-permute-start(f32[4,7,1,1024]{3,2,0,1:T(1,128)S(1)} %copy.1183), channel_id=1, source_target_pairs={{0,1},{1,2},{2,3},{4,5},{5,6},{6,7},{8,9},{9,10},{10,11},{12,13},{... | collective-permute-start | bytes 344072 | tf_op jit(solution)/shard_map/ppermute | solution.py:42
  94.1 47.6 %copy-start.37 = (f32[4,1024]{1,0:T(4,128)}, f32[4,1024]{1,0:T(4,128)S(1)}, u32[]{:S(2)}) copy-start(f32[4,1024]{1,0:T(4,128)S(1)} %add.1262) | copy-start | bytes 49156
  94.2 48.2 %copy-start.33 = (f32[4,1024]{1,0:T(4,128)}, f32[4,1024]{1,0:T(4,128)S(1)}, u32[]{:S(2)}) copy-start(f32[4,1024]{1,0:T(4,128)S(1)} %add.1246) | copy-start | bytes 49156
  94.2 48.2 %copy-start.35 = (f32[4,1024]{1,0:T(4,128)}, f32[4,1024]{1,0:T(4,128)S(1)}, u32[]{:S(2)}) copy-start(f32[4,1024]{1,0:T(4,128)S(1)} %add.1253) | copy-start | bytes 49156
  94.2 2.6 %copy-start.45 = (pred[6]{0:T(512)(128)(4,1)}, pred[6]{0:T(512)(128)(4,1)S(1)}, u32[]{:S(2)}) copy-start(pred[6]{0:T(512)(128)(4,1)S(1)} %add_compare_fusion.1) | copy-start | bytes 22
  98.9 24.5 %copy-start.49 = (pred[32]{0:T(512)(128)(4,1)S(1)}, pred[32]{0:T(512)(128)(4,1)}, u32[]{:S(2)}) copy-start(pred[32]{0:T(512)(128)(4,1)} %copy-done.47) | copy-start | bytes 100
  100.5 10.9 %all-to-all-start.4 = ((f32[8,1,128]{2,1,0:T(1,128)}), f32[8,1,128]{2,1,0:T(1,128)S(1)}, u32[]{:S(2)}, u32[]{:S(2)}) async-start(f32[8,1,128]{2,1,0:T(1,128)} %reshape.1657), calls=%async_computation.4 | async-start | bytes 8192 | tf_op jit(solution)/shard_map/all_to_all | solution.py:226
  113.5 8.5 %all-to-all-start.5 = ((f32[8,1,128]{2,1,0:T(1,128)}), f32[8,1,128]{2,1,0:T(1,128)S(1)}, u32[]{:S(2)}, u32[]{:S(2)}) async-start(f32[8,1,128]{2,1,0:T(1,128)} %reshape.1659), calls=%async_computation.5 | async-start | bytes 8192 | tf_op jit(solution)/shard_map/all_to_all | solution.py:217
  125.6 5.7 %collective-permute-start.3 = (f32[4,1,1024]{2,1,0:T(1,128)S(1)}, f32[4,1,1024]{2,1,0:T(1,128)S(1)}, u32[]{:S(2)}, u32[]{:S(2)}) collective-permute-start(f32[4,1,1024]{2,1,0:T(1,128)S(1)} %slice.2064), channel_id=1, source_target_pairs={{1,0},{2,1},{3,2},{5,4},{6,5},{7,6},{9,8},{10,9},{11,10},{13,12},{... | collective-permute-start | bytes 49160 | tf_op jit(solution)/shard_map/ppermute | solution.py:42
  132.5 4.9 %collective-permute-start.4 = (f32[4,7,2,1024]{3,2,0,1:T(2,128)S(1)}, f32[4,7,2,1024]{3,2,0,1:T(2,128)S(1)}, u32[]{:S(2)}, u32[]{:S(2)}) collective-permute-start(f32[4,7,2,1024]{3,2,0,1:T(2,128)S(1)} %get-tuple-element.373), channel_id=1, source_target_pairs={{0,1},{1,2},{2,3},{4,5},{5,6},{6,7},{8,9},{9,10},{10,11},{12,13},{... | collective-permute-start | bytes 688136 | tf_op jit(solution)/shard_map/ppermute | solution.py:31
  134.4 7.3 %collective-permute-start.5 = (f32[4,7,2,1024]{3,2,0,1:T(2,128)S(1)}, f32[4,7,2,1024]{3,2,0,1:T(2,128)S(1)}, u32[]{:S(2)}, u32[]{:S(2)}) collective-permute-start(f32[4,7,2,1024]{3,2,0,1:T(2,128)S(1)} %get-tuple-element.374), channel_id=1, source_target_pairs={{1,0},{2,1},{3,2},{5,4},{6,5},{7,6},{9,8},{10,9},{11,10},{13,12},{... | collective-permute-start | bytes 688136 | tf_op jit(solution)/shard_map/ppermute | solution.py:34
  146.5 17.5 %copy-start.50 = (pred[32]{0:T(512)(128)(4,1)S(1)}, pred[32]{0:T(512)(128)(4,1)}, u32[]{:S(2)}) copy-start(pred[32]{0:T(512)(128)(4,1)} %copy-done.47) | copy-start | bytes 100
  179.8 14.3 %copy-start.38 = (f32[4,1024]{1,0:T(4,128)S(1)}, f32[4,1024]{1,0:T(4,128)}, u32[]{:S(2)}) copy-start(f32[4,1024]{1,0:T(4,128)} %copy-done.37) | copy-start | bytes 49156
  179.8 14.3 %copy-start.46 = (pred[6]{0:T(512)(128)(4,1)S(1)}, pred[6]{0:T(512)(128)(4,1)}, u32[]{:S(2)}) copy-start(pred[6]{0:T(512)(128)(4,1)} %copy-done.45) | copy-start | bytes 22
  182.2 12.4 %copy-start.9 = (f32[4,1024]{1,0:T(4,128)S(1)}, f32[4,1024]{1,0:T(4,128)}, u32[]{:S(2)}) copy-start(f32[4,1024]{1,0:T(4,128)} %copy-done.8) | copy-start | bytes 49156
  182.6 12.2 %copy-start.7 = (f32[4,1024]{1,0:T(4,128)S(1)}, f32[4,1024]{1,0:T(4,128)}, u32[]{:S(2)}) copy-start(f32[4,1024]{1,0:T(4,128)} %copy-done.6) | copy-start | bytes 49156
  182.6 12.2 %copy-start.17 = (f32[4,1024]{1,0:T(4,128)S(1)}, f32[4,1024]{1,0:T(4,128)}, u32[]{:S(2)}) copy-start(f32[4,1024]{1,0:T(4,128)} %copy-done.16) | copy-start | bytes 49156
  182.6 7.1 %collective-permute-start.6 = (f32[4,7,2,1024]{3,2,0,1:T(2,128)S(1)}, f32[4,7,2,1024]{3,2,0,1:T(2,128)S(1)}, u32[]{:S(2)}, u32[]{:S(2)}) collective-permute-start(f32[4,7,2,1024]{3,2,0,1:T(2,128)S(1)} %get-tuple-element.372), channel_id=1, source_target_pairs={{0,1},{1,2},{2,3},{4,5},{5,6},{6,7},{8,9},{9,10},{10,11},{12,13},{... | collective-permute-start | bytes 688136 | tf_op jit(solution)/shard_map/ppermute | solution.py:31
  186.8 7.3 %collective-permute-start.7 = (f32[4,7,2,1024]{3,2,0,1:T(2,128)S(1)}, f32[4,7,2,1024]{3,2,0,1:T(2,128)S(1)}, u32[]{:S(2)}, u32[]{:S(2)}) collective-permute-start(f32[4,7,2,1024]{3,2,0,1:T(2,128)S(1)} %get-tuple-element.371), channel_id=1, source_target_pairs={{1,0},{2,1},{3,2},{5,4},{6,5},{7,6},{9,8},{10,9},{11,10},{13,12},{... | collective-permute-start | bytes 688136 | tf_op jit(solution)/shard_map/ppermute | solution.py:34
  196.7 0.9 copy-start.15
  197.9 19.1 %copy-start.51 = (pred[32]{0:T(512)(128)(4,1)S(1)}, pred[32]{0:T(512)(128)(4,1)}, u32[]{:S(2)}) copy-start(pred[32]{0:T(512)(128)(4,1)} %copy-done.47) | copy-start | bytes 100
  219.2 5.5 %collective-permute-start.8 = (f32[4,1,1024]{2,1,0:T(1,128)S(1)}, f32[4,1,1024]{2,1,0:T(1,128)S(1)}, u32[]{:S(2)}, u32[]{:S(2)}) collective-permute-start(f32[4,1,1024]{2,1,0:T(1,128)S(1)} %slice.2196), channel_id=1, source_target_pairs={{1,0},{2,1},{3,2},{5,4},{6,5},{7,6},{9,8},{10,9},{11,10},{13,12},{... | collective-permute-start | bytes 49160 | tf_op jit(solution)/shard_map/ppermute | solution.py:42
  (24 other events, 16.9 us)
where the time goes:
time: 228 us; the launch traced here: 226 us
  local copies, waits for them, and re-layouts  74.5 us (33%)
  starting transfers between devices  54.3 us (24%)
  waiting for transfers between devices  35.8 us (16%)
  blocking collectives  31.2 us (14%)
  other arithmetic  23.6 us (10%)
  matrix products  4.37 us (2%)
  between operations  2.6 us (1%)
    scatter x18, local copies, waits for them, and re-layouts, insert_edges(): lattice.at[:, edge_type, :, :, column].set(shaped[:, side_index, slot_type])  27.9 us
    all_to_all x3, starting transfers between devices, assemble(): lax.all_to_all(outgoing, 'dom', split_axis=0, concat_axis=0, tiled=True)  17.5 us
    all_to_all x2, blocking collectives, assemble(): lax.all_to_all(outgoing, 'dom', split_axis=0, concat_axis=0, tiled=True)  15.8 us
    all_to_all x2, blocking collectives, owner_sum(): lax.all_to_all(summed.reshape(peer_count, capacity, -1), 'dom', split_axi...  15.5 us
    ppermute x3, starting transfers between devices, with_halo(): lax.ppermute(lax.slice_in_dim(block, block.shape[dim] - width, None, axis...  12.9 us
    ppermute x3, waiting for transfers between devices, with_halo(): lax.ppermute(lax.slice_in_dim(block, 0, width, axis=dim), axis, backward)  10.2 us
    all_to_all x3, starting transfers between devices, owner_sum(): lax.all_to_all(summed.reshape(peer_count, capacity, -1), 'dom', split_axi...  9.95 us
    all_to_all x3, waiting for transfers between devices, assemble(): lax.all_to_all(outgoing, 'dom', split_axis=0, concat_axis=0, tiled=True)  9.88 us
  transfers between devices with their start and end apart: 15, of which 11 were waited for; matrix products, arithmetic and copies ran while one was open for 13% of the time, Pallas kernels for 0%

commit v1 on v0

--- a/solution.py
+++ b/solution.py
@@ -1,6 +1,8 @@
 import jax
 import jax.numpy as jnp
 from jax import lax
+from jax.experimental import pallas as pl
+from jax.experimental.pallas import tpu as pltpu
 from jax.sharding import PartitionSpec as P
 
 LAT = 32
@@ -268,6 +270,581 @@
     return (edge_field, potential)
 
 
+LANES = 128
+XS = (0, LAT - 1)
+
+
+def lane_roll(v, s):
+    s = s % v.shape[-1]
+    return pltpu.roll(v, s, v.ndim - 1) if s else v
+
+
+def row_roll(v, s):
+    s = s % v.shape[0]
+    return pltpu.roll(v, s, 0) if s else v
+
+
+def iota(shape, dim):
+    return lax.broadcasted_iota(jnp.int32, shape, dim)
+
+
+class Plane:
+    def __init__(self, shape):
+        self.lane = iota(shape, 1)
+        self.x = self.lane & (LAT - 1)
+        self.cells = shape[1]
+        self.side = (self.x == 0) | (self.x == LAT - 1)
+
+    def ax(self, v):
+        return jnp.where(self.x < LAT - 1, lane_roll(v, -1), 0.0)
+
+    def ay(self, v):
+        return jnp.where(self.lane < self.cells - LAT, lane_roll(v, -LAT), 0.0)
+
+    def bx(self, v):
+        return jnp.where(self.x > 0, lane_roll(v, 1), 0.0)
+
+    def by(self, v):
+        return jnp.where(self.lane >= LAT, lane_roll(v, LAT), 0.0)
+
+    def bxy(self, v):
+        return jnp.where((self.lane >= LAT) & (self.x > 0), lane_roll(v, LAT + 1), 0.0)
+
+    def axy(self, v):
+        return jnp.where(
+            (self.lane < self.cells - LAT) & (self.x < LAT - 1), lane_roll(v, -LAT - 1), 0.0
+        )
+
+
+def zb(v):
+    return row_roll(v, 1)
+
+
+def za(v):
+    return row_roll(v, -1)
+
+
+def pack(feats, x_at):
+    rows = feats[0].shape[0]
+    low = iota((rows, LANES), 1) & 31
+    out = jnp.zeros((rows, LANES), jnp.float32)
+    for g, feat in enumerate(feats):
+        for c in range(8):
+            at = 8 * g + c
+            column = feat[:, LANES * c : LANES * (c + 1)]
+            out = jnp.where(low == at, lane_roll(column, at - x_at), out)
+    return out
+
+
+def unpack(packed_sides, g, base):
+    rows = packed_sides[0].shape[0]
+    low = iota((rows, LANES), 1) & 31
+    columns = []
+    for c in range(8):
+        column = base[:, LANES * c : LANES * (c + 1)]
+        for x_at, packed in zip(XS, packed_sides):
+            column = jnp.where(low == x_at, lane_roll(packed, x_at - 8 * g - c), column)
+        columns.append(column)
+    return jnp.concatenate(columns, axis=1)
+
+
+def packed_behind(v):
+    lane = iota(v.shape, 1)
+    first = jnp.where((lane & 7) == 0, 0.0, lane_roll(v, 33))
+    return jnp.where(lane < 32, first, lane_roll(v, 32))
+
+
+def packed_ahead(v):
+    lane = iota(v.shape, 1)
+    last = jnp.where((lane & 7) == 7, 0.0, lane_roll(v, -33))
+    return jnp.where(lane >= 96, last, lane_roll(v, -32))
+
+
+def group_of(shape):
+    return (iota(shape, 1) >> 3) & 3
+
+
+def group_sum(same, block):
+    total = None
+    rest = block
+    for _ in range(3):
+        part = rest.astype(jnp.bfloat16)
+        rest = rest - part.astype(jnp.float32)
+        piece = jnp.dot(same, part, preferred_element_type=jnp.float32)
+        total = piece if total is None else total + piece
+    return total
+
+
+def node_back(r, valid):
+    own = -(((r[0] + r[1]) + (r[2] + r[3])) + ((r[4] + r[5]) + r[6]))
+    back = zb(r[2]) + valid.bx(r[0] + zb(r[4])) + valid.by(r[1] + zb(r[5]))
+    return own + back + valid.bxy(r[3] + zb(r[6]))
+
+
+def node_grad(c, plane):
+    cx, cy, cxy = plane.ax(c), plane.ay(c), plane.axy(c)
+    ends = (cx, cy, za(c), cxy, za(cx), za(cy), za(cxy))
+    return [end - c for end in ends]
+
+
+def curl_curl(e, mu, plane, valid):
+    far = (
+        plane.ax(e[1]),
+        plane.ay(e[0]),
+        plane.ax(e[2]),
+        za(e[0]),
+        plane.ay(e[2]),
+        za(e[1]),
+        plane.axy(e[2]),
+        za(e[3]),
+    )
+    w = []
+    for f, (first, second, diagonal) in enumerate(FACE_EDGES):
+        w.append(jnp.where(valid, mu[f] * (e[first] + far[f] - e[diagonal]), 0.0))
+    return [
+        w[0] + w[2] + plane.by(w[1]) + zb(w[3]),
+        w[1] + w[4] + plane.bx(w[0]) + zb(w[5]),
+        w[3] + w[5] + w[7] + plane.bx(w[2]) + plane.by(w[4]) + plane.bxy(w[6]),
+        w[6] + zb(w[7]) - w[0] - w[1],
+        -w[2] - w[3],
+        -w[4] - w[5],
+        -w[6] - w[7],
+    ]
+
+
+def plane_flags(axis, planes, halo, cells):
+    depth = planes * lax.axis_size(axis)
+    at = lax.axis_index(axis) * planes - halo + iota((planes + 2 * halo, cells), 0)
+    return at >= 1, (at >= 0) & (at < depth)
+
+
+HALO = 2
+
+
+def first_kernel(n_dom, n_sub, macros, planes, cells, slots, recv_rows):
+    rows = planes + 2 * HALO
+    sides = 2 * macros
+    capacity = recv_rows // n_dom
+
+    def body(zone_ref, table_ref, source_ref, owner_ref, group_ref, pay_ref, coef_ref, w_ref, nw_ref, sx_ref, hold_ref):
+        k = lax.axis_index("sub")
+        d = lax.axis_index("dom")
+        plane = Plane((rows, cells))
+        inside, _ = plane_flags("sub", planes, HALO, cells)
+        owner = owner_ref[...]
+        si, sj = iota((slots, slots), 0), iota((slots, slots), 1)
+        owner_f = owner.astype(jnp.float32)
+        column = jnp.sum(jnp.where(si == sj, owner_f, 0.0), axis=1, keepdims=True)
+        lower = jnp.where((column == owner_f) & (si < sj), 1.0, 0.0)
+        position = jnp.sum(lower, axis=0, keepdims=True)
+        flat = owner_f * recv_rows + (d * capacity).astype(jnp.float32) + position
+        keyed = group_ref[...].astype(jnp.float32) + (d * recv_rows).astype(jnp.float32)
+
+        def spread_lanes(values, g):
+            count = values.shape[1]
+            place = iota((count, LANES), 0)
+            place = 32 * (place >> 3) + (place & 7) + 8 * g
+            hot = jnp.where(place == iota((count, LANES), 1), 1.0, 0.0)
+            return jnp.dot(
+                jnp.broadcast_to(values, (8, count)), hot, precision=lax.Precision.HIGHEST
+            )
+
+        index_rows = spread_lanes(flat, 0) + spread_lanes(keyed, 1)
+        low = iota((rows, LANES), 1) & 31
+        sx_ref[...] = jnp.zeros_like(sx_ref)
+
+        def macro_step(m, carry):
+            zone = jnp.broadcast_to(zone_ref[pl.ds(m, 1), :], (8, cells))
+            mass8 = jnp.zeros((8, cells), jnp.float32)
+            curl8 = jnp.zeros((8, cells), jnp.float32)
+            for z in range(table_ref.shape[1]):
+                hit = zone == z
+                mass8 = jnp.where(hit, table_ref[0:8, z : z + 1], mass8)
+                curl8 = jnp.where(hit, table_ref[8:16, z : z + 1], curl8)
+            coef_ref[m, 0:8, :] = mass8
+            coef_ref[m, 8:16, :] = curl8
+
+            def coef(i):
+                return jnp.broadcast_to(coef_ref[m, i : i + 1, :], (rows, cells))
+
+            mass = [coef(t) for t in range(7)]
+            mu = [coef(8 + f) for f in range(8)]
+            flat_diag = [
+                mass[0] + mu[0] + mu[2] + plane.by(mu[1]),
+                mass[1] + mu[1] + mu[4] + plane.bx(mu[0]),
+                mass[2] + mu[3] + mu[5] + mu[7] + plane.bx(mu[2]) + plane.by(mu[4]) + plane.bxy(mu[6]),
+                mass[3] + mu[0] + mu[1] + mu[6],
+                mass[4] + mu[2] + mu[3],
+                mass[5] + mu[4] + mu[5],
+                mass[6] + mu[6] + mu[7],
+            ]
+            rise = {0: mu[3], 1: mu[5], 3: mu[7]}
+            for t in range(7):
+                diag = flat_diag[t]
+                if t in rise:
+                    diag = diag + jnp.where(inside, rise[t], 0.0)
+                w_ref[m, t] = EDGE_DAMPING / diag
+            node_flat = plane.bx(mass[0]) + plane.by(mass[1]) + plane.bxy(mass[3])
+            for t in range(7):
+                node_flat = node_flat + mass[t]
+            node_rise = mass[2] + plane.bx(mass[4]) + plane.by(mass[5]) + plane.bxy(mass[6])
+            nw_ref[m] = NODE_DAMPING / (node_flat + jnp.where(inside, node_rise, 0.0))
+            for t in range(7):
+                sx_ref[t, HALO : HALO + planes, :] = source_ref[m, t]
+            src = [sx_ref[t] for t in range(7)]
+            left = []
+            for t in range(7):
+                value = src[t] - mass[t] * (w_ref[m, t] * src[t])
+                if t in SHARED_TYPES:
+                    value = jnp.where(plane.side, 0.0, value)
+                left.append(value)
+            node = node_back(left, plane)
+            k0, k1 = k == 0, k == 1
+            extra = [
+                jnp.where(k0, mass[1], jnp.where(k1, flat_diag[1] + mu[5], flat_diag[1])),
+                jnp.where(k0, mass[2], jnp.where(k1, flat_diag[2], node_flat + node_rise)),
+                jnp.where(k0, mass[5], jnp.where(k1, flat_diag[5], node_flat)),
+            ]
+            for s, x_at in enumerate(XS):
+                packed = pack([src[1], src[2], src[5], node], x_at)
+                extras = jnp.where(k == 3, index_rows, pack(extra, x_at))
+                row = jnp.where(low < 24, extras, row_roll(packed, -(HALO + planes)))
+                hold_ref[m, s, 0:8, :] = packed
+                hold_ref[m, s, 8:16, :] = row
+            return carry
+
+        lax.fori_loop(0, macros, macro_step, 0)
+        for m in range(macros):
+            for s in range(2):
+                ms = 2 * m + s
+                for p in range(planes):
+                    pay_ref[0, p * sides + ms : p * sides + ms + 1, :] = hold_ref[m, s, HALO + p : HALO + p + 1, :]
+                at = planes * sides + ms
+                pay_ref[0, at : at + 1, :] = hold_ref[m, s, 8:9, :]
+        block = pay_ref[0]
+        for dest in range(1, n_dom * n_sub):
+            pay_ref[dest] = block
+
+    f32 = jnp.float32
+    return pl.pallas_call(
+        body,
+        name="first",
+        out_shape=(
+            jax.ShapeDtypeStruct((n_dom * n_sub, (planes + 1) * sides, LANES), f32),
+            jax.ShapeDtypeStruct((macros, 16, cells), f32),
+            jax.ShapeDtypeStruct((macros, 7, rows, cells), f32),
+            jax.ShapeDtypeStruct((macros, rows, cells), f32),
+        ),
+        scratch_shapes=[
+            pltpu.VMEM((7, rows, cells), f32),
+            pltpu.VMEM((macros, 2, 16, LANES), f32),
+        ],
+    )
+
+
+class Boundary:
+    def __init__(self, recv_ref, n_dom, n_sub, macros, planes):
+        self.recv, self.n_dom, self.n_sub = recv_ref, n_dom, n_sub
+        self.sides, self.planes = 2 * macros, planes
+        self.rows = n_dom * self.sides
+        self.group = group_of((self.rows, LANES))
+
+    def rows_of(self, ref, k, at):
+        n = self.sides
+        return jnp.concatenate(
+            [ref[d * self.n_sub + k, at * n : (at + 1) * n, :] for d in range(self.n_dom)], axis=0
+        )
+
+    def mass(self):
+        return self.rows_of(self.recv, 0, self.planes)
+
+    def fold(self, r, r_below):
+        total = jnp.where(self.group == 0, packed_behind(r), 0.0) - r
+        if r_below is not None:
+            total = total + jnp.where(self.group == 1, r_below, 0.0)
+            total = total + jnp.where(self.group == 2, packed_behind(r_below), 0.0)
+        return lane_roll(total, 24) + lane_roll(total, 16) + lane_roll(total, 8)
+
+    def layer_nodes(self, same, nodes):
+        out = [None] * self.n_sub
+        for start in range(0, self.n_sub, 4):
+            count = min(4, self.n_sub - start)
+            block = None
+            for i in range(count):
+                stacked = jnp.concatenate(nodes[start + i], axis=0)
+                group = group_of(stacked.shape)
+                moved = jnp.where(group == i, lane_roll(stacked, 8 * (i - 3)), 0.0)
+                block = moved if block is None else block + moved
+            summed = group_sum(same, block)
+            for i in range(count):
+                out[start + i] = lane_roll(summed, 8 * (3 - i))
+        return out
+
+
+def same_group(b, slots, recv_rows, capacity_rows):
+    recv, n_sub, planes, sides = b.recv, b.n_sub, b.planes, b.sides
+    index = b.rows_of(recv, 3, planes)
+    lane = iota(index.shape, 1)
+    side = iota(index.shape, 0) % sides
+    flat = []
+    for p in range(planes):
+        slot = side * planes + p
+        at = 32 * (slot >> 3) + (slot & 7)
+        flat.append(jnp.sum(jnp.where(lane == at, index, 0.0), axis=1, keepdims=True))
+    flat = jnp.concatenate(flat, axis=0).astype(jnp.int32)
+    total = flat.shape[0]
+    owner = flat // recv_rows
+    receive = flat - owner * recv_rows
+    table = jnp.zeros((total, LANES), jnp.float32)
+    for e in range(b.n_dom):
+        row = recv[e * n_sub + 3, planes * sides : planes * sides + 1, :]
+        table = jnp.where(owner == e, jnp.broadcast_to(row, (total, LANES)), table)
+    at = 32 * (receive >> 3) + (receive & 7) + 8
+    key = jnp.sum(jnp.where(iota((total, LANES), 1) == at, table, 0.0), axis=1, keepdims=True)
+    square = (total, total)
+    key_row = jnp.sum(jnp.where(iota(square, 0) == iota(square, 1), key, 0.0), axis=0, keepdims=True)
+    return jnp.where(key == key_row, 1.0, 0.0).astype(jnp.bfloat16)
+
+
+def second_kernel(n_dom, n_sub, macros, planes, cells, slots, recv_rows):
+    rows = planes + 2 * HALO
+    sides = 2 * macros
+    total = n_dom * slots
+    depth = n_sub * planes
+
+    def body(recv_ref, source_ref, low_ref, high_ref, coef_ref, w_ref, nw_ref, pay_ref, same_ref, base_ref, dw_ref, e2_ref, c1_ref, c2_ref, sh_ref, own_ref, turn_ref, sx_ref, hold_ref):
+        k = lax.axis_index("sub")
+        d = lax.axis_index("dom")
+        b = Boundary(recv_ref, n_dom, n_sub, macros, planes)
+        same_ref[...] = same_group(b, slots, recv_rows, None)
+        same = same_ref[...]
+        group = b.group
+        extra_e = b.rows_of(recv_ref, 1, planes)
+        extra_n = b.rows_of(recv_ref, 2, planes)
+        inner = jnp.where(group == 3, lane_roll(extra_n, 16), extra_e)
+        lowest = jnp.where(
+            group == 0, extra_n, jnp.where(group == 3, lane_roll(extra_n, 8), extra_e)
+        )
+        damp = jnp.where(group_of((total, LANES)) == 3, NODE_DAMPING, EDGE_DAMPING)
+        dw_ref[0] = damp / group_sum(same, jnp.concatenate([lowest] + [inner] * (planes - 1), axis=0))
+        dw_ref[1] = damp / group_sum(same, jnp.concatenate([inner] * planes, axis=0))
+        mass = b.mass()
+        n = b.rows
+        sh_ref[...] = jnp.zeros_like(sh_ref)
+        nodes = [[None] * planes for _ in range(n_sub)]
+        below = None
+        for layer in range(n_sub):
+            stacked = jnp.concatenate([b.rows_of(recv_ref, layer, p) for p in range(planes)], axis=0)
+            e1 = group_sum(same, stacked) * dw_ref[min(layer, 1)]
+            for p in range(planes):
+                at = layer * planes + p
+                src = stacked[p * n : (p + 1) * n]
+                e1_p = e1[p * n : (p + 1) * n]
+                sh_ref[HALO + at] = e1_p
+                r = jnp.where(group < 3, src - mass * e1_p, 0.0)
+                node = src + b.fold(r, below)
+                if p == 0 and layer > 0:
+                    node = node + b.rows_of(recv_ref, layer - 1, planes)
+                nodes[layer][p] = node
+                below = r
+        summed = b.layer_nodes(same, nodes)
+        above = None
+        for layer in reversed(range(n_sub)):
+            c1 = summed[layer] * dw_ref[min(layer, 1)]
+            for p in reversed(range(planes)):
+                at = layer * planes + p
+                c = jnp.where(group == 3, c1[p * n : (p + 1) * n], 0.0)
+                e1_p = sh_ref[HALO + at]
+                sh_ref[HALO + at] = jnp.where(group == 3, c, e1_p)
+                up = jnp.zeros_like(c) if above is None else above
+                rise = lane_roll(packed_ahead(c) - c, -24)
+                rise = jnp.where(group == 1, lane_roll(up - c, -16), rise)
+                rise = jnp.where(group == 2, lane_roll(packed_ahead(up) - c, -8), rise)
+                base_ref[at] = jnp.where(group < 3, e1_p + rise, 0.0)
+                above = c
+        for i in range(rows):
+            own_ref[i] = sh_ref[k * planes + i, pl.ds(pl.multiple_of(d * sides, sides), sides), :]
+        for ms in range(sides):
+            turn_ref[ms] = own_ref[:, ms, :]
+        plane = Plane((rows, cells))
+        _, valid = plane_flags("sub", planes, HALO, cells)
+
+        def macro_step(m, carry):
+            def coef(i):
+                return jnp.broadcast_to(coef_ref[m, i : i + 1, :], (rows, cells))
+
+            own = [turn_ref[2 * m], turn_ref[2 * m + 1]]
+            e1, r1 = [], []
+            for t in range(7):
+                sx_ref[t, 0:HALO, :] = low_ref[m, t]
+                sx_ref[t, HALO : HALO + planes, :] = source_ref[m, t]
+                sx_ref[t, HALO + planes : rows, :] = high_ref[m, t]
+            for t in range(7):
+                value = w_ref[m, t] * sx_ref[t]
+                if t in SHARED_TYPES:
+                    value = unpack(own, SHARED_TYPES.index(t), value)
+                e1.append(value)
+                r1.append(sx_ref[t] - coef(t) * value)
+            c1 = jnp.where(valid, nw_ref[m] * node_back(r1, plane), 0.0)
+            c1 = unpack(own, 3, c1)
+            c1_ref[m] = c1
+            grad = node_grad(c1, plane)
+            curled = curl_curl(e1, [coef(8 + f) for f in range(8)], plane, valid)
+            res, left = [], []
+            for t in range(7):
+                g = jnp.where(valid, grad[t], 0.0)
+                res_t = jnp.where(valid, r1[t] - curled[t] - coef(t) * g, 0.0)
+                e2 = e1[t] + g + w_ref[m, t] * res_t
+                left_t = sx_ref[t] - coef(t) * e2
+                if t in SHARED_TYPES:
+                    e2 = jnp.where(plane.side, 0.0, e2)
+                    left_t = jnp.where(plane.side, 0.0, left_t)
+                    res.append(res_t)
+                left.append(left_t)
+                e2_ref[m, t] = e2[HALO : HALO + planes]
+            node = node_back(left, plane)
+            c2_ref[m] = jnp.where(valid, nw_ref[m] * node, 0.0)
+            for s, x_at in enumerate(XS):
+                hold_ref[m, s] = pack(res + [node], x_at)
+            return carry
+
+        lax.fori_loop(0, macros, macro_step, 0)
+        for m in range(macros):
+            for s in range(2):
+                ms = 2 * m + s
+                for p in range(planes):
+                    pay_ref[0, p * sides + ms : p * sides + ms + 1, :] = hold_ref[m, s, HALO + p : HALO + p + 1, :]
+        block = pay_ref[0]
+        for dest in range(1, n_dom * n_sub):
+            pay_ref[dest] = block
+
+    f32 = jnp.float32
+    n = n_dom * sides
+    return pl.pallas_call(
+        body,
+        name="second",
+        out_shape=(
+            jax.ShapeDtypeStruct((n_dom * n_sub, planes * sides, LANES), f32),
+            jax.ShapeDtypeStruct((total, total), jnp.bfloat16),
+            jax.ShapeDtypeStruct((depth, n, LANES), f32),
+            jax.ShapeDtypeStruct((2, total, LANES), f32),
+            jax.ShapeDtypeStruct((macros, 7, planes, cells), f32),
+            jax.ShapeDtypeStruct((macros, rows, cells), f32),
+            jax.ShapeDtypeStruct((macros, rows, cells), f32),
+        ),
+        scratch_shapes=[
+            pltpu.VMEM((depth + 2 * HALO, n, LANES), f32),
+            pltpu.VMEM((rows, sides, LANES), f32),
+            pltpu.VMEM((sides, rows, LANES), f32),
+            pltpu.VMEM((7, rows, cells), f32),
+            pltpu.VMEM((macros, 2, rows, LANES), f32),
+        ],
+    )
+
+
+def third_kernel(n_dom, n_sub, macros, planes, cells, slots, recv_rows):
+    rows = planes + 2 * HALO
+    sides = 2 * macros
+    depth = n_sub * planes
+
+    def body(recv_ref, first_ref, same_ref, base_ref, dw_ref, e2_ref, c1_ref, c2_ref, edge_ref, pot_ref, sh_ref, own_ref, turn_ref):
+        k = lax.axis_index("sub")
+        d = lax.axis_index("dom")
+        b = Boundary(first_ref, n_dom, n_sub, macros, planes)
+        same = same_ref[...]
+        group = b.group
+        mass = b.mass()
+        n = b.rows
+        sh_ref[...] = jnp.zeros_like(sh_ref)
+        nodes = [[None] * planes for _ in range(n_sub)]
+        below = None
+        for layer in range(n_sub):
+            stacked = jnp.concatenate([b.rows_of(recv_ref, layer, p) for p in range(planes)], axis=0)
+            step = group_sum(same, stacked) * dw_ref[min(layer, 1)]
+            for p in range(planes):
+                at = layer * planes + p
+                e2_p = base_ref[at] + step[p * n : (p + 1) * n]
+                sh_ref[HALO + at] = e2_p
+                src = b.rows_of(first_ref, layer, p)
+                r = jnp.where(group < 3, src - mass * e2_p, 0.0)
+                nodes[layer][p] = stacked[p * n : (p + 1) * n] + b.fold(r, below)
+                below = r
+        summed = b.layer_nodes(same, nodes)
+        for layer in range(n_sub):
+            c2 = summed[layer] * dw_ref[min(layer, 1)]
+            for p in range(planes):
+                at = HALO + layer * planes + p
+                sh_ref[at] = jnp.where(group == 3, c2[p * n : (p + 1) * n], sh_ref[at])
+        for i in range(rows):
+            own_ref[i] = sh_ref[k * planes + i, pl.ds(pl.multiple_of(d * sides, sides), sides), :]
+        for ms in range(sides):
+            turn_ref[ms] = own_ref[:, ms, :]
+        plane = Plane((rows, cells))
+
+        def macro_step(m, carry):
+            own = [turn_ref[2 * m], turn_ref[2 * m + 1]]
+            c2 = unpack(own, 3, c2_ref[m])
+            pot_ref[m] = (c1_ref[m] + c2)[HALO : HALO + planes]
+            grad = node_grad(c2, plane)
+            for t in range(7):
+                g = grad[t]
+                if t in SHARED_TYPES:
+                    zero = jnp.zeros((rows, cells), jnp.float32)
+                    g = g + unpack(own, SHARED_TYPES.index(t), zero)
+                edge_ref[m, t] = e2_ref[m, t] + g[HALO : HALO + planes]
+            return carry
+
+        lax.fori_loop(0, macros, macro_step, 0)
+
+    f32 = jnp.float32
+    n = n_dom * sides
+    return pl.pallas_call(
+        body,
+        name="third",
+        out_shape=(
+            jax.ShapeDtypeStruct((macros, 7, planes, cells), f32),
+            jax.ShapeDtypeStruct((macros, planes, cells), f32),
+        ),
+        scratch_shapes=[
+            pltpu.VMEM((depth + 2 * HALO, n, LANES), f32),
+            pltpu.VMEM((rows, sides, LANES), f32),
+            pltpu.VMEM((sides, rows, LANES), f32),
+        ],
+    )
+
+
+def local_small(source, zone_ids, kappa_table, mu_table, owner_dev, owner_group):
+    macros, _, planes, cells = source.shape
+    n_dom, n_sub = lax.axis_size("dom"), lax.axis_size("sub")
+    sizes = (n_dom, n_sub, macros, planes, cells, owner_dev.shape[1], owner_group.shape[1])
+    table = jnp.zeros((16, kappa_table.shape[0]), jnp.float32)
+    table = table.at[0:7].set(kappa_table.T).at[8:16].set(mu_table.T)
+    up = [(i, i + 1) for i in range(n_sub - 1)]
+    down = [(i + 1, i) for i in range(n_sub - 1)]
+    low = lax.ppermute(source[:, :, planes - HALO :], "sub", up)
+    high = lax.ppermute(source[:, :, :HALO], "sub", down)
+    pay, coef, w, nw = first_kernel(*sizes)(zone_ids, table, source, owner_dev, owner_group)
+    everyone = ("dom", "sub")
+    recv = lax.all_to_all(pay, everyone, 0, 0)
+    pay, same, base, dw, e2, c1, c2 = second_kernel(*sizes)(recv, source, low, high, coef, w, nw)
+    again = lax.all_to_all(pay, everyone, 0, 0)
+    return third_kernel(*sizes)(again, recv, same, base, dw, e2, c1, c2)
+
+
+def fits_small(mesh, source, owner_dev, owner_group):
+    macros = source.shape[0] // mesh.shape["dom"]
+    planes = source.shape[2] // mesh.shape["sub"]
+    return (
+        macros == 4
+        and planes == 4
+        and source.shape[3] == LAT * LAT
+        and mesh.shape["sub"] == 4
+        and owner_dev.shape[1] == 2 * macros * planes
+        and owner_group.shape[1] == 32
+        and mesh.shape["dom"] <= 8
+    )
+
+
 def solution(mesh):
     in_specs = (
         P("dom", None, "sub", None),
@@ -278,4 +855,12 @@
         P("dom", None),
     )
     out_specs = (P("dom", None, "sub", None), P("dom", "sub", None))
-    return jax.shard_map(local, mesh=mesh, in_specs=in_specs, out_specs=out_specs, check_vma=False)
+
+    def step(source, zone_ids, kappa_table, mu_table, owner_dev, owner_group):
+        body = local_small if fits_small(mesh, source, owner_dev, owner_group) else local
+        mapped = jax.shard_map(
+            body, mesh=mesh, in_specs=in_specs, out_specs=out_specs, check_vma=False
+        )
+        return mapped(source, zone_ids, kappa_table, mu_table, owner_dev, owner_group)
+
+    return step

time: 228 us -> 66 us (0.29)
  local copies, waits for them, and re-layouts: 74.5 us -> 2.35 us
  starting transfers between devices: 54.3 us -> 12.6 us
  waiting for transfers between devices: 35.8 us -> 12 us
  other arithmetic: 23.6 us -> 0 us
  Pallas kernels: 0 us -> 18.3 us
  blocking collectives: 31.2 us -> 18.9 us
  matrix products: 4.37 us -> 0 us
    scatter x24 -> x2, local copies, waits for them, and re-layouts: 32.7 us -> 0.7 us  [local_small(): table = table.at[0:7].set(kappa_table.T).at[8:16].set(mu_table.T)]
    ppermute x9 -> x2, starting transfers between devices: 26.9 us -> 5.56 us  [the longest x1 3.4 us: local_small(): low = lax.ppermute(source[:, :, planes - HALO:], 'sub', up)]
    all_to_all x6 -> x1, starting transfers between devices: 27.4 us -> 7.08 us  [local_small(): recv = lax.all_to_all(pay, everyone, 0, 0)]
    pallas_call x0 -> x3, Pallas kernels: none -> 18.3 us  [the longest x1 9.03 us: local_small(): second_kernel(*sizes)(recv, source, low, high, coef, w, nw)]
    ppermute x9 -> x2, waiting for transfers between devices: 18.1 us -> 4.62 us  [the longest x1 4.61 us: local_small(): high = lax.ppermute(source[:, :, :HALO], 'sub', down)]
    all_to_all x4 -> x1, blocking collectives: 31.2 us -> 18.9 us  [local_small(): again = lax.all_to_all(pay, everyone, 0, 0)]
    another operation x32 -> x0, local copies, waits for them, and re-layouts: 10.6 us -> none
    all_to_all x6 -> x1, waiting for transfers between devices: 17.7 us -> 7.41 us  [local_small(): recv = lax.all_to_all(pay, everyone, 0, 0)]
  transfers between devices with their start and end apart: 15 -> 3, of which waited for: 11 -> 2; matrix products, arithmetic and copies ran while one was open for 13% -> 0% of each run, Pallas kernels for 0% -> 0%
where the time goes in v1:
time: 66 us; the launch traced here: 64.9 us
  blocking collectives  18.9 us (29%)
  Pallas kernels  18.3 us (28%)
  starting transfers between devices  12.6 us (19%)
  waiting for transfers between devices  12 us (18%)
  local copies, waits for them, and re-layouts  2.35 us (4%)
  between operations  0.69 us (1%)
    all_to_all x1, blocking collectives, local_small(): again = lax.all_to_all(pay, everyone, 0, 0)  18.9 us
    pallas_call x1, Pallas kernels, local_small(): second_kernel(*sizes)(recv, source, low, high, coef, w, nw)  9.03 us
    all_to_all x1, waiting for transfers between devices, local_small(): recv = lax.all_to_all(pay, everyone, 0, 0)  7.41 us
    all_to_all x1, starting transfers between devices, local_small(): recv = lax.all_to_all(pay, everyone, 0, 0)  7.08 us
    pallas_call x1, Pallas kernels, local_small(): return third_kernel(*sizes)(again, recv, same, base, dw, e2, c1, c2)  4.78 us
    ppermute x1, waiting for transfers between devices, local_small(): high = lax.ppermute(source[:, :, :HALO], 'sub', down)  4.61 us
    pallas_call x1, Pallas kernels, local_small(): first_kernel(*sizes)(zone_ids, table, source, owner_dev, owner_group)  4.47 us
    ppermute x1, starting transfers between devices, local_small(): low = lax.ppermute(source[:, :, planes - HALO:], 'sub', up)  3.4 us
  transfers between devices with their start and end apart: 3, of which 2 were waited for; matrix products, arithmetic and copies ran while one was open for 0% of the time, Pallas kernels for 0%

profile of v1, /device:TPU:1, one launch (start us, length us, event | category | flops | bytes accessed | tf_op | source)
XLA Modules:
  0.0 64.9 jit_solution(3989127043218092792)
XLA Ops:
  0.6 0.0 copy-start.5
  0.6 0.7 %scatter.6 = f32[16,16]{1,0:T(8,128)S(1)} pad(f32[7,16]{1,0:T(8,128)} %bitcast.3, f32[]{:T(128)} %constant.54.clone.1), padding=0_9x0_0 | pad | bytes 1476 | tf_op jit(solution)/shard_map/scatter | solution.py:821
  1.3 0.0 copy-done.5
  1.3 0.0 copy-start.4
  1.3 0.6 copy-done.4
  1.9 4.5 %first.1 = (f32[32,40,128]{2,1,0:T(8,128)}, f32[4,16,1024]{2,1,0:T(8,128)}, f32[4,7,8,1024]{3,2,1,0:T(8,128)}, f32[4,8,1024]{2,1,0:T(8,128)}) custom-call(s32[4,1024]{1,0:T(4,128)} %zone_ref.1, f32[16,16]{1,0:T(8,128)} %copy-done.4, f32[4,7,4,1024]{3,2,1,0:T(4,128)} %source_ref.3, s32[1,32]{1,0:T(1,128)} %owner_ref.1, s32[1,32]{1,0:T(1,128)} %group_ref.1), custom_call_target="tpu_custom_call" | custom-call | tf_op jit(solution)/shard_map/first/pallas_call | solution.py:826
  6.4 0.0 copy-start.1
  6.4 7.1 %all-to-all-start = ((f32[32,40,128]{2,1,0:T(8,128)}), f32[32,40,128]{2,1,0:T(8,128)S(1)}, u32[]{:S(2)}, u32[]{:S(2)}) async-start(f32[32,40,128]{2,1,0:T(8,128)} %get-tuple-element.37), calls=%async_computation | async-start | bytes 1310720 | tf_op jit(solution)/shard_map/all_to_all | solution.py:828
  13.5 0.0 copy-done.1
  13.5 0.2 fusion
  13.7 2.2 %collective-permute-start.1 = (f32[4,7,2,1024]{3,2,1,0:T(2,128)S(1)}, f32[4,7,2,1024]{3,2,1,0:T(2,128)S(1)}, u32[]{:S(2)}, u32[]{:S(2)}) collective-permute-start(f32[4,7,2,1024]{3,2,1,0:T(2,128)S(1)} %get-tuple-element.48), channel_id=1, source_target_pairs={{1,0},{2,1},{3,2},{5,4},{6,5},{7,6},{9,8},{10,9},{11,10},{13,12},{... | collective-permute-start | bytes 688136 | tf_op jit(solution)/shard_map/ppermute | solution.py:825
  15.9 3.4 %collective-permute-start = (f32[4,7,2,1024]{3,2,1,0:T(2,128)S(1)}, f32[4,7,2,1024]{3,2,1,0:T(2,128)S(1)}, u32[]{:S(2)}, u32[]{:S(2)}) collective-permute-start(f32[4,7,2,1024]{3,2,1,0:T(2,128)S(1)} %get-tuple-element.49), channel_id=1, source_target_pairs={{0,1},{1,2},{2,3},{4,5},{5,6},{6,7},{8,9},{9,10},{10,11},{12,13},{... | collective-permute-start | bytes 688136 | tf_op jit(solution)/shard_map/ppermute | solution.py:824
  19.3 4.6 %collective-permute-done.1.high_ref = f32[4,7,2,1024]{3,2,1,0:T(2,128)S(1)} collective-permute-done((f32[4,7,2,1024]{3,2,1,0:T(2,128)S(1)}, f32[4,7,2,1024]{3,2,1,0:T(2,128)S(1)}, u32[]{:S(2)}, u32[]{:S(2)}) %collective-permute-start.1) | collective-permute-done | bytes 229408 | tf_op jit(solution)/shard_map/ppermute | solution.py:825
  23.9 0.0 copy-start.2
  23.9 0.0 collective-permute-done.low_ref
  23.9 0.0 copy-start.3
  23.9 7.4 %all-to-all-done.recv_ref.first_ref = f32[32,40,128]{2,1,0:T(8,128)S(1)} async-done(((f32[32,40,128]{2,1,0:T(8,128)}), f32[32,40,128]{2,1,0:T(8,128)S(1)}, u32[]{:S(2)}, u32[]{:S(2)}) %all-to-all-start) | async-done | bytes 655392 | tf_op jit(solution)/shard_map/all_to_all | solution.py:828
  31.3 0.0 copy-start
  31.3 0.0 copy-done.2
  31.3 0.0 copy-done.3
  31.3 0.9 %copy-done = f32[32,40,128]{2,1,0:T(8,128)} copy-done((f32[32,40,128]{2,1,0:T(8,128)}, f32[32,40,128]{2,1,0:T(8,128)S(1)}, u32[]{:S(2)}) %copy-start) | copy-done | bytes 655384
  32.2 9.0 %second.1 = (f32[32,32,128]{2,1,0:T(8,128)}, bf16[256,256]{1,0:T(8,128)(2,1)}, f32[16,64,128]{2,1,0:T(8,128)}, f32[2,256,128]{2,1,0:T(8,128)}, f32[4,7,4,1024]{3...) custom-call(f32[32,40,128]{2,1,0:T(8,128)} %copy-done, f32[4,7,4,1024]{3,2,1,0:T(4,128)} %source_ref.3, ...), custom_call_target="tpu_custom_call" | custom-call | tf_op jit(solution)/shard_map/second/pallas_call | solution.py:829
  41.2 18.9 %all_to_all.10.recv_ref = f32[32,32,128]{2,1,0:T(8,128)} all-to-all(f32[32,32,128]{2,1,0:T(8,128)} %get-tuple-element.41), channel_id=1, replica_groups=mesh['dom'=8,'sub'=4] {'dom','sub'}, dimensions={0} | all-to-all | bytes 1048576 | tf_op jit(solution)/shard_map/all_to_all | solution.py:830
  60.1 4.8 %third.1 = (f32[4,7,4,1024]{3,2,1,0:T(4,128)}, f32[4,4,1024]{2,1,0:T(4,128)}) custom-call(f32[32,32,128]{2,1,0:T(8,128)} %all_to_all.10.recv_ref, f32[32,40,128]{2,1,0:T(8,128)} %copy-done, bf16[256,256]{1,0:T(8,128)(2,1)} %get-tuple-element.42.same_ref, f32[16,64,128]{2,1,0:T(8,128)} %get-tuple-element.43.base_ref, ...), custom_call_target="tpu_custom_call" | custom-call | tf_op jit(solution)/shard_map/third/pallas_call | solution.py:831
  (1 shorter events, 0.0 us)
Async XLA Ops:
  0.6 0.7 %copy-start.5 = (f32[16,8]{0,1:T(8,128)S(1)}, f32[16,8]{0,1:T(8,128)}, u32[]{:S(2)}) copy-start(f32[16,8]{0,1:T(8,128)} %param.13) | copy-start | bytes 1540
  1.3 0.6 copy-start.4
  6.4 7.1 %copy-start.1 = (f32[4,7,4,1024]{3,2,1,0:T(4,128)S(1)}, f32[4,7,4,1024]{3,2,1,0:T(4,128)}, u32[]{:S(2)}) copy-start(f32[4,7,4,1024]{3,2,1,0:T(4,128)} %source_ref.3) | copy-start | bytes 1376260
  6.4 24.9 %all-to-all-start = ((f32[32,40,128]{2,1,0:T(8,128)}), f32[32,40,128]{2,1,0:T(8,128)S(1)}, u32[]{:S(2)}, u32[]{:S(2)}) async-start(f32[32,40,128]{2,1,0:T(8,128)} %get-tuple-element.37), calls=%async_computation | async-start | bytes 1310720 | tf_op jit(solution)/shard_map/all_to_all | solution.py:828
  13.7 10.2 %collective-permute-start.1 = (f32[4,7,2,1024]{3,2,1,0:T(2,128)S(1)}, f32[4,7,2,1024]{3,2,1,0:T(2,128)S(1)}, u32[]{:S(2)}, u32[]{:S(2)}) collective-permute-start(f32[4,7,2,1024]{3,2,1,0:T(2,128)S(1)} %get-tuple-element.48), channel_id=1, source_target_pairs={{1,0},{2,1},{3,2},{5,4},{6,5},{7,6},{9,8},{10,9},{11,10},{13,12},{... | collective-permute-start | bytes 688136 | tf_op jit(solution)/shard_map/ppermute | solution.py:825
  15.9 8.0 %collective-permute-start = (f32[4,7,2,1024]{3,2,1,0:T(2,128)S(1)}, f32[4,7,2,1024]{3,2,1,0:T(2,128)S(1)}, u32[]{:S(2)}, u32[]{:S(2)}) collective-permute-start(f32[4,7,2,1024]{3,2,1,0:T(2,128)S(1)} %get-tuple-element.49), channel_id=1, source_target_pairs={{0,1},{1,2},{2,3},{4,5},{5,6},{6,7},{8,9},{9,10},{10,11},{12,13},{... | collective-permute-start | bytes 688136 | tf_op jit(solution)/shard_map/ppermute | solution.py:824
  23.9 7.4 %copy-start.2 = (f32[4,7,2,1024]{3,2,1,0:T(2,128)}, f32[4,7,2,1024]{3,2,1,0:T(2,128)S(1)}, u32[]{:S(2)}) copy-start(f32[4,7,2,1024]{3,2,1,0:T(2,128)S(1)} %collective-permute-done.1.high_ref) | copy-start | bytes 688132
  23.9 7.4 %copy-start.3 = (f32[4,7,2,1024]{3,2,1,0:T(2,128)}, f32[4,7,2,1024]{3,2,1,0:T(2,128)S(1)}, u32[]{:S(2)}) copy-start(f32[4,7,2,1024]{3,2,1,0:T(2,128)S(1)} %collective-permute-done.low_ref) | copy-start | bytes 688132
  31.3 0.9 %copy-start = (f32[32,40,128]{2,1,0:T(8,128)}, f32[32,40,128]{2,1,0:T(8,128)S(1)}, u32[]{:S(2)}) copy-start(f32[32,40,128]{2,1,0:T(8,128)S(1)} %all-to-all-done.recv_ref.first_ref) | copy-start | bytes 1966084

commit v2 on v0

--- a/solution.py
+++ b/solution.py
@@ -1,7 +1,10 @@
 import jax
 import jax.numpy as jnp
 from jax import lax
+from jax.experimental import pallas as pl
+from jax.experimental.pallas import tpu as pltpu
 from jax.sharding import PartitionSpec as P
+
 
 LAT = 32
 SWEEPS = 2
@@ -152,7 +155,7 @@
 
 
 def edge_sides(values):
-    macro_count, type_count, plane_count, cell_count = values.shape
+    macro_count, type_count, plane_count, _ = values.shape
     lattice = values.reshape(macro_count, type_count, plane_count, LAT, LAT)
     chosen = jnp.stack([lattice[:, edge_type] for edge_type in SHARED_TYPES], axis=1)
     sides = jnp.stack([chosen[..., 0], chosen[..., LAT - 1]], axis=1)
@@ -160,7 +163,7 @@
 
 
 def insert_edges(values, blocks):
-    macro_count, type_count, plane_count, cell_count = values.shape
+    macro_count, type_count, plane_count, _ = values.shape
     shaped = blocks.reshape(macro_count, 2, plane_count, 3, LAT)
     shaped = jnp.transpose(shaped, (0, 1, 3, 2, 4))
     lattice = values.reshape(macro_count, type_count, plane_count, LAT, LAT)
@@ -171,14 +174,14 @@
 
 
 def node_sides(values):
-    macro_count, plane_count, cell_count = values.shape
+    macro_count, plane_count, _ = values.shape
     lattice = values.reshape(macro_count, plane_count, LAT, LAT)
     sides = jnp.stack([lattice[..., 0], lattice[..., LAT - 1]], axis=1)
     return sides.reshape(-1, LAT)
 
 
 def insert_nodes(values, blocks):
-    macro_count, plane_count, cell_count = values.shape
+    macro_count, plane_count, _ = values.shape
     shaped = blocks.reshape(macro_count, 2, plane_count, LAT)
     lattice = values.reshape(macro_count, plane_count, LAT, LAT)
     for side_index, column in ((0, 0), (1, LAT - 1)):
@@ -268,6 +271,882 @@
     return (edge_field, potential)
 
 
+LANES = 128
+HALO = 2
+VMEM_BYTES = 24 * 1024 * 1024
+LOOSE_TYPES = (0, 3, 4, 6)
+
+
+def lane_roll(v, s):
+    s = s % v.shape[-1]
+    return pltpu.roll(v, s, v.ndim - 1) if s else v
+
+
+def row_roll(v, s):
+    s = s % v.shape[0]
+    return pltpu.roll(v, s, 0) if s else v
+
+
+def iota(shape, dim):
+    return lax.broadcasted_iota(jnp.int32, shape, dim)
+
+
+def zb(v):
+    return row_roll(v, 1)
+
+
+def za(v):
+    return row_roll(v, -1)
+
+
+class Plane:
+    def __init__(self, shape):
+        self.lane = iota(shape, 1)
+        self.x = self.lane & (LAT - 1)
+        self.cells = shape[1]
+        self.side = (self.x == 0) | (self.x == LAT - 1)
+
+    def ax(self, v):
+        return jnp.where(self.x < LAT - 1, lane_roll(v, -1), 0.0)
+
+    def ay(self, v):
+        return jnp.where(self.lane < self.cells - LAT, lane_roll(v, -LAT), 0.0)
+
+    def bx(self, v):
+        return jnp.where(self.x > 0, lane_roll(v, 1), 0.0)
+
+    def by(self, v):
+        return jnp.where(self.lane >= LAT, lane_roll(v, LAT), 0.0)
+
+    def bxy(self, v):
+        return jnp.where((self.lane >= LAT) & (self.x > 0), lane_roll(v, LAT + 1), 0.0)
+
+    def axy(self, v):
+        inner = (self.lane < self.cells - LAT) & (self.x < LAT - 1)
+        return jnp.where(inner, lane_roll(v, -LAT - 1), 0.0)
+
+
+def yb(v):
+    lane = iota(v.shape, 1)
+    first = jnp.where(lane < 4, 0.0, lane_roll(v, 36))
+    return jnp.where(lane < 32, first, lane_roll(v, 32))
+
+
+def ya(v):
+    lane = iota(v.shape, 1)
+    last = jnp.where(lane >= 124, 0.0, lane_roll(v, -36))
+    return jnp.where(lane >= 96, last, lane_roll(v, -32))
+
+
+class Strip:
+    def __init__(self, shape):
+        half = shape[0] // 2
+        self.col = iota(shape, 1) & 3
+        self.upper = iota(shape, 0) >= half
+        self.own = self.col == 0
+
+    def ax(self, v):
+        wrap = jnp.where(self.upper, lane_roll(v, 3), 0.0)
+        step = jnp.where(self.upper & self.own, 0.0, lane_roll(v, -1))
+        return jnp.where(self.col == 3, wrap, step)
+
+    def bx(self, v):
+        wrap = jnp.where(self.upper, lane_roll(v, -3), 0.0)
+        step = jnp.where(self.upper & (self.col == 1), 0.0, lane_roll(v, 1))
+        return jnp.where(self.own, wrap, step)
+
+    def ay(self, v):
+        return ya(v)
+
+    def by(self, v):
+        return yb(v)
+
+    def bxy(self, v):
+        return yb(self.bx(v))
+
+    def axy(self, v):
+        return ya(self.ax(v))
+
+
+def to_strip(v):
+    lane = iota((v.shape[0], LANES), 1)
+    block = (lane & 31) >> 2
+    low = jnp.zeros((v.shape[0], LANES), v.dtype)
+    high = low
+    for c in range(8):
+        column = v[:, LANES * c : LANES * (c + 1)]
+        low = jnp.where(block == c, lane_roll(column, 4 * c), low)
+        high = jnp.where(block == c, lane_roll(column, 4 * c - 28), high)
+    high = jnp.where((lane & 3) == 0, lane_roll(high, -3), lane_roll(high, 1))
+    return jnp.concatenate([low, high], axis=0)
+
+
+def plus(*terms):
+    total = None
+    for term in terms:
+        if term is not None:
+            total = term if total is None else total + term
+    return total
+
+
+def on(f, v):
+    return None if v is None else f(v)
+
+
+def minus(v):
+    return on(lambda a: -a, v)
+
+
+def times(c, v):
+    return on(lambda a: c * a, v)
+
+
+def table_lookup(zone, table_ref, width):
+    out = [jnp.zeros(zone.shape, jnp.float32)] * width
+    for z in range(table_ref.shape[1]):
+        hit = zone == z
+        out = [jnp.where(hit, table_ref[i, z], v) for i, v in enumerate(out)]
+    return out
+
+
+def diagonals(mass, mu, sh):
+    flat = [
+        mass[0] + mu[0] + mu[2] + sh.by(mu[1]),
+        mass[1] + mu[1] + mu[4] + sh.bx(mu[0]),
+        mass[2] + mu[3] + mu[5] + mu[7] + sh.bx(mu[2]) + sh.by(mu[4]) + sh.bxy(mu[6]),
+        mass[3] + mu[0] + mu[1] + mu[6],
+        mass[4] + mu[2] + mu[3],
+        mass[5] + mu[4] + mu[5],
+        mass[6] + mu[6] + mu[7],
+    ]
+    rise = {0: mu[3], 1: mu[5], 3: mu[7]}
+    node_flat = sh.bx(mass[0]) + sh.by(mass[1]) + sh.bxy(mass[3])
+    for t in range(7):
+        node_flat = node_flat + mass[t]
+    node_rise = mass[2] + sh.bx(mass[4]) + sh.by(mass[5]) + sh.bxy(mass[6])
+    return flat, rise, node_flat, node_rise
+
+
+def grad_at(c, c_up, sh, types=range(7)):
+    moves = (sh.ax, sh.ay, lambda v: v, sh.axy, sh.ax, sh.ay, sh.axy)
+    out = [None] * 7
+    for t in types:
+        out[t] = plus(on(moves[t], c_up if EDGE_OFFSETS[t][0] else c), minus(c))
+    return out
+
+
+def back_at(r, r_below, sh):
+    return plus(
+        minus(plus(*r)),
+        r_below[2],
+        on(sh.bx, plus(r[0], r_below[4])),
+        on(sh.by, plus(r[1], r_below[5])),
+        on(sh.bxy, plus(r[3], r_below[6])),
+    )
+
+
+NONE7 = [None] * 7
+
+
+def first_kernel(n_dom, n_sub, macros, planes, cells):
+    sides = 2 * macros
+    blocks = 2 * planes
+
+    def body(kappa_ref, mu_ref, zone_ref, source_ref, pay_ref, coef_ref, hold_ref):
+        k = lax.axis_index("sub")
+        shape = (sides, LANES)
+        sh = Strip(shape)
+        row = iota(shape, 0)
+        group = iota(shape, 1) & 3
+        zone = to_strip(zone_ref[...])
+        mass = table_lookup(zone, kappa_ref, 7)
+        mu = table_lookup(zone, mu_ref, 8)
+        flat, rise, node_flat, node_rise = diagonals(mass, mu, sh)
+        w = [EDGE_DAMPING / (flat[t] + rise[t] if t in rise else flat[t]) for t in range(7)]
+        w_low = [EDGE_DAMPING / flat[t] if t in rise else w[t] for t in range(7)]
+        lowest = k == 0
+        w_zero = [jnp.where(lowest, w_low[t], w[t]) for t in range(7)]
+        nw = NODE_DAMPING / (node_flat + node_rise)
+        nw_zero = jnp.where(lowest, NODE_DAMPING / node_flat, nw)
+        for i, v in enumerate(mass + mu + w + w_zero + [nw, nw_zero]):
+            coef_ref[i] = v
+        has_below = jnp.where(lowest, 0.0, 1.0)
+        has_above = jnp.where(k == n_sub - 1, 0.0, 1.0)
+
+        def loose(t, v):
+            return jnp.where(sh.own, 0.0, v) if t in SHARED_TYPES else v
+
+        def flagged(p, v):
+            flag = has_below if p < 0 else has_above if p >= planes else None
+            return v if flag is None or v is None else v * flag
+
+        src = {p: [to_strip(source_ref[:, t, p, :]) for t in range(7)] for p in range(planes)}
+        e1, r1 = {}, {}
+        for p in range(planes):
+            wp = w_zero if p == 0 else w
+            e1[p] = [loose(t, wp[t] * src[p][t]) for t in range(7)]
+            r1[p] = [loose(t, src[p][t] - mass[t] * e1[p][t]) for t in range(7)]
+        n1, c1 = {}, {}
+        for p in range(planes + 1):
+            n1[p] = back_at(r1.get(p, NONE7), r1.get(p - 1, NONE7), sh)
+            c1[p] = jnp.where(sh.own, 0.0, (nw_zero if p == 0 else nw) * n1[p])
+            c1[p] = flagged(p, c1[p])
+        faces = {}
+        for p in range(-1, planes):
+            e, e_up = e1.get(p, NONE7), e1.get(p + 1, NONE7)
+            far = (
+                on(sh.ax, e[1]),
+                on(sh.ay, e[0]),
+                on(sh.ax, e[2]),
+                e_up[0],
+                on(sh.ay, e[2]),
+                e_up[1],
+                on(sh.axy, e[2]),
+                e_up[3],
+            )
+            faces[p] = [
+                flagged(p, times(mu[f], plus(e[a], far[f], minus(e[g]))))
+                for f, (a, _, g) in enumerate(FACE_EDGES)
+            ]
+        res, r2 = {}, {}
+        none8 = [None] * 8
+        for p in range(-1, planes + 1):
+            f, f_below = faces.get(p, none8), faces.get(p - 1, none8)
+            curled = [
+                plus(f[0], f[2], on(sh.by, f[1]), f_below[3]),
+                plus(f[1], f[4], on(sh.bx, f[0]), f_below[5]),
+                plus(f[3], f[5], f[7], on(sh.bx, f[2]), on(sh.by, f[4]), on(sh.bxy, f[6])),
+                plus(f[6], f_below[7], minus(f[0]), minus(f[1])),
+                minus(plus(f[2], f[3])),
+                minus(plus(f[4], f[5])),
+                minus(plus(f[6], f[7])),
+            ]
+            grad = grad_at(c1.get(p), c1.get(p + 1), sh)
+            wp = w_zero if p == 0 else w
+            res[p], r2[p] = [], []
+            for t in range(7):
+                g = grad[t]
+                value = plus(
+                    r1.get(p, NONE7)[t], minus(curled[t]), minus(times(mass[t], g))
+                )
+                res[p].append(value)
+                e2 = plus(e1.get(p, NONE7)[t], g, times(wp[t], value))
+                s = src[p][t] if p in src else None
+                left = flagged(p, plus(s, minus(times(mass[t], e2))))
+                r2[p].append(on(lambda v: loose(t, v), left))
+        n2 = {p: back_at(r2.get(p, NONE7), r2.get(p - 1, NONE7), sh) for p in range(-1, planes + 2)}
+
+        def merge(g0, g1, g2, g3):
+            out = jnp.where(group == 1, lane_roll(g1, 1), g0)
+            out = jnp.where(group == 2, lane_roll(g2, 2), out)
+            return jnp.where(group == 3, lane_roll(g3, 3), out)
+
+        high = jnp.where(row < macros, row_roll(n2[planes + 1], macros), n1[planes])
+        spare = [flagged(-1, res[-1][2]), high, n2[-1], n2[planes]]
+        for p in range(planes):
+            hold_ref[p * sides : (p + 1) * sides, :] = merge(src[p][1], src[p][2], src[p][5], n1[p])
+            at = planes + p
+            hold_ref[at * sides : (at + 1) * sides, :] = merge(res[p][1], res[p][2], spare[p], n2[p])
+        block = hold_ref[...]
+        for dest in range(n_dom * n_sub):
+            pay_ref[dest] = block
+
+    f32 = jnp.float32
+    smem = pl.BlockSpec(memory_space=pltpu.SMEM)
+    vmem = pl.BlockSpec(memory_space=pltpu.VMEM)
+    return pl.pallas_call(
+        body,
+        compiler_params=pltpu.CompilerParams(vmem_limit_bytes=VMEM_BYTES),
+        name="first",
+        in_specs=[smem, smem, vmem, vmem],
+        out_shape=(
+            pltpu.VMEM((n_dom * n_sub, blocks * sides, LANES), f32),
+            pltpu.VMEM((31, sides, LANES), f32),
+        ),
+        scratch_shapes=[pltpu.VMEM((blocks * sides, LANES), f32)],
+    )
+
+
+def label_kernel(n_dom, n_sub, macros, planes, cells, slots, recv_rows):
+    sides = 2 * macros
+    capacity = recv_rows // n_dom
+
+    def body(zone_ref, owner_ref, group_ref, pay_ref):
+        d = lax.axis_index("dom")
+        shape = (sides, LANES)
+        row = iota(shape, 0)
+        group = iota(shape, 1) & 3
+        owner = owner_ref[...].astype(jnp.float32)
+        si, sj = iota((slots, slots), 0), iota((slots, slots), 1)
+        column = jnp.sum(jnp.where(si == sj, owner, 0.0), axis=1, keepdims=True)
+        lower = jnp.where((column == owner) & (si < sj), 1.0, 0.0)
+        position = jnp.sum(lower, axis=0, keepdims=True)
+        flat_index = owner * recv_rows + (d * capacity).astype(jnp.float32) + position
+        keyed = group_ref[...].astype(jnp.float32) + (d * recv_rows).astype(jnp.float32)
+
+        def spread_lanes(values):
+            count = values.shape[1]
+            place = iota((count, LANES), 0)
+            place = 32 * (place >> 3) + 4 * (place & 7) + 3
+            hot = jnp.where(place == iota((count, LANES), 1), 1.0, 0.0)
+            rows = jnp.broadcast_to(values, (sides, count))
+            return jnp.dot(rows, hot, precision=lax.Precision.HIGHEST)
+
+        index = jnp.where(row < macros, spread_lanes(flat_index), spread_lanes(keyed))
+        zone = to_strip(zone_ref[...]).astype(jnp.float32)
+        block = jnp.where(group == 2, lane_roll(zone, -1), lane_roll(zone, 1))
+        block = jnp.where(group == 3, index, block)
+        pay_ref[...] = block
+
+    return pl.pallas_call(
+        body,
+        compiler_params=pltpu.CompilerParams(vmem_limit_bytes=VMEM_BYTES),
+        name="label",
+        out_shape=pltpu.VMEM((sides, LANES), jnp.float32),
+    )
+
+
+def inner_kernel(n_dom, n_sub, macros, planes, cells):
+    rows = planes + 2 * HALO
+
+    def body(kappa_ref, mu_ref, zone_ref, source_ref, low_ref, high_ref, edge_ref, pot_ref, coef_ref, sx_ref, w_ref):
+        k = lax.axis_index("sub")
+        sh = Plane((rows, cells))
+        at = k * planes - HALO + iota((rows, cells), 0)
+        inside, valid = at >= 1, (at >= 0) & (at < n_sub * planes)
+        zones = zone_ref[...]
+        for i, v in enumerate(table_lookup(zones, kappa_ref, 7) + table_lookup(zones, mu_ref, 8)):
+            coef_ref[i] = v
+
+        def macro_step(m, carry):
+            def coef(i):
+                return jnp.broadcast_to(coef_ref[i, pl.ds(m, 1), :], (rows, cells))
+
+            mass = [coef(t) for t in range(7)]
+            mu = [coef(7 + f) for f in range(8)]
+            flat, rise, node_flat, node_rise = diagonals(mass, mu, sh)
+            for t in range(7):
+                diag = flat[t]
+                if t in rise:
+                    diag = diag + jnp.where(inside, rise[t], 0.0)
+                w_ref[t] = EDGE_DAMPING / diag
+            w_ref[7] = NODE_DAMPING / (node_flat + jnp.where(inside, node_rise, 0.0))
+            node_open = valid & jnp.logical_not(sh.side)
+
+            def loose(t, v):
+                return jnp.where(sh.side, 0.0, v) if t in SHARED_TYPES else v
+
+            def node_back(r):
+                own = -(((r[0] + r[1]) + (r[2] + r[3])) + ((r[4] + r[5]) + r[6]))
+                back = zb(r[2]) + sh.bx(r[0] + zb(r[4])) + sh.by(r[1] + zb(r[5]))
+                return jnp.where(node_open, w_ref[7] * (own + back + sh.bxy(r[3] + zb(r[6]))), 0.0)
+
+            def node_grad(c):
+                cx, cy, cxy = sh.ax(c), sh.ay(c), sh.axy(c)
+                ends = (cx, cy, za(c), cxy, za(cx), za(cy), za(cxy))
+                return [jnp.where(valid, end - c, 0.0) for end in ends]
+
+            e, r1 = [], []
+            for t in range(7):
+                sx_ref[t, 0:HALO, :] = low_ref[m, t]
+                sx_ref[t, HALO : HALO + planes, :] = source_ref[m, t]
+                sx_ref[t, HALO + planes : rows, :] = high_ref[m, t]
+            for t in range(7):
+                e.append(loose(t, w_ref[t] * sx_ref[t]))
+                r1.append(loose(t, sx_ref[t] - mass[t] * e[t]))
+            c1 = node_back(r1)
+            grad = node_grad(c1)
+            far = (
+                sh.ax(e[1]),
+                sh.ay(e[0]),
+                sh.ax(e[2]),
+                za(e[0]),
+                sh.ay(e[2]),
+                za(e[1]),
+                sh.axy(e[2]),
+                za(e[3]),
+            )
+            f = [
+                jnp.where(valid, mu[i] * (e[a] + far[i] - e[g]), 0.0)
+                for i, (a, _, g) in enumerate(FACE_EDGES)
+            ]
+            curled = [
+                f[0] + f[2] + sh.by(f[1]) + zb(f[3]),
+                f[1] + f[4] + sh.bx(f[0]) + zb(f[5]),
+                f[3] + f[5] + f[7] + sh.bx(f[2]) + sh.by(f[4]) + sh.bxy(f[6]),
+                f[6] + zb(f[7]) - f[0] - f[1],
+                -f[2] - f[3],
+                -f[4] - f[5],
+                -f[6] - f[7],
+            ]
+            e2, left = [], []
+            for t in range(7):
+                res = r1[t] - curled[t] - mass[t] * grad[t]
+                value = jnp.where(valid, loose(t, e[t] + grad[t] + w_ref[t] * res), 0.0)
+                e2.append(value)
+                left.append(loose(t, sx_ref[t] - mass[t] * value))
+            c2 = node_back(left)
+            grad = node_grad(c2)
+            for t in range(7):
+                edge_ref[m, t] = (e2[t] + grad[t])[HALO : HALO + planes]
+            pot_ref[m] = (c1 + c2)[HALO : HALO + planes]
+            return carry
+
+        lax.fori_loop(0, macros, macro_step, 0)
+
+    f32 = jnp.float32
+    smem = pl.BlockSpec(memory_space=pltpu.SMEM)
+    vmem = pl.BlockSpec(memory_space=pltpu.VMEM)
+    return pl.pallas_call(
+        body,
+        compiler_params=pltpu.CompilerParams(vmem_limit_bytes=VMEM_BYTES),
+        name="inner",
+        in_specs=[smem, smem, vmem, vmem, vmem, vmem],
+        out_shape=(
+            pltpu.VMEM((macros, 7, planes, cells), f32),
+            pltpu.VMEM((macros, planes, cells), f32),
+        ),
+        scratch_shapes=[
+            pltpu.VMEM((15, macros, cells), f32),
+            pltpu.VMEM((7, rows, cells), f32),
+            pltpu.VMEM((8, rows, cells), f32),
+        ],
+    )
+
+
+def group_sum(same, block):
+    parts = []
+    rest = block
+    for _ in range(3):
+        parts.append(rest.astype(jnp.bfloat16))
+        rest = rest - parts[-1].astype(jnp.float32)
+    wide = jnp.concatenate([same] * 3, axis=1)
+    return jnp.dot(wide, jnp.concatenate(parts, axis=0), preferred_element_type=jnp.float32)
+
+
+def prepare_kernel(n_dom, n_sub, macros, planes, cells, slots, recv_rows):
+    sides = 2 * macros
+    n = n_dom * sides
+    total = n * planes
+
+    def body(kappa_ref, mu_ref, *refs):
+        same_ref, weight_ref, field_ref, recv_ref = refs[n_dom + 1 :]
+        d = lax.axis_index("dom")
+        for i in range(n_dom):
+            recv_ref[d ^ i] = refs[i][...]
+        shape = (n, LANES)
+        group = iota(shape, 1) & 3
+        index = jnp.concatenate([recv_ref[e] for e in range(n_dom)], axis=0)
+        lane = iota(shape, 1)
+        row = iota(shape, 0) % sides
+        firsts = []
+        for e in range(n_dom):
+            one = recv_ref[e, 0:1, :]
+            firsts.append(jnp.broadcast_to(one, (sides, LANES)))
+        firsts = jnp.concatenate(firsts, axis=0)
+        flat = []
+        for p in range(planes):
+            slot = (2 * (row % macros) + row // macros) * planes + p
+            here = lane == 32 * (slot >> 3) + 4 * (slot & 7) + 3
+            flat.append(jnp.sum(jnp.where(here, firsts, 0.0), axis=1, keepdims=True))
+        flat = jnp.concatenate(flat, axis=0).astype(jnp.int32)
+        owner = flat // recv_rows
+        receive = flat - owner * recv_rows
+        table = jnp.zeros((total, LANES), jnp.float32)
+        for e in range(n_dom):
+            one = recv_ref[e, macros : macros + 1, :]
+            table = jnp.where(owner == e, jnp.broadcast_to(one, (total, LANES)), table)
+        here = iota((total, LANES), 1) == 32 * (receive >> 3) + 4 * (receive & 7) + 3
+        key = jnp.sum(jnp.where(here, table, 0.0), axis=1, keepdims=True)
+        square = (total, total)
+        diagonal = iota(square, 0) == iota(square, 1)
+        key_row = jnp.sum(jnp.where(diagonal, key, 0.0), axis=0, keepdims=True)
+        same = jnp.where(key == key_row, 1.0, 0.0).astype(jnp.bfloat16)
+
+        zone = index.astype(jnp.int32)
+        mass = table_lookup(zone, kappa_ref, 7)
+        mu = table_lookup(zone, mu_ref, 8)
+        upper = (iota(shape, 0) % sides) >= macros
+
+        def near(v):
+            return jnp.where(upper, lane_roll(v, -1), 0.0)
+
+        def place(*fields):
+            out = jnp.zeros(shape, jnp.float32)
+            for g, field in enumerate(fields):
+                if field is not None:
+                    out = jnp.where(group == g, lane_roll(field, g - 1), out)
+            return out
+
+        near_mu = [near(v) for v in mu]
+        near_mass = [near(v) for v in mass]
+        edge_mass = place(mass[1], mass[2], mass[5])
+        e1_low = mass[1] + mu[1] + mu[4] + near_mu[0]
+        e2_diag = mass[2] + mu[3] + mu[5] + mu[7] + near_mu[2] + yb(mu[4]) + yb(near_mu[6])
+        e5_diag = mass[5] + mu[4] + mu[5]
+        node_low = near_mass[0] + yb(mass[1]) + yb(near_mass[3])
+        for t in range(7):
+            node_low = node_low + mass[t]
+        node_diag = node_low + mass[2] + near_mass[4] + yb(mass[5]) + yb(near_mass[6])
+        self_coef = place(mu[1] + near_mu[0], mu[3] + mu[7] + near_mu[2] + yb(near_mu[6]))
+        cross_coef = place(mu[4], mu[5])
+
+        def loose_terms(low):
+            diag = {
+                0: mass[0] + mu[0] + mu[2] + yb(mu[1]),
+                3: mass[3] + mu[0] + mu[1] + mu[6],
+                4: mass[4] + mu[2] + mu[3],
+                6: mass[6] + mu[6] + mu[7],
+            }
+            if not low:
+                diag[0] = diag[0] + mu[3]
+                diag[3] = diag[3] + mu[7]
+            al = {t: mass[t] * (EDGE_DAMPING / diag[t]) for t in LOOSE_TYPES}
+            be = {t: mass[t] * (1.0 - al[t]) for t in LOOSE_TYPES}
+            al_n = {t: near(al[t]) for t in LOOSE_TYPES}
+            be_n = {t: near(be[t]) for t in LOOSE_TYPES}
+            p0 = al[3] * mu[1] + al_n[0] * near_mu[0]
+            r0 = -al[0] * yb(mu[1]) - yb(al_n[3] * near_mu[0])
+            p1 = al[4] * mu[3] + al[6] * mu[7] + al_n[0] * near_mu[2] + yb(al_n[3] * near_mu[6])
+            r1 = -al[0] * mu[3] - al[3] * mu[7] - al_n[4] * near_mu[2] - yb(al_n[6] * near_mu[6])
+            p3 = -(be[0] + be[3] + be[4] + be[6]) - be_n[0] - yb(be_n[3])
+            if not low:
+                p3 = p3 - be_n[4] - yb(be_n[6])
+            return place(p0, p1, None, p3), place(r0, r1)
+
+        terms = (loose_terms(True), loose_terms(False))
+        low_diag = place(e1_low, e2_diag, e5_diag, node_low)
+        high_diag = place(e1_low + mu[5], e2_diag, e5_diag, node_diag)
+
+        blocks = [
+            jnp.concatenate([low_diag] + [high_diag] * (planes - 1), axis=0),
+            jnp.concatenate([high_diag] * planes, axis=0),
+        ]
+        same_ref[...] = same
+        summed = group_sum(same, jnp.concatenate(blocks, axis=1))
+        damp = jnp.where((iota((total, LANES), 1) & 3) == 3, NODE_DAMPING, EDGE_DAMPING)
+        for i in range(2):
+            weight_ref[i] = damp / summed[:, LANES * i : LANES * (i + 1)]
+        out = (edge_mass, self_coef, cross_coef) + terms[0] + terms[1]
+        for i, v in enumerate(out):
+            field_ref[i] = v
+
+    f32 = jnp.float32
+    smem = pl.BlockSpec(memory_space=pltpu.SMEM)
+    vmem = pl.BlockSpec(memory_space=pltpu.VMEM)
+    return pl.pallas_call(
+        body,
+        compiler_params=pltpu.CompilerParams(vmem_limit_bytes=VMEM_BYTES),
+        name="prepare",
+        in_specs=[smem, smem] + [vmem] * (n_dom + 1),
+        out_shape=(
+            pltpu.VMEM((total, total), jnp.bfloat16),
+            pltpu.VMEM((2, total, LANES), f32),
+            pltpu.VMEM((7, n, LANES), f32),
+        ),
+        scratch_shapes=[pltpu.VMEM((n_dom, sides, LANES), f32)],
+    )
+
+
+def solve_kernel(n_dom, n_sub, macros, planes, cells):
+    sides = 2 * macros
+    n = n_dom * sides
+    depth = n_sub * planes
+
+    def body(recv_ref, coef_ref, edge_in, pot_in, same_ref, weight_ref, field_ref, edge_ref, pot_ref, one_ref, two_ref, turn_ref):
+        k = lax.axis_index("sub")
+        d = lax.axis_index("dom")
+        shape = (n, LANES)
+        group = iota(shape, 1) & 3
+        edges = group < 3
+        upper = (iota(shape, 0) % sides) >= macros
+
+        def rows_of(layer, at):
+            parts = [
+                recv_ref[e * n_sub + layer, at * sides : (at + 1) * sides, :] for e in range(n_dom)
+            ]
+            return jnp.concatenate(parts, axis=0)
+
+        same = same_ref[...]
+        blocks = [
+            jnp.concatenate([rows_of(layer, p) for p in range(planes)], axis=0)
+            for layer in range(n_sub)
+        ]
+        summed = group_sum(same, jnp.concatenate(blocks, axis=1))
+
+        def lanes(v, i):
+            return v[:, LANES * i : LANES * (i + 1)]
+
+        weight = [weight_ref[0], weight_ref[1]]
+        edge_mass, self_coef, cross_coef = (field_ref[i] for i in range(3))
+        terms = ((field_ref[3], field_ref[4]), (field_ref[5], field_ref[6]))
+
+        def fold(v):
+            return lane_roll(v, 3) + lane_roll(v, 2) + lane_roll(v, 1)
+
+        def fold_edges(r, r_below):
+            out = jnp.where(group == 0, yb(r), 0.0) - r
+            if r_below is not None:
+                out = out + jnp.where(group == 1, r_below, 0.0)
+                out = out + jnp.where(group == 2, yb(r_below), 0.0)
+            return out
+
+        def node_sums(nodes):
+            block = None
+            for layer in range(n_sub):
+                stacked = jnp.concatenate(nodes[layer], axis=0)
+                moved = lane_roll(stacked, layer - 3)
+                moved = jnp.where((iota(moved.shape, 1) & 3) == layer, moved, 0.0)
+                block = moved if block is None else block + moved
+            out = group_sum(same, block)
+            return [lane_roll(out, 3 - layer) for layer in range(n_sub)]
+
+        def of(v, p):
+            return v[p * n : (p + 1) * n]
+
+        e1, r1 = {}, {}
+        nodes = [[None] * planes for _ in range(n_sub)]
+        for layer in range(n_sub):
+            value = lanes(summed, layer) * weight[min(layer, 1)]
+            for p in range(planes):
+                at = layer * planes + p
+                src = of(blocks[layer], p)
+                e1[at] = jnp.where(edges, of(value, p), 0.0)
+                r1[at] = jnp.where(edges, src - edge_mass * e1[at], 0.0)
+                node = src + fold(fold_edges(r1[at], r1.get(at - 1)))
+                if p == 0 and layer > 0:
+                    shifted = lane_roll(rows_of(layer - 1, planes + 1), 1)
+                    node = node + jnp.where(upper, shifted, 0.0)
+                nodes[layer][p] = node
+        node_sum = node_sums(nodes)
+        c1 = {}
+        for at in range(depth):
+            layer, p = at // planes, at % planes
+            value = of(node_sum[layer], p) * of(weight[min(layer, 1)], p)
+            c1[at] = jnp.where(group == 3, value, 0.0)
+            one_ref[HALO + at] = e1[at] + c1[at]
+
+        cross = {}
+        base = {}
+        for at in range(depth):
+            e = e1[at]
+            first = lane_roll(ya(e), -1) - lane_roll(e, -2)
+            second = -lane_roll(e, -1)
+            if at + 1 in e1:
+                second = second + lane_roll(e1[at + 1], 1)
+            cross[at] = jnp.where(
+                group < 2, cross_coef * (e + jnp.where(group == 0, first, second)), 0.0
+            )
+        second_blocks = []
+        for layer in range(n_sub):
+            stacked = []
+            for p in range(planes):
+                at = layer * planes + p
+                v = cross[at]
+                own0 = v if at == 0 else v + lane_roll(cross[at - 1], -1)
+                own1 = v + lane_roll(yb(v), 1)
+                own2 = -(lane_roll(v, 2) + lane_roll(v, 1))
+                coupled = jnp.where(group == 0, own0, jnp.where(group == 1, own1, own2))
+                c = c1[at]
+                ahead = ya(c)
+                rise0 = lane_roll(ahead - c, -3)
+                if at + 1 in c1:
+                    up = c1[at + 1]
+                    rise1 = lane_roll(up - c, -2)
+                    rise2 = lane_roll(ya(up) - c, -1)
+                else:
+                    rise1, rise2 = lane_roll(-c, -2), lane_roll(-c, -1)
+                rise = jnp.where(group == 0, rise0, jnp.where(group == 1, rise1, rise2))
+                rise = jnp.where(edges, rise, 0.0)
+                base[at] = e1[at] + rise
+                given = jnp.where(group < 2, rows_of(layer, planes + p), 0.0)
+                if p == planes - 1 and layer + 1 < n_sub:
+                    extra = lane_roll(rows_of(layer + 1, planes), -1)
+                    given = given + jnp.where(group == 1, extra, 0.0)
+                res = r1[at] + given - self_coef * e1[at] - coupled - edge_mass * rise
+                stacked.append(jnp.where(edges, res, 0.0))
+            second_blocks.append(jnp.concatenate(stacked, axis=0))
+        summed = group_sum(same, jnp.concatenate(second_blocks, axis=1))
+        e2, r2 = {}, {}
+        for layer in range(n_sub):
+            value = lanes(summed, layer) * weight[min(layer, 1)]
+            for p in range(planes):
+                at = layer * planes + p
+                e2[at] = jnp.where(edges, base[at] + of(value, p), 0.0)
+                src = of(blocks[layer], p)
+                r2[at] = jnp.where(edges, src - edge_mass * e2[at], 0.0)
+                by_p, by_r = terms[min(at, 1)]
+                e = e1[at]
+                behind = yb(e)
+                if at > 0:
+                    behind = jnp.where(group == 1, e1[at - 1], behind)
+                    reach = jnp.where(group < 2, by_r * behind, 0.0)
+                else:
+                    reach = jnp.where(group == 0, by_r * behind, 0.0)
+                inner = fold_edges(r2[at], r2.get(at - 1)) + jnp.where(group < 2, by_p * e, 0.0)
+                node = rows_of(layer, planes + p) + fold(inner + reach) + by_p * c1[at]
+                if p == 0 and layer > 0:
+                    node = node + lane_roll(rows_of(layer - 1, 2 * planes - 1), 1)
+                if p == 1 and layer > 0:
+                    shifted = row_roll(lane_roll(rows_of(layer - 1, planes + 1), 1), macros)
+                    node = node + jnp.where(upper, shifted, 0.0)
+                if p == planes - 1 and layer + 1 < n_sub:
+                    node = node + lane_roll(rows_of(layer + 1, planes + 2), 1)
+                nodes[layer][p] = node
+        node_sum = node_sums(nodes)
+        for at in range(depth):
+            layer, p = at // planes, at % planes
+            value = of(node_sum[layer], p) * of(weight[min(layer, 1)], p)
+            two_ref[HALO + at] = jnp.where(group == 3, value, e2[at])
+        for ref in (one_ref, two_ref):
+            for i in range(HALO):
+                ref[i] = jnp.zeros(shape, jnp.float32)
+                ref[HALO + depth + i] = jnp.zeros(shape, jnp.float32)
+
+        strip = (sides, LANES)
+        sh = Strip(strip)
+        has_below = jnp.where(k == 0, 0.0, 1.0)
+        has_above = jnp.where(k == n_sub - 1, 0.0, 1.0)
+
+        def flagged(p, v):
+            flag = has_below if p < 0 else has_above if p >= planes else None
+            return v if flag is None or v is None else v * flag
+
+        mine = pl.ds(pl.multiple_of(d * sides, sides), sides)
+
+        def taken(ref, p, g):
+            value = ref[k * planes + p + HALO, mine, :]
+            return jnp.where(sh.own, lane_roll(value, -g), 0.0)
+
+        my_mass = [coef_ref[t] for t in range(7)]
+        my_mu = [coef_ref[7 + f] for f in range(8)]
+        loose_r = {}
+        step_e = {}
+        c_one = {p: taken(one_ref, p, 3) for p in range(-1, planes + 2)}
+        faces = {}
+        for p in range(-1, planes + 1):
+            ea, eb = taken(one_ref, p, 0), taken(one_ref, p, 1)
+            faces[p] = (
+                my_mu[0] * sh.ax(ea),
+                my_mu[1] * ea,
+                my_mu[2] * sh.ax(eb),
+                my_mu[3] * eb,
+                my_mu[6] * sh.axy(eb),
+                my_mu[7] * eb,
+            )
+        for p in range(-1, planes + 1):
+            f0, f1, f2, f3, f6, f7 = faces[p]
+            types = LOOSE_TYPES if p >= 0 else (4, 6)
+            grad = grad_at(c_one[p], c_one[p + 1], sh, types)
+            curled = {4: -f2 - f3, 6: -f6 - f7}
+            if p >= 0:
+                below = faces[p - 1]
+                curled[0] = f0 + f2 + yb(f1) + below[3]
+                curled[3] = f6 + below[5] - f0 - f1
+            step_e[p], loose_r[p] = [None] * 7, [None] * 7
+            for t in types:
+                weight_t = coef_ref[22 + t] if p == 0 else coef_ref[15 + t]
+                value = grad[t] - weight_t * (curled[t] + my_mass[t] * grad[t])
+                value = flagged(p, value)
+                step_e[p][t] = value
+                loose_r[p][t] = -my_mass[t] * value
+        c_two = {}
+        for p in range(planes + 1):
+            node = back_at(loose_r[p], loose_r[p - 1], sh)
+            node = (coef_ref[30] if p == 0 else coef_ref[29]) * node
+            node = jnp.where(sh.own, taken(two_ref, p, 3), node)
+            c_two[p] = flagged(p, node)
+
+        def plain(v):
+            return jnp.where(sh.upper, jnp.where(sh.col == 3, lane_roll(v, 3), lane_roll(v, -1)), v)
+
+        for p in range(planes):
+            grad = grad_at(c_two[p], c_two[p + 1], sh)
+            for t in range(7):
+                if t in SHARED_TYPES:
+                    start = taken(two_ref, p, SHARED_TYPES.index(t))
+                else:
+                    start = step_e[p][t]
+                turn_ref[t, :, p, :] = plain(start + grad[t])
+            turn_ref[7, :, p, :] = plain(c_one[p] + c_two[p])
+
+        x = iota((planes, LANES), 1) & (LAT - 1)
+
+        def overlaid(v, low, high):
+            columns = []
+            for c in range(8):
+                add = jnp.where(x >= LAT - 4, lane_roll(high, 28 - 4 * c), 0.0)
+                add = jnp.where(x < 4, lane_roll(low, -4 * c), add)
+                columns.append(v[:, LANES * c : LANES * (c + 1)] + add)
+            return jnp.concatenate(columns, axis=1)
+
+        def macro_step(m, carry):
+            for t in range(7):
+                low, high = turn_ref[t, m], turn_ref[t, macros + m]
+                edge_ref[m, t] = overlaid(edge_in[m, t], low, high)
+            pot_ref[m] = overlaid(pot_in[m], turn_ref[7, m], turn_ref[7, macros + m])
+            return carry
+
+        lax.fori_loop(0, macros, macro_step, 0)
+
+    f32 = jnp.float32
+    return pl.pallas_call(
+        body,
+        compiler_params=pltpu.CompilerParams(vmem_limit_bytes=VMEM_BYTES),
+        name="solve",
+        out_shape=(
+            jax.ShapeDtypeStruct((macros, 7, planes, cells), f32),
+            jax.ShapeDtypeStruct((macros, planes, cells), f32),
+        ),
+        scratch_shapes=[
+            pltpu.VMEM((depth + 2 * HALO, n, LANES), f32),
+            pltpu.VMEM((depth + 2 * HALO, n, LANES), f32),
+            pltpu.VMEM((8, sides, planes, LANES), f32),
+        ],
+    )
+
+
+def near_core(*values):
+    return [pltpu.with_memory_space_constraint(v, pltpu.VMEM) for v in values]
+
+
+def local_small(source, zone_ids, kappa_table, mu_table, owner_dev, owner_group):
+    macros, _, planes, cells = source.shape
+    n_dom, n_sub = lax.axis_size("dom"), lax.axis_size("sub")
+    sizes = (n_dom, n_sub, macros, planes, cells)
+    lists = (owner_dev.shape[1], owner_group.shape[1])
+    up = [(i, i + 1) for i in range(n_sub - 1)]
+    down = [(i + 1, i) for i in range(n_sub - 1)]
+    tables = (kappa_table.T, mu_table.T)
+    far = [pltpu.with_memory_space_constraint(v, pltpu.HBM) for v in (*tables, zone_ids, source)]
+    pay, coef = first_kernel(*sizes)(*far)
+    recv = lax.all_to_all(pay, ("dom", "sub"), 0, 0)
+    labels = label_kernel(*sizes, *lists)(zone_ids, owner_dev, owner_group)
+    labels = [labels]
+    for i in range(1, n_dom):
+        route = [(e, e ^ i) for e in range(n_dom)]
+        labels.append(lax.ppermute(labels[0], "dom", route))
+    low = lax.ppermute(source[:, :, planes - HALO :], "sub", up)
+    high = lax.ppermute(source[:, :, :HALO], "sub", down)
+    edge, pot = inner_kernel(*sizes)(*tables, zone_ids, source, *near_core(low, high))
+    fields = prepare_kernel(*sizes, *lists)(*tables, *near_core(*labels, pot))
+    return solve_kernel(*sizes)(*near_core(recv, coef, edge, pot, *fields))
+
+
+def fits_small(mesh, source, owner_dev, owner_group):
+    macros = source.shape[0] // mesh.shape["dom"]
+    planes = source.shape[2] // mesh.shape["sub"]
+    return (
+        macros == 4
+        and planes == 4
+        and source.shape[3] == LAT * LAT
+        and mesh.shape["sub"] == 4
+        and owner_dev.shape[1] == 2 * macros * planes
+        and owner_group.shape[1] == 32
+        and mesh.shape["dom"] in (1, 2, 4, 8)
+    )
+
+
 def solution(mesh):
     in_specs = (
         P("dom", None, "sub", None),
@@ -278,4 +1157,12 @@
         P("dom", None),
     )
     out_specs = (P("dom", None, "sub", None), P("dom", "sub", None))
-    return jax.shard_map(local, mesh=mesh, in_specs=in_specs, out_specs=out_specs, check_vma=False)
+
+    def step(source, zone_ids, kappa_table, mu_table, owner_dev, owner_group):
+        body = local_small if fits_small(mesh, source, owner_dev, owner_group) else local
+        mapped = jax.shard_map(
+            body, mesh=mesh, in_specs=in_specs, out_specs=out_specs, check_vma=False
+        )
+        return mapped(source, zone_ids, kappa_table, mu_table, owner_dev, owner_group)
+
+    return step

time: 228 us -> 57.7 us (0.25)
  the two profiles are of different devices: /device:TPU:1 before, /device:TPU:0 now
where the time goes in v2:
time: 57.7 us; the launch traced here: 57.4 us
  starting transfers between devices  26 us (45%)
  Pallas kernels  22.5 us (39%)
  waiting for transfers between devices  7.86 us (14%)
  between operations  0.8 us (1%)
    ppermute x7, starting transfers between devices, local_small(): labels.append(lax.ppermute(labels[0], 'dom', route))  15.2 us
    pallas_call x1, Pallas kernels, local_small(): return solve_kernel(*sizes)(*near_core(recv, coef, edge, pot, *fields))  11.8 us
    ppermute x7, waiting for transfers between devices, local_small(): labels.append(lax.ppermute(labels[0], 'dom', route))  7.85 us
    all_to_all x1, starting transfers between devices, local_small(): recv = lax.all_to_all(pay, ('dom', 'sub'), 0, 0)  7.33 us
    pallas_call x1, Pallas kernels, local_small(): pay, coef = first_kernel(*sizes)(*far)  4.61 us
    pallas_call x1, Pallas kernels, local_small(): inner_kernel(*sizes)(*tables, zone_ids, source, *near_core(low, high))  3.56 us
    pallas_call x1, Pallas kernels, local_small(): fields = prepare_kernel(*sizes, *lists)(*tables, *near_core(*labels, pot))  2.37 us
    ppermute x1, starting transfers between devices, local_small(): low = lax.ppermute(source[:, :, planes - HALO:], 'sub', up)  2.17 us
  transfers between devices with their start and end apart: 10, of which 2 were waited for; matrix products, arithmetic and copies ran while one was open for 0% of the time, Pallas kernels for 11%

profile of v2, /device:TPU:0, one launch (start us, length us, event | category | flops | bytes accessed | tf_op | source)
XLA Modules:
  0.0 57.4 jit_solution(10824623120126037823)
XLA Ops:
  0.6 4.6 %first.1 = (f32[32,64,128]{2,1,0:T(8,128)}, f32[31,8,128]{2,1,0:T(8,128)S(1)}) custom-call(f32[7,16]{1,0:T(8,128)} %bitcast.2, f32[8,16]{1,0:T(8,128)} %bitcast.5, s32[4,1024]{1,0:T(4,128)} %zone_ref.5, f32[4,7,4,1024]{3,2,1,0:T(4,128)} %source_ref.3), custom_call_target="tpu_custom_call" | custom-call | tf_op jit(solution)/shard_map/first/pallas_call | solution.py:1122
  5.2 0.0 copy-start
  5.2 7.3 %all-to-all-start = ((f32[32,64,128]{2,1,0:T(8,128)}), f32[32,64,128]{2,1,0:T(8,128)S(1)}, u32[]{:S(2)}, u32[]{:S(2)}) async-start(f32[32,64,128]{2,1,0:T(8,128)} %get-tuple-element.9), calls=%async_computation | async-start | bytes 2097152 | tf_op jit(solution)/shard_map/all_to_all | solution.py:1123
  12.6 0.0 copy-done
  12.6 0.0 copy-start.1
  12.6 0.2 fusion
  12.8 0.0 copy-start.4
  12.8 0.0 copy-start.5
  12.8 2.2 %collective-permute-start = (f32[4,7,2,1024]{3,2,1,0:T(2,128)S(1)}, f32[4,7,2,1024]{3,2,1,0:T(2,128)S(1)}, u32[]{:S(2)}, u32[]{:S(2)}) collective-permute-start(f32[4,7,2,1024]{3,2,1,0:T(2,128)S(1)} %get-tuple-element.17), channel_id=1, source_target_pairs={{0,1},{1,2},{2,3},{4,5},{5,6},{6,7},{8,9},{9,10},{10,11},{12,13},{... | collective-permute-start | bytes 688136 | tf_op jit(solution)/shard_map/ppermute | solution.py:1129
  15.0 0.0 copy-start.2
  15.0 0.0 copy-start.3
  15.0 1.3 %collective-permute-start.1 = (f32[4,7,2,1024]{3,2,1,0:T(2,128)S(1)}, f32[4,7,2,1024]{3,2,1,0:T(2,128)S(1)}, u32[]{:S(2)}, u32[]{:S(2)}) collective-permute-start(f32[4,7,2,1024]{3,2,1,0:T(2,128)S(1)} %get-tuple-element.16), channel_id=1, source_target_pairs={{1,0},{2,1},{3,2},{5,4},{6,5},{7,6},{9,8},{10,9},{11,10},{13,12},{... | collective-permute-start | bytes 688136 | tf_op jit(solution)/shard_map/ppermute | solution.py:1130
  16.3 0.0 copy-done.1
  16.3 0.0 copy-done.4
  16.3 0.0 copy-done.5
  16.3 0.2 label.1.refs_0_
  16.5 1.7 %collective-permute-start.2 = (f32[8,128]{1,0:T(8,128)S(1)}, f32[8,128]{1,0:T(8,128)S(1)}, u32[]{:S(2)}, u32[]{:S(2)}) collective-permute-start(f32[8,128]{1,0:T(8,128)S(1)} %label.1.refs_0_), channel_id=1, source_target_pairs={{0,4},{4,0},{8,12},{12,8},{16,20},{20,16},{24,28},{28,24},{1,5},{5... | collective-permute-start | bytes 12296 | tf_op jit(solution)/shard_map/ppermute | solution.py:1128
  18.2 1.5 %collective-permute-start.3 = (f32[8,128]{1,0:T(8,128)S(1)}, f32[8,128]{1,0:T(8,128)S(1)}, u32[]{:S(2)}, u32[]{:S(2)}) collective-permute-start(f32[8,128]{1,0:T(8,128)S(1)} %label.1.refs_0_), channel_id=1, source_target_pairs={{0,8},{4,12},{8,0},{12,4},{16,24},{20,28},{24,16},{28,20},{1,9},{5... | collective-permute-start | bytes 12296 | tf_op jit(solution)/shard_map/ppermute | solution.py:1128
  19.7 0.4 collective-permute-start.4
  20.1 0.1 collective-permute-done.2.refs_1_
  20.2 2.5 %collective-permute-start.5 = (f32[8,128]{1,0:T(8,128)S(1)}, f32[8,128]{1,0:T(8,128)S(1)}, u32[]{:S(2)}, u32[]{:S(2)}) collective-permute-start(f32[8,128]{1,0:T(8,128)S(1)} %label.1.refs_0_), channel_id=1, source_target_pairs={{0,16},{4,20},{8,24},{12,28},{16,0},{20,4},{24,8},{28,12},{1,17},{... | collective-permute-start | bytes 12296 | tf_op jit(solution)/shard_map/ppermute | solution.py:1128
  22.7 7.7 %collective-permute-done.3.refs_2_ = f32[8,128]{1,0:T(8,128)S(1)} collective-permute-done((f32[8,128]{1,0:T(8,128)S(1)}, f32[8,128]{1,0:T(8,128)S(1)}, u32[]{:S(2)}, u32[]{:S(2)}) %collective-permute-start.3) | collective-permute-done | bytes 4128 | tf_op jit(solution)/shard_map/ppermute | solution.py:1128
  30.4 5.3 %collective-permute-start.6 = (f32[8,128]{1,0:T(8,128)S(1)}, f32[8,128]{1,0:T(8,128)S(1)}, u32[]{:S(2)}, u32[]{:S(2)}) collective-permute-start(f32[8,128]{1,0:T(8,128)S(1)} %label.1.refs_0_), channel_id=1, source_target_pairs={{0,20},{4,16},{8,28},{12,24},{16,4},{20,0},{24,12},{28,8},{1,21},{... | collective-permute-start | bytes 12296 | tf_op jit(solution)/shard_map/ppermute | solution.py:1128
  35.8 0.0 collective-permute-done.low_ref
  35.8 0.5 collective-permute-start.7
  36.3 0.0 collective-permute-done.1.high_ref
  36.3 3.3 %collective-permute-start.8 = (f32[8,128]{1,0:T(8,128)S(1)}, f32[8,128]{1,0:T(8,128)S(1)}, u32[]{:S(2)}, u32[]{:S(2)}) collective-permute-start(f32[8,128]{1,0:T(8,128)S(1)} %label.1.refs_0_), channel_id=1, source_target_pairs={{0,28},{4,24},{8,20},{12,16},{16,12},{20,8},{24,4},{28,0},{1,29},{... | collective-permute-start | bytes 12296 | tf_op jit(solution)/shard_map/ppermute | solution.py:1128
  39.6 0.0 copy-done.2
  39.6 0.0 copy-done.3
  39.6 3.6 %inner.1 = (f32[4,7,4,1024]{3,2,1,0:T(4,128)S(1)}, f32[4,4,1024]{2,1,0:T(4,128)S(1)}) custom-call(f32[7,16]{1,0:T(8,128)S(1)} %bitcast.3, f32[8,16]{1,0:T(8,128)S(1)} %bitcast.6, s32[4,1024]{1,0:T(4,128)S(1)} %copy-done.1, f32[4,7,4,1024]{3,2,1,0:T(4,128)S(1)} %copy-done, f32[4,7,2,1024]{3,2,1,0:T(2,128)S(1)} %collective-permute-done.low_ref, ...), custom_call_target="tpu_custom_call" | custom-call | tf_op jit(solution)/shard_map/inner/pallas_call | solution.py:1131
  43.2 0.0 collective-permute-done.4.refs_3_
  43.2 0.0 collective-permute-done.5.refs_4_
  43.2 0.0 collective-permute-done.6.refs_5_
  43.2 0.0 collective-permute-done.7.refs_6_
  43.2 0.0 collective-permute-done.8.refs_7_
  43.2 2.4 %prepare.1 = (bf16[256,256]{1,0:T(8,128)(2,1)S(1)}, f32[2,256,128]{2,1,0:T(8,128)S(1)}, f32[7,64,128]{2,1,0:T(8,128)S(1)}) custom-call(f32[7,16]{1,0:T(8,128)S(1)} %bitcast.4, f32[8,16]{1,0:T(8,128)S(1)} %bitcast.7, f32[8,128]{1,0:T(8,128)S(1)} %label.1.refs_0_, f32[8,128]{1,0:T(8,128)S(1)} %collective-permute-done.2.refs_1_, ...), custom_call_target="tpu_custom_call" | custom-call | tf_op jit(solution)/shard_map/prepare/pallas_call | solution.py:1132
  45.6 0.0 all-to-all-done.recv_ref
  45.6 11.8 %solve.1 = (f32[4,7,4,1024]{3,2,1,0:T(4,128)}, f32[4,4,1024]{2,1,0:T(4,128)}) custom-call(f32[32,64,128]{2,1,0:T(8,128)S(1)} %all-to-all-done.recv_ref, f32[31,8,128]{2,1,0:T(8,128)S(1)} %get-tuple-element.10.coef_ref, f32[4,7,4,1024]{3,2,1,0:T(4,128)S(1)} %get-tuple-element.11.edge_in, f32[4,4,1024]{2,1,0:T(4,128)S(1)} %get-tuple-element.12.refs_8_.pot_in, ...), custom_call_target="tpu_custom_call" | custom-call | tf_op jit(solution)/shard_map/solve/pallas_call | solution.py:1133
Async XLA Ops:
  5.2 7.3 %copy-start = (f32[4,7,4,1024]{3,2,1,0:T(4,128)S(1)}, f32[4,7,4,1024]{3,2,1,0:T(4,128)}, u32[]{:S(2)}) copy-start(f32[4,7,4,1024]{3,2,1,0:T(4,128)} %source_ref.3) | copy-start | bytes 1376260
  5.2 40.3 %all-to-all-start = ((f32[32,64,128]{2,1,0:T(8,128)}), f32[32,64,128]{2,1,0:T(8,128)S(1)}, u32[]{:S(2)}, u32[]{:S(2)}) async-start(f32[32,64,128]{2,1,0:T(8,128)} %get-tuple-element.9), calls=%async_computation | async-start | bytes 2097152 | tf_op jit(solution)/shard_map/all_to_all | solution.py:1123
  12.6 3.7 %copy-start.1 = (s32[4,1024]{1,0:T(4,128)S(1)}, s32[4,1024]{1,0:T(4,128)}, u32[]{:S(2)}) copy-start(s32[4,1024]{1,0:T(4,128)} %zone_ref.5) | copy-start | bytes 49156
  12.8 3.5 %copy-start.4 = (s32[1,32]{1,0:T(1,128)S(1)}, s32[1,32]{1,0:T(1,128)}, u32[]{:S(2)}) copy-start(s32[1,32]{1,0:T(1,128)} %owner_ref.1) | copy-start | bytes 388
  12.8 3.5 %copy-start.5 = (s32[1,32]{1,0:T(1,128)S(1)}, s32[1,32]{1,0:T(1,128)}, u32[]{:S(2)}) copy-start(s32[1,32]{1,0:T(1,128)} %group_ref.1) | copy-start | bytes 388
  12.8 23.0 %collective-permute-start = (f32[4,7,2,1024]{3,2,1,0:T(2,128)S(1)}, f32[4,7,2,1024]{3,2,1,0:T(2,128)S(1)}, u32[]{:S(2)}, u32[]{:S(2)}) collective-permute-start(f32[4,7,2,1024]{3,2,1,0:T(2,128)S(1)} %get-tuple-element.17), channel_id=1, source_target_pairs={{0,1},{1,2},{2,3},{4,5},{5,6},{6,7},{8,9},{9,10},{10,11},{12,13},{... | collective-permute-start | bytes 688136 | tf_op jit(solution)/shard_map/ppermute | solution.py:1129
  15.0 24.6 %copy-start.2 = (f32[16,7]{0,1:T(8,128)S(1)}, f32[16,7]{0,1:T(8,128)}, u32[]{:S(2)}) copy-start(f32[16,7]{0,1:T(8,128)} %param.8) | copy-start | bytes 1348
  15.0 24.6 %copy-start.3 = (f32[16,8]{0,1:T(8,128)S(1)}, f32[16,8]{0,1:T(8,128)}, u32[]{:S(2)}) copy-start(f32[16,8]{0,1:T(8,128)} %param.9) | copy-start | bytes 1540
  15.0 21.3 %collective-permute-start.1 = (f32[4,7,2,1024]{3,2,1,0:T(2,128)S(1)}, f32[4,7,2,1024]{3,2,1,0:T(2,128)S(1)}, u32[]{:S(2)}, u32[]{:S(2)}) collective-permute-start(f32[4,7,2,1024]{3,2,1,0:T(2,128)S(1)} %get-tuple-element.16), channel_id=1, source_target_pairs={{1,0},{2,1},{3,2},{5,4},{6,5},{7,6},{9,8},{10,9},{11,10},{13,12},{... | collective-permute-start | bytes 688136 | tf_op jit(solution)/shard_map/ppermute | solution.py:1130
  16.5 3.7 %collective-permute-start.2 = (f32[8,128]{1,0:T(8,128)S(1)}, f32[8,128]{1,0:T(8,128)S(1)}, u32[]{:S(2)}, u32[]{:S(2)}) collective-permute-start(f32[8,128]{1,0:T(8,128)S(1)} %label.1.refs_0_), channel_id=1, source_target_pairs={{0,4},{4,0},{8,12},{12,8},{16,20},{20,16},{24,28},{28,24},{1,5},{5... | collective-permute-start | bytes 12296 | tf_op jit(solution)/shard_map/ppermute | solution.py:1128
  18.2 12.2 %collective-permute-start.3 = (f32[8,128]{1,0:T(8,128)S(1)}, f32[8,128]{1,0:T(8,128)S(1)}, u32[]{:S(2)}, u32[]{:S(2)}) collective-permute-start(f32[8,128]{1,0:T(8,128)S(1)} %label.1.refs_0_), channel_id=1, source_target_pairs={{0,8},{4,12},{8,0},{12,4},{16,24},{20,28},{24,16},{28,20},{1,9},{5... | collective-permute-start | bytes 12296 | tf_op jit(solution)/shard_map/ppermute | solution.py:1128
  19.7 23.5 %collective-permute-start.4 = (f32[8,128]{1,0:T(8,128)S(1)}, f32[8,128]{1,0:T(8,128)S(1)}, u32[]{:S(2)}, u32[]{:S(2)}) collective-permute-start(f32[8,128]{1,0:T(8,128)S(1)} %label.1.refs_0_), channel_id=1, source_target_pairs={{0,12},{4,8},{8,4},{12,0},{16,28},{20,24},{24,20},{28,16},{1,13},{... | collective-permute-start | bytes 12296 | tf_op jit(solution)/shard_map/ppermute | solution.py:1128
  20.2 23.0 %collective-permute-start.5 = (f32[8,128]{1,0:T(8,128)S(1)}, f32[8,128]{1,0:T(8,128)S(1)}, u32[]{:S(2)}, u32[]{:S(2)}) collective-permute-start(f32[8,128]{1,0:T(8,128)S(1)} %label.1.refs_0_), channel_id=1, source_target_pairs={{0,16},{4,20},{8,24},{12,28},{16,0},{20,4},{24,8},{28,12},{1,17},{... | collective-permute-start | bytes 12296 | tf_op jit(solution)/shard_map/ppermute | solution.py:1128
  30.4 12.7 %collective-permute-start.6 = (f32[8,128]{1,0:T(8,128)S(1)}, f32[8,128]{1,0:T(8,128)S(1)}, u32[]{:S(2)}, u32[]{:S(2)}) collective-permute-start(f32[8,128]{1,0:T(8,128)S(1)} %label.1.refs_0_), channel_id=1, source_target_pairs={{0,20},{4,16},{8,28},{12,24},{16,4},{20,0},{24,12},{28,8},{1,21},{... | collective-permute-start | bytes 12296 | tf_op jit(solution)/shard_map/ppermute | solution.py:1128
  35.8 7.4 %collective-permute-start.7 = (f32[8,128]{1,0:T(8,128)S(1)}, f32[8,128]{1,0:T(8,128)S(1)}, u32[]{:S(2)}, u32[]{:S(2)}) collective-permute-start(f32[8,128]{1,0:T(8,128)S(1)} %label.1.refs_0_), channel_id=1, source_target_pairs={{0,24},{4,28},{8,16},{12,20},{16,8},{20,12},{24,0},{28,4},{1,25},{... | collective-permute-start | bytes 12296 | tf_op jit(solution)/shard_map/ppermute | solution.py:1128
  36.3 6.9 %collective-permute-start.8 = (f32[8,128]{1,0:T(8,128)S(1)}, f32[8,128]{1,0:T(8,128)S(1)}, u32[]{:S(2)}, u32[]{:S(2)}) collective-permute-start(f32[8,128]{1,0:T(8,128)S(1)} %label.1.refs_0_), channel_id=1, source_target_pairs={{0,28},{4,24},{8,20},{12,16},{16,12},{20,8},{24,4},{28,0},{1,29},{... | collective-permute-start | bytes 12296 | tf_op jit(solution)/shard_map/ppermute | solution.py:1128

commit v3 on v2

--- a/solution.py
+++ b/solution.py
@@ -452,7 +452,7 @@
     sides = 2 * macros
     blocks = 2 * planes
 
-    def body(kappa_ref, mu_ref, zone_ref, source_ref, pay_ref, coef_ref, hold_ref):
+    def body(kappa_ref, mu_ref, zone_ref, source_ref, pay_ref, coef_ref, hold_ref, sems):
         k = lax.axis_index("sub")
         shape = (sides, LANES)
         sh = Strip(shape)
@@ -547,9 +547,14 @@
             hold_ref[p * sides : (p + 1) * sides, :] = merge(src[p][1], src[p][2], src[p][5], n1[p])
             at = planes + p
             hold_ref[at * sides : (at + 1) * sides, :] = merge(res[p][1], res[p][2], spare[p], n2[p])
-        block = hold_ref[...]
-        for dest in range(n_dom * n_sub):
-            pay_ref[dest] = block
+        copies = [
+            pltpu.make_async_copy(hold_ref, pay_ref.at[dest], sems.at[dest])
+            for dest in range(n_dom * n_sub)
+        ]
+        for copy in copies:
+            copy.start()
+        for copy in copies:
+            copy.wait()
 
     f32 = jnp.float32
     smem = pl.BlockSpec(memory_space=pltpu.SMEM)
@@ -560,10 +565,14 @@
         name="first",
         in_specs=[smem, smem, vmem, vmem],
         out_shape=(
-            pltpu.VMEM((n_dom * n_sub, blocks * sides, LANES), f32),
+            jax.ShapeDtypeStruct((n_dom * n_sub, blocks * sides, LANES), f32),
             pltpu.VMEM((31, sides, LANES), f32),
         ),
-        scratch_shapes=[pltpu.VMEM((blocks * sides, LANES), f32)],
+        out_specs=(pl.BlockSpec(memory_space=pltpu.HBM), vmem),
+        scratch_shapes=[
+            pltpu.VMEM((blocks * sides, LANES), f32),
+            pltpu.SemaphoreType.DMA((n_dom * n_sub,)),
+        ],
     )
 
 
@@ -771,16 +780,13 @@
         def near(v):
             return jnp.where(upper, lane_roll(v, -1), 0.0)
 
-        def place(*fields):
-            out = jnp.zeros(shape, jnp.float32)
-            for g, field in enumerate(fields):
-                if field is not None:
-                    out = jnp.where(group == g, lane_roll(field, g - 1), out)
-            return out
+        def everywhere(v):
+            out = jnp.where(group == 0, lane_roll(v, -1), v)
+            out = jnp.where(group == 2, lane_roll(v, 1), out)
+            return jnp.where(group == 3, lane_roll(v, 2), out)
 
         near_mu = [near(v) for v in mu]
         near_mass = [near(v) for v in mass]
-        edge_mass = place(mass[1], mass[2], mass[5])
         e1_low = mass[1] + mu[1] + mu[4] + near_mu[0]
         e2_diag = mass[2] + mu[3] + mu[5] + mu[7] + near_mu[2] + yb(mu[4]) + yb(near_mu[6])
         e5_diag = mass[5] + mu[4] + mu[5]
@@ -788,8 +794,6 @@
         for t in range(7):
             node_low = node_low + mass[t]
         node_diag = node_low + mass[2] + near_mass[4] + yb(mass[5]) + yb(near_mass[6])
-        self_coef = place(mu[1] + near_mu[0], mu[3] + mu[7] + near_mu[2] + yb(near_mu[6]))
-        cross_coef = place(mu[4], mu[5])
 
         def loose_terms(low):
             diag = {
@@ -812,24 +816,42 @@
             p3 = -(be[0] + be[3] + be[4] + be[6]) - be_n[0] - yb(be_n[3])
             if not low:
                 p3 = p3 - be_n[4] - yb(be_n[6])
-            return place(p0, p1, None, p3), place(r0, r1)
-
-        terms = (loose_terms(True), loose_terms(False))
-        low_diag = place(e1_low, e2_diag, e5_diag, node_low)
-        high_diag = place(e1_low + mu[5], e2_diag, e5_diag, node_diag)
-
-        blocks = [
-            jnp.concatenate([low_diag] + [high_diag] * (planes - 1), axis=0),
-            jnp.concatenate([high_diag] * planes, axis=0),
-        ]
+            return p0, r0, p1, p3, r1
+
+        low_terms, high_terms = loose_terms(True), loose_terms(False)
+
+        def lowest(low, high):
+            return jnp.where(group == 0, everywhere(low), everywhere(high))
+
+        blocks = []
+        for low, high in (
+            (e1_low, e1_low + mu[5]),
+            (e2_diag, e2_diag),
+            (e5_diag, e5_diag),
+            (node_low, node_diag),
+        ):
+            high_all = everywhere(high)
+            low_all = high_all if low is high else jnp.where(group == 0, everywhere(low), high_all)
+            blocks.append(jnp.concatenate([low_all] + [high_all] * (planes - 1), axis=0))
         same_ref[...] = same
         summed = group_sum(same, jnp.concatenate(blocks, axis=1))
-        damp = jnp.where((iota((total, LANES), 1) & 3) == 3, NODE_DAMPING, EDGE_DAMPING)
-        for i in range(2):
+        for i in range(4):
+            damp = EDGE_DAMPING if i < 3 else NODE_DAMPING
             weight_ref[i] = damp / summed[:, LANES * i : LANES * (i + 1)]
-        out = (edge_mass, self_coef, cross_coef) + terms[0] + terms[1]
+        out = [
+            mass[1],
+            mass[2],
+            mass[5],
+            mu[1] + near_mu[0],
+            mu[3] + mu[7] + near_mu[2] + yb(near_mu[6]),
+            mu[4],
+            mu[5],
+        ]
+        out += list(high_terms)
         for i, v in enumerate(out):
-            field_ref[i] = v
+            field_ref[i] = everywhere(v)
+        for i in range(4):
+            field_ref[12 + i] = lowest(low_terms[i], high_terms[i])
 
     f32 = jnp.float32
     smem = pl.BlockSpec(memory_space=pltpu.SMEM)
@@ -841,8 +863,8 @@
         in_specs=[smem, smem] + [vmem] * (n_dom + 1),
         out_shape=(
             pltpu.VMEM((total, total), jnp.bfloat16),
-            pltpu.VMEM((2, total, LANES), f32),
-            pltpu.VMEM((7, n, LANES), f32),
+            pltpu.VMEM((4, total, LANES), f32),
+            pltpu.VMEM((16, n, LANES), f32),
         ),
         scratch_shapes=[pltpu.VMEM((n_dom, sides, LANES), f32)],
     )
@@ -851,14 +873,12 @@
 def solve_kernel(n_dom, n_sub, macros, planes, cells):
     sides = 2 * macros
     n = n_dom * sides
-    depth = n_sub * planes
 
     def body(recv_ref, coef_ref, edge_in, pot_in, same_ref, weight_ref, field_ref, edge_ref, pot_ref, one_ref, two_ref, turn_ref):
         k = lax.axis_index("sub")
         d = lax.axis_index("dom")
         shape = (n, LANES)
         group = iota(shape, 1) & 3
-        edges = group < 3
         upper = (iota(shape, 0) % sides) >= macros
 
         def rows_of(layer, at):
@@ -868,140 +888,106 @@
             return jnp.concatenate(parts, axis=0)
 
         same = same_ref[...]
-        blocks = [
-            jnp.concatenate([rows_of(layer, p) for p in range(planes)], axis=0)
-            for layer in range(n_sub)
-        ]
-        summed = group_sum(same, jnp.concatenate(blocks, axis=1))
-
-        def lanes(v, i):
-            return v[:, LANES * i : LANES * (i + 1)]
-
-        weight = [weight_ref[0], weight_ref[1]]
-        edge_mass, self_coef, cross_coef = (field_ref[i] for i in range(3))
-        terms = ((field_ref[3], field_ref[4]), (field_ref[5], field_ref[6]))
-
-        def fold(v):
-            return lane_roll(v, 3) + lane_roll(v, 2) + lane_roll(v, 1)
-
-        def fold_edges(r, r_below):
-            out = jnp.where(group == 0, yb(r), 0.0) - r
-            if r_below is not None:
-                out = out + jnp.where(group == 1, r_below, 0.0)
-                out = out + jnp.where(group == 2, yb(r_below), 0.0)
-            return out
-
-        def node_sums(nodes):
-            block = None
-            for layer in range(n_sub):
-                stacked = jnp.concatenate(nodes[layer], axis=0)
-                moved = lane_roll(stacked, layer - 3)
-                moved = jnp.where((iota(moved.shape, 1) & 3) == layer, moved, 0.0)
-                block = moved if block is None else block + moved
-            out = group_sum(same, block)
-            return [lane_roll(out, 3 - layer) for layer in range(n_sub)]
+        edge_mass = [field_ref[i] for i in range(3)]
 
         def of(v, p):
             return v[p * n : (p + 1) * n]
 
-        e1, r1 = {}, {}
-        nodes = [[None] * planes for _ in range(n_sub)]
-        for layer in range(n_sub):
-            value = lanes(summed, layer) * weight[min(layer, 1)]
-            for p in range(planes):
-                at = layer * planes + p
-                src = of(blocks[layer], p)
-                e1[at] = jnp.where(edges, of(value, p), 0.0)
-                r1[at] = jnp.where(edges, src - edge_mass * e1[at], 0.0)
-                node = src + fold(fold_edges(r1[at], r1.get(at - 1)))
-                if p == 0 and layer > 0:
-                    shifted = lane_roll(rows_of(layer - 1, planes + 1), 1)
-                    node = node + jnp.where(upper, shifted, 0.0)
-                nodes[layer][p] = node
-        node_sum = node_sums(nodes)
-        c1 = {}
-        for at in range(depth):
-            layer, p = at // planes, at % planes
-            value = of(node_sum[layer], p) * of(weight[min(layer, 1)], p)
-            c1[at] = jnp.where(group == 3, value, 0.0)
-            one_ref[HALO + at] = e1[at] + c1[at]
-
-        cross = {}
-        base = {}
-        for at in range(depth):
-            e = e1[at]
-            first = lane_roll(ya(e), -1) - lane_roll(e, -2)
-            second = -lane_roll(e, -1)
-            if at + 1 in e1:
-                second = second + lane_roll(e1[at + 1], 1)
-            cross[at] = jnp.where(
-                group < 2, cross_coef * (e + jnp.where(group == 0, first, second)), 0.0
+        def weight(i, p):
+            return weight_ref[i, p * n : (p + 1) * n, :]
+
+        def by_layer(at):
+            r = [rows_of(layer, at) for layer in range(4)]
+            even = (group & 1) == 0
+            halves = []
+            for i in (0, 2):
+                halves.append(jnp.where(even, r[i], lane_roll(r[i + 1], 1)))
+                halves.append(jnp.where(even, lane_roll(r[i], -1), r[i + 1]))
+            low = group < 2
+            out = [jnp.where(low, halves[i], lane_roll(halves[i + 2], 2)) for i in (0, 1)]
+            return out + [jnp.where(low, lane_roll(halves[i], -2), halves[i + 2]) for i in (0, 1)]
+
+        def from_below(v):
+            return jnp.where(group > 0, lane_roll(v, 1), 0.0)
+
+        def from_above(v):
+            return jnp.where(group < 3, lane_roll(v, -1), 0.0)
+
+        def below(f, p):
+            return f[p - 1] if p > 0 else from_below(f[planes - 1])
+
+        def above(f, p):
+            return f[p + 1] if p < planes - 1 else from_above(f[0])
+
+        def summed(fields):
+            block = jnp.concatenate([jnp.concatenate(f, axis=0) for f in fields], axis=1)
+            out = group_sum(same, block)
+            return [out[:, LANES * i : LANES * (i + 1)] for i in range(len(fields))]
+
+        span = range(planes)
+
+        def edge_terms(r):
+            by0 = [yb(r[0][p]) for p in span]
+            by2 = [yb(r[2][p]) for p in span]
+            out = []
+            for p in span:
+                value = by0[p] - r[0][p] - r[1][p] - r[2][p]
+                out.append(value + below(r[1], p) + below(by2, p))
+            return out
+
+        given = [by_layer(p) for p in span]
+        more = [by_layer(planes + p) for p in span]
+        src = [[given[p][i] for p in span] for i in range(3)]
+        sums = summed(src)
+        e1 = [[of(sums[i], p) * weight(i, p) for p in span] for i in range(3)]
+        r1 = [[src[i][p] - edge_mass[i] * e1[i][p] for p in span] for i in range(3)]
+        nodes = [given[p][3] + v for p, v in enumerate(edge_terms(r1))]
+        nodes[0] = nodes[0] + jnp.where(upper, from_below(more[1][2]), 0.0)
+        (sums,) = summed([nodes])
+        c1 = [of(sums, p) * weight(3, p) for p in span]
+        for p in span:
+            one_ref[0, p], one_ref[1, p], one_ref[2, p] = e1[0][p], e1[1][p], c1[p]
+
+        w4 = [field_ref[5] * (e1[0][p] + ya(e1[1][p]) - e1[2][p]) for p in span]
+        w5 = [field_ref[6] * (e1[1][p] + above(e1[0], p) - e1[2][p]) for p in span]
+        ahead = [ya(c1[p]) for p in span]
+        base, res = [[], [], []], [[], [], []]
+        for p in span:
+            curled = (
+                field_ref[3] * e1[0][p] + w4[p] + below(w5, p),
+                field_ref[4] * e1[1][p] + w5[p] + yb(w4[p]),
+                -w4[p] - w5[p],
             )
-        second_blocks = []
-        for layer in range(n_sub):
-            stacked = []
-            for p in range(planes):
-                at = layer * planes + p
-                v = cross[at]
-                own0 = v if at == 0 else v + lane_roll(cross[at - 1], -1)
-                own1 = v + lane_roll(yb(v), 1)
-                own2 = -(lane_roll(v, 2) + lane_roll(v, 1))
-                coupled = jnp.where(group == 0, own0, jnp.where(group == 1, own1, own2))
-                c = c1[at]
-                ahead = ya(c)
-                rise0 = lane_roll(ahead - c, -3)
-                if at + 1 in c1:
-                    up = c1[at + 1]
-                    rise1 = lane_roll(up - c, -2)
-                    rise2 = lane_roll(ya(up) - c, -1)
-                else:
-                    rise1, rise2 = lane_roll(-c, -2), lane_roll(-c, -1)
-                rise = jnp.where(group == 0, rise0, jnp.where(group == 1, rise1, rise2))
-                rise = jnp.where(edges, rise, 0.0)
-                base[at] = e1[at] + rise
-                given = jnp.where(group < 2, rows_of(layer, planes + p), 0.0)
-                if p == planes - 1 and layer + 1 < n_sub:
-                    extra = lane_roll(rows_of(layer + 1, planes), -1)
-                    given = given + jnp.where(group == 1, extra, 0.0)
-                res = r1[at] + given - self_coef * e1[at] - coupled - edge_mass * rise
-                stacked.append(jnp.where(edges, res, 0.0))
-            second_blocks.append(jnp.concatenate(stacked, axis=0))
-        summed = group_sum(same, jnp.concatenate(second_blocks, axis=1))
-        e2, r2 = {}, {}
-        for layer in range(n_sub):
-            value = lanes(summed, layer) * weight[min(layer, 1)]
-            for p in range(planes):
-                at = layer * planes + p
-                e2[at] = jnp.where(edges, base[at] + of(value, p), 0.0)
-                src = of(blocks[layer], p)
-                r2[at] = jnp.where(edges, src - edge_mass * e2[at], 0.0)
-                by_p, by_r = terms[min(at, 1)]
-                e = e1[at]
-                behind = yb(e)
-                if at > 0:
-                    behind = jnp.where(group == 1, e1[at - 1], behind)
-                    reach = jnp.where(group < 2, by_r * behind, 0.0)
-                else:
-                    reach = jnp.where(group == 0, by_r * behind, 0.0)
-                inner = fold_edges(r2[at], r2.get(at - 1)) + jnp.where(group < 2, by_p * e, 0.0)
-                node = rows_of(layer, planes + p) + fold(inner + reach) + by_p * c1[at]
-                if p == 0 and layer > 0:
-                    node = node + lane_roll(rows_of(layer - 1, 2 * planes - 1), 1)
-                if p == 1 and layer > 0:
-                    shifted = row_roll(lane_roll(rows_of(layer - 1, planes + 1), 1), macros)
-                    node = node + jnp.where(upper, shifted, 0.0)
-                if p == planes - 1 and layer + 1 < n_sub:
-                    node = node + lane_roll(rows_of(layer + 1, planes + 2), 1)
-                nodes[layer][p] = node
-        node_sum = node_sums(nodes)
-        for at in range(depth):
-            layer, p = at // planes, at % planes
-            value = of(node_sum[layer], p) * of(weight[min(layer, 1)], p)
-            two_ref[HALO + at] = jnp.where(group == 3, value, e2[at])
-        for ref in (one_ref, two_ref):
-            for i in range(HALO):
-                ref[i] = jnp.zeros(shape, jnp.float32)
-                ref[HALO + depth + i] = jnp.zeros(shape, jnp.float32)
+            grad = (ahead[p] - c1[p], above(c1, p) - c1[p], above(ahead, p) - c1[p])
+            for i in range(3):
+                value = r1[i][p] - curled[i] - edge_mass[i] * grad[i]
+                if i < 2:
+                    value = value + more[p][i]
+                if i == 1 and p == planes - 1:
+                    value = value + from_above(more[0][2])
+                res[i].append(value)
+                base[i].append(e1[i][p] + grad[i])
+        sums = summed(res)
+        e2 = [[base[i][p] + of(sums[i], p) * weight(i, p) for p in span] for i in range(3)]
+        r2 = [[src[i][p] - edge_mass[i] * e2[i][p] for p in span] for i in range(3)]
+        nodes = []
+        for p, value in enumerate(edge_terms(r2)):
+            p0, r0, p1, p3 = (field_ref[(12 if p == 0 else 7) + i] for i in range(4))
+            value = value + more[p][3] + p0 * e1[0][p] + r0 * yb(e1[0][p]) + p1 * e1[1][p]
+            value = value + field_ref[11] * below(e1[1], p) + p3 * c1[p]
+            if p == 0:
+                value = value + from_below(more[planes - 1][2])
+            if p == 1:
+                moved = row_roll(more[1][2], macros)
+                value = value + jnp.where(upper, from_below(moved), 0.0)
+            if p == planes - 1:
+                value = value + from_above(more[2][2])
+            nodes.append(value)
+        (sums,) = summed([nodes])
+        for p in span:
+            for i in range(3):
+                two_ref[i, p] = e2[i][p]
+            two_ref[3, p] = of(sums, p) * weight(3, p)
 
         strip = (sides, LANES)
         sh = Strip(strip)
@@ -1013,16 +999,21 @@
             return v if flag is None or v is None else v * flag
 
         mine = pl.ds(pl.multiple_of(d * sides, sides), sides)
-
-        def taken(ref, p, g):
-            value = ref[k * planes + p + HALO, mine, :]
-            return jnp.where(sh.own, lane_roll(value, -g), 0.0)
+        turned = {}
+
+        def taken(ref, p, i):
+            step, plane = p // planes, p % planes
+            key = (ref is two_ref, i, plane)
+            if key not in turned:
+                turned[key] = pltpu.roll(ref[i, plane, mine, :], (LANES - k) & (LANES - 1), 1)
+            value = jnp.where(sh.own, lane_roll(turned[key], -step), 0.0)
+            return value * (has_below if step < 0 else has_above) if step else value
 
         my_mass = [coef_ref[t] for t in range(7)]
         my_mu = [coef_ref[7 + f] for f in range(8)]
         loose_r = {}
         step_e = {}
-        c_one = {p: taken(one_ref, p, 3) for p in range(-1, planes + 2)}
+        c_one = {p: taken(one_ref, p, 2) for p in range(-1, planes + 2)}
         faces = {}
         for p in range(-1, planes + 1):
             ea, eb = taken(one_ref, p, 0), taken(one_ref, p, 1)
@@ -1099,8 +1090,8 @@
             jax.ShapeDtypeStruct((macros, planes, cells), f32),
         ),
         scratch_shapes=[
-            pltpu.VMEM((depth + 2 * HALO, n, LANES), f32),
-            pltpu.VMEM((depth + 2 * HALO, n, LANES), f32),
+            pltpu.VMEM((3, planes, n, LANES), f32),
+            pltpu.VMEM((4, planes, n, LANES), f32),
             pltpu.VMEM((8, sides, planes, LANES), f32),
         ],
     )

time: 57.7 us -> 50.5 us (0.88)
  Pallas kernels: 22.5 us -> 15.3 us
    pallas_call x1, Pallas kernels: 11.8 us -> 4.11 us  [local_small(): return solve_kernel(*sizes)(*near_core(recv, coef, edge, pot, *fields))]
  transfers between devices with their start and end apart: 10 -> 10, of which waited for: 2 -> 2; matrix products, arithmetic and copies ran while one was open for 0% -> 0% of each run, Pallas kernels for 11% -> 13%
where the time goes in v3:
time: 50.5 us; the launch traced here: 50.2 us
  starting transfers between devices  26 us (51%)
  Pallas kernels  15.3 us (30%)
  waiting for transfers between devices  7.86 us (16%)
  between operations  0.82 us (2%)
    ppermute x7, starting transfers between devices, local_small(): labels.append(lax.ppermute(labels[0], 'dom', route))  15.2 us
    ppermute x7, waiting for transfers between devices, local_small(): labels.append(lax.ppermute(labels[0], 'dom', route))  7.85 us
    all_to_all x1, starting transfers between devices, local_small(): recv = lax.all_to_all(pay, ('dom', 'sub'), 0, 0)  7.33 us
    pallas_call x1, Pallas kernels, local_small(): pay, coef = first_kernel(*sizes)(*far)  4.75 us
    pallas_call x1, Pallas kernels, local_small(): return solve_kernel(*sizes)(*near_core(recv, coef, edge, pot, *fields))  4.11 us
    pallas_call x1, Pallas kernels, local_small(): inner_kernel(*sizes)(*tables, zone_ids, source, *near_core(low, high))  3.56 us
    pallas_call x1, Pallas kernels, local_small(): fields = prepare_kernel(*sizes, *lists)(*tables, *near_core(*labels, pot))  2.72 us
    ppermute x1, starting transfers between devices, local_small(): low = lax.ppermute(source[:, :, planes - HALO:], 'sub', up)  2.17 us
  transfers between devices with their start and end apart: 10, of which 2 were waited for; matrix products, arithmetic and copies ran while one was open for 0% of the time, Pallas kernels for 13%

profile of v3, /device:TPU:0, one launch (start us, length us, event | category | flops | bytes accessed | tf_op | source)
XLA Modules:
  0.0 50.2 jit_solution(15357815969461915836)
XLA Ops:
  0.6 4.8 %first.1 = (f32[32,64,128]{2,1,0:T(8,128)}, f32[31,8,128]{2,1,0:T(8,128)S(1)}) custom-call(f32[7,16]{1,0:T(8,128)} %bitcast.2, f32[8,16]{1,0:T(8,128)} %bitcast.5, s32[4,1024]{1,0:T(4,128)} %zone_ref.5, f32[4,7,4,1024]{3,2,1,0:T(4,128)} %source_ref.3), custom_call_target="tpu_custom_call" | custom-call | tf_op jit(solution)/shard_map/first/pallas_call | solution.py:1113
  5.4 0.0 copy-start
  5.4 7.3 %all-to-all-start = ((f32[32,64,128]{2,1,0:T(8,128)}), f32[32,64,128]{2,1,0:T(8,128)S(1)}, u32[]{:S(2)}, u32[]{:S(2)}) async-start(f32[32,64,128]{2,1,0:T(8,128)} %get-tuple-element.9), calls=%async_computation | async-start | bytes 2097152 | tf_op jit(solution)/shard_map/all_to_all | solution.py:1114
  12.7 0.0 copy-done
  12.7 0.0 copy-start.1
  12.8 0.2 fusion
  12.9 0.0 copy-start.4
  13.0 0.0 copy-start.5
  13.0 2.2 %collective-permute-start = (f32[4,7,2,1024]{3,2,1,0:T(2,128)S(1)}, f32[4,7,2,1024]{3,2,1,0:T(2,128)S(1)}, u32[]{:S(2)}, u32[]{:S(2)}) collective-permute-start(f32[4,7,2,1024]{3,2,1,0:T(2,128)S(1)} %get-tuple-element.17), channel_id=1, source_target_pairs={{0,1},{1,2},{2,3},{4,5},{5,6},{6,7},{8,9},{9,10},{10,11},{12,13},{... | collective-permute-start | bytes 688136 | tf_op jit(solution)/shard_map/ppermute | solution.py:1120
  15.1 0.0 copy-start.2
  15.2 0.0 copy-start.3
  15.2 1.3 %collective-permute-start.1 = (f32[4,7,2,1024]{3,2,1,0:T(2,128)S(1)}, f32[4,7,2,1024]{3,2,1,0:T(2,128)S(1)}, u32[]{:S(2)}, u32[]{:S(2)}) collective-permute-start(f32[4,7,2,1024]{3,2,1,0:T(2,128)S(1)} %get-tuple-element.16), channel_id=1, source_target_pairs={{1,0},{2,1},{3,2},{5,4},{6,5},{7,6},{9,8},{10,9},{11,10},{13,12},{... | collective-permute-start | bytes 688136 | tf_op jit(solution)/shard_map/ppermute | solution.py:1121
  16.5 0.0 copy-done.1
  16.5 0.0 copy-done.4
  16.5 0.0 copy-done.5
  16.5 0.2 label.1.refs_0_
  16.7 1.7 %collective-permute-start.2 = (f32[8,128]{1,0:T(8,128)S(1)}, f32[8,128]{1,0:T(8,128)S(1)}, u32[]{:S(2)}, u32[]{:S(2)}) collective-permute-start(f32[8,128]{1,0:T(8,128)S(1)} %label.1.refs_0_), channel_id=1, source_target_pairs={{0,4},{4,0},{8,12},{12,8},{16,20},{20,16},{24,28},{28,24},{1,5},{5... | collective-permute-start | bytes 12296 | tf_op jit(solution)/shard_map/ppermute | solution.py:1119
  18.4 1.5 %collective-permute-start.3 = (f32[8,128]{1,0:T(8,128)S(1)}, f32[8,128]{1,0:T(8,128)S(1)}, u32[]{:S(2)}, u32[]{:S(2)}) collective-permute-start(f32[8,128]{1,0:T(8,128)S(1)} %label.1.refs_0_), channel_id=1, source_target_pairs={{0,8},{4,12},{8,0},{12,4},{16,24},{20,28},{24,16},{28,20},{1,9},{5... | collective-permute-start | bytes 12296 | tf_op jit(solution)/shard_map/ppermute | solution.py:1119
  19.8 0.4 collective-permute-start.4
  20.2 0.1 collective-permute-done.2.refs_1_
  20.4 2.5 %collective-permute-start.5 = (f32[8,128]{1,0:T(8,128)S(1)}, f32[8,128]{1,0:T(8,128)S(1)}, u32[]{:S(2)}, u32[]{:S(2)}) collective-permute-start(f32[8,128]{1,0:T(8,128)S(1)} %label.1.refs_0_), channel_id=1, source_target_pairs={{0,16},{4,20},{8,24},{12,28},{16,0},{20,4},{24,8},{28,12},{1,17},{... | collective-permute-start | bytes 12296 | tf_op jit(solution)/shard_map/ppermute | solution.py:1119
  22.9 7.7 %collective-permute-done.3.refs_2_ = f32[8,128]{1,0:T(8,128)S(1)} collective-permute-done((f32[8,128]{1,0:T(8,128)S(1)}, f32[8,128]{1,0:T(8,128)S(1)}, u32[]{:S(2)}, u32[]{:S(2)}) %collective-permute-start.3) | collective-permute-done | bytes 4128 | tf_op jit(solution)/shard_map/ppermute | solution.py:1119
  30.6 5.3 %collective-permute-start.6 = (f32[8,128]{1,0:T(8,128)S(1)}, f32[8,128]{1,0:T(8,128)S(1)}, u32[]{:S(2)}, u32[]{:S(2)}) collective-permute-start(f32[8,128]{1,0:T(8,128)S(1)} %label.1.refs_0_), channel_id=1, source_target_pairs={{0,20},{4,16},{8,28},{12,24},{16,4},{20,0},{24,12},{28,8},{1,21},{... | collective-permute-start | bytes 12296 | tf_op jit(solution)/shard_map/ppermute | solution.py:1119
  36.0 0.0 collective-permute-done.low_ref
  36.0 0.5 collective-permute-start.7
  36.4 0.0 collective-permute-done.1.high_ref
  36.4 3.3 %collective-permute-start.8 = (f32[8,128]{1,0:T(8,128)S(1)}, f32[8,128]{1,0:T(8,128)S(1)}, u32[]{:S(2)}, u32[]{:S(2)}) collective-permute-start(f32[8,128]{1,0:T(8,128)S(1)} %label.1.refs_0_), channel_id=1, source_target_pairs={{0,28},{4,24},{8,20},{12,16},{16,12},{20,8},{24,4},{28,0},{1,29},{... | collective-permute-start | bytes 12296 | tf_op jit(solution)/shard_map/ppermute | solution.py:1119
  39.8 0.0 copy-done.2
  39.8 0.0 copy-done.3
  39.8 3.6 %inner.1 = (f32[4,7,4,1024]{3,2,1,0:T(4,128)S(1)}, f32[4,4,1024]{2,1,0:T(4,128)S(1)}) custom-call(f32[7,16]{1,0:T(8,128)S(1)} %bitcast.3, f32[8,16]{1,0:T(8,128)S(1)} %bitcast.6, s32[4,1024]{1,0:T(4,128)S(1)} %copy-done.1, f32[4,7,4,1024]{3,2,1,0:T(4,128)S(1)} %copy-done, f32[4,7,2,1024]{3,2,1,0:T(2,128)S(1)} %collective-permute-done.low_ref, ...), custom_call_target="tpu_custom_call" | custom-call | tf_op jit(solution)/shard_map/inner/pallas_call | solution.py:1122
  43.3 0.0 collective-permute-done.4.refs_3_
  43.3 0.0 collective-permute-done.5.refs_4_
  43.3 0.0 collective-permute-done.6.refs_5_
  43.4 0.0 collective-permute-done.7.refs_6_
  43.4 0.0 collective-permute-done.8.refs_7_
  43.4 2.7 %prepare.1 = (bf16[256,256]{1,0:T(8,128)(2,1)S(1)}, f32[4,256,128]{2,1,0:T(8,128)S(1)}, f32[16,64,128]{2,1,0:T(8,128)S(1)}) custom-call(f32[7,16]{1,0:T(8,128)S(1)} %bitcast.4, f32[8,16]{1,0:T(8,128)S(1)} %bitcast.7, f32[8,128]{1,0:T(8,128)S(1)} %label.1.refs_0_, f32[8,128]{1,0:T(8,128)S(1)} %collective-permute-done.2.refs_1_, ...), custom_call_target="tpu_custom_call" | custom-call | tf_op jit(solution)/shard_map/prepare/pallas_call | solution.py:1123
  46.1 0.0 all-to-all-done.recv_ref
  46.1 4.1 %solve.1 = (f32[4,7,4,1024]{3,2,1,0:T(4,128)}, f32[4,4,1024]{2,1,0:T(4,128)}) custom-call(f32[32,64,128]{2,1,0:T(8,128)S(1)} %all-to-all-done.recv_ref, f32[31,8,128]{2,1,0:T(8,128)S(1)} %get-tuple-element.10.coef_ref, f32[4,7,4,1024]{3,2,1,0:T(4,128)S(1)} %get-tuple-element.11.edge_in, f32[4,4,1024]{2,1,0:T(4,128)S(1)} %get-tuple-element.12.refs_8_.pot_in, ...), custom_call_target="tpu_custom_call" | custom-call | tf_op jit(solution)/shard_map/solve/pallas_call | solution.py:1124
Async XLA Ops:
  5.4 7.4 %copy-start = (f32[4,7,4,1024]{3,2,1,0:T(4,128)S(1)}, f32[4,7,4,1024]{3,2,1,0:T(4,128)}, u32[]{:S(2)}) copy-start(f32[4,7,4,1024]{3,2,1,0:T(4,128)} %source_ref.3) | copy-start | bytes 1376260
  5.4 40.7 %all-to-all-start = ((f32[32,64,128]{2,1,0:T(8,128)}), f32[32,64,128]{2,1,0:T(8,128)S(1)}, u32[]{:S(2)}, u32[]{:S(2)}) async-start(f32[32,64,128]{2,1,0:T(8,128)} %get-tuple-element.9), calls=%async_computation | async-start | bytes 2097152 | tf_op jit(solution)/shard_map/all_to_all | solution.py:1114
  12.7 3.7 %copy-start.1 = (s32[4,1024]{1,0:T(4,128)S(1)}, s32[4,1024]{1,0:T(4,128)}, u32[]{:S(2)}) copy-start(s32[4,1024]{1,0:T(4,128)} %zone_ref.5) | copy-start | bytes 49156
  12.9 3.5 %copy-start.4 = (s32[1,32]{1,0:T(1,128)S(1)}, s32[1,32]{1,0:T(1,128)}, u32[]{:S(2)}) copy-start(s32[1,32]{1,0:T(1,128)} %owner_ref.1) | copy-start | bytes 388
  13.0 3.5 %copy-start.5 = (s32[1,32]{1,0:T(1,128)S(1)}, s32[1,32]{1,0:T(1,128)}, u32[]{:S(2)}) copy-start(s32[1,32]{1,0:T(1,128)} %group_ref.1) | copy-start | bytes 388
  13.0 23.0 %collective-permute-start = (f32[4,7,2,1024]{3,2,1,0:T(2,128)S(1)}, f32[4,7,2,1024]{3,2,1,0:T(2,128)S(1)}, u32[]{:S(2)}, u32[]{:S(2)}) collective-permute-start(f32[4,7,2,1024]{3,2,1,0:T(2,128)S(1)} %get-tuple-element.17), channel_id=1, source_target_pairs={{0,1},{1,2},{2,3},{4,5},{5,6},{6,7},{8,9},{9,10},{10,11},{12,13},{... | collective-permute-start | bytes 688136 | tf_op jit(solution)/shard_map/ppermute | solution.py:1120
  15.1 24.6 %copy-start.2 = (f32[16,7]{0,1:T(8,128)S(1)}, f32[16,7]{0,1:T(8,128)}, u32[]{:S(2)}) copy-start(f32[16,7]{0,1:T(8,128)} %param.8) | copy-start | bytes 1348
  15.2 24.6 %copy-start.3 = (f32[16,8]{0,1:T(8,128)S(1)}, f32[16,8]{0,1:T(8,128)}, u32[]{:S(2)}) copy-start(f32[16,8]{0,1:T(8,128)} %param.9) | copy-start | bytes 1540
  15.2 21.3 %collective-permute-start.1 = (f32[4,7,2,1024]{3,2,1,0:T(2,128)S(1)}, f32[4,7,2,1024]{3,2,1,0:T(2,128)S(1)}, u32[]{:S(2)}, u32[]{:S(2)}) collective-permute-start(f32[4,7,2,1024]{3,2,1,0:T(2,128)S(1)} %get-tuple-element.16), channel_id=1, source_target_pairs={{1,0},{2,1},{3,2},{5,4},{6,5},{7,6},{9,8},{10,9},{11,10},{13,12},{... | collective-permute-start | bytes 688136 | tf_op jit(solution)/shard_map/ppermute | solution.py:1121
  16.7 3.7 %collective-permute-start.2 = (f32[8,128]{1,0:T(8,128)S(1)}, f32[8,128]{1,0:T(8,128)S(1)}, u32[]{:S(2)}, u32[]{:S(2)}) collective-permute-start(f32[8,128]{1,0:T(8,128)S(1)} %label.1.refs_0_), channel_id=1, source_target_pairs={{0,4},{4,0},{8,12},{12,8},{16,20},{20,16},{24,28},{28,24},{1,5},{5... | collective-permute-start | bytes 12296 | tf_op jit(solution)/shard_map/ppermute | solution.py:1119
  18.4 12.2 %collective-permute-start.3 = (f32[8,128]{1,0:T(8,128)S(1)}, f32[8,128]{1,0:T(8,128)S(1)}, u32[]{:S(2)}, u32[]{:S(2)}) collective-permute-start(f32[8,128]{1,0:T(8,128)S(1)} %label.1.refs_0_), channel_id=1, source_target_pairs={{0,8},{4,12},{8,0},{12,4},{16,24},{20,28},{24,16},{28,20},{1,9},{5... | collective-permute-start | bytes 12296 | tf_op jit(solution)/shard_map/ppermute | solution.py:1119
  19.8 23.5 %collective-permute-start.4 = (f32[8,128]{1,0:T(8,128)S(1)}, f32[8,128]{1,0:T(8,128)S(1)}, u32[]{:S(2)}, u32[]{:S(2)}) collective-permute-start(f32[8,128]{1,0:T(8,128)S(1)} %label.1.refs_0_), channel_id=1, source_target_pairs={{0,12},{4,8},{8,4},{12,0},{16,28},{20,24},{24,20},{28,16},{1,13},{... | collective-permute-start | bytes 12296 | tf_op jit(solution)/shard_map/ppermute | solution.py:1119
  20.4 23.0 %collective-permute-start.5 = (f32[8,128]{1,0:T(8,128)S(1)}, f32[8,128]{1,0:T(8,128)S(1)}, u32[]{:S(2)}, u32[]{:S(2)}) collective-permute-start(f32[8,128]{1,0:T(8,128)S(1)} %label.1.refs_0_), channel_id=1, source_target_pairs={{0,16},{4,20},{8,24},{12,28},{16,0},{20,4},{24,8},{28,12},{1,17},{... | collective-permute-start | bytes 12296 | tf_op jit(solution)/shard_map/ppermute | solution.py:1119
  30.6 12.7 %collective-permute-start.6 = (f32[8,128]{1,0:T(8,128)S(1)}, f32[8,128]{1,0:T(8,128)S(1)}, u32[]{:S(2)}, u32[]{:S(2)}) collective-permute-start(f32[8,128]{1,0:T(8,128)S(1)} %label.1.refs_0_), channel_id=1, source_target_pairs={{0,20},{4,16},{8,28},{12,24},{16,4},{20,0},{24,12},{28,8},{1,21},{... | collective-permute-start | bytes 12296 | tf_op jit(solution)/shard_map/ppermute | solution.py:1119
  36.0 7.4 %collective-permute-start.7 = (f32[8,128]{1,0:T(8,128)S(1)}, f32[8,128]{1,0:T(8,128)S(1)}, u32[]{:S(2)}, u32[]{:S(2)}) collective-permute-start(f32[8,128]{1,0:T(8,128)S(1)} %label.1.refs_0_), channel_id=1, source_target_pairs={{0,24},{4,28},{8,16},{12,20},{16,8},{20,12},{24,0},{28,4},{1,25},{... | collective-permute-start | bytes 12296 | tf_op jit(solution)/shard_map/ppermute | solution.py:1119
  36.4 6.9 %collective-permute-start.8 = (f32[8,128]{1,0:T(8,128)S(1)}, f32[8,128]{1,0:T(8,128)S(1)}, u32[]{:S(2)}, u32[]{:S(2)}) collective-permute-start(f32[8,128]{1,0:T(8,128)S(1)} %label.1.refs_0_), channel_id=1, source_target_pairs={{0,28},{4,24},{8,20},{12,16},{16,12},{20,8},{24,4},{28,0},{1,29},{... | collective-permute-start | bytes 12296 | tf_op jit(solution)/shard_map/ppermute | solution.py:1119

commit v4 on v3

--- a/solution.py
+++ b/solution.py
@@ -451,6 +451,7 @@
 def first_kernel(n_dom, n_sub, macros, planes, cells):
     sides = 2 * macros
     blocks = 2 * planes
+    half = planes * sides
 
     def body(kappa_ref, mu_ref, zone_ref, source_ref, pay_ref, coef_ref, hold_ref, sems):
         k = lax.axis_index("sub")
@@ -548,7 +549,9 @@
             at = planes + p
             hold_ref[at * sides : (at + 1) * sides, :] = merge(res[p][1], res[p][2], spare[p], n2[p])
         copies = [
-            pltpu.make_async_copy(hold_ref, pay_ref.at[dest], sems.at[dest])
+            pltpu.make_async_copy(
+                hold_ref.at[pl.ds(dest % 2 * half, half)], pay_ref.at[dest], sems.at[dest]
+            )
             for dest in range(n_dom * n_sub)
         ]
         for copy in copies:
@@ -565,7 +568,7 @@
         name="first",
         in_specs=[smem, smem, vmem, vmem],
         out_shape=(
-            jax.ShapeDtypeStruct((n_dom * n_sub, blocks * sides, LANES), f32),
+            jax.ShapeDtypeStruct((n_dom * n_sub, half, LANES), f32),
             pltpu.VMEM((31, sides, LANES), f32),
         ),
         out_specs=(pl.BlockSpec(memory_space=pltpu.HBM), vmem),
@@ -874,17 +877,22 @@
     sides = 2 * macros
     n = n_dom * sides
 
-    def body(recv_ref, coef_ref, edge_in, pot_in, same_ref, weight_ref, field_ref, edge_ref, pot_ref, one_ref, two_ref, turn_ref):
+    def body(recv_ref, swap_ref, coef_ref, edge_in, pot_in, same_ref, weight_ref, field_ref, edge_ref, pot_ref, one_ref, two_ref, turn_ref):
         k = lax.axis_index("sub")
         d = lax.axis_index("dom")
         shape = (n, LANES)
         group = iota(shape, 1) & 3
         upper = (iota(shape, 0) % sides) >= macros
 
+        odd = (k & 1) == 1
+
         def rows_of(layer, at):
-            parts = [
-                recv_ref[e * n_sub + layer, at * sides : (at + 1) * sides, :] for e in range(n_dom)
-            ]
+            at, late = at % planes, at >= planes
+            parts = []
+            for e in range(n_dom):
+                rows = (e * n_sub + layer, slice(at * sides, (at + 1) * sides), slice(None))
+                mine, other = recv_ref[rows], swap_ref[rows]
+                parts.append(jnp.where(odd, mine, other) if late else jnp.where(odd, other, mine))
             return jnp.concatenate(parts, axis=0)
 
         same = same_ref[...]
@@ -1112,6 +1120,7 @@
     far = [pltpu.with_memory_space_constraint(v, pltpu.HBM) for v in (*tables, zone_ids, source)]
     pay, coef = first_kernel(*sizes)(*far)
     recv = lax.all_to_all(pay, ("dom", "sub"), 0, 0)
+    swapped = lax.ppermute(recv, "sub", [(i, i ^ 1) for i in range(n_sub)])
     labels = label_kernel(*sizes, *lists)(zone_ids, owner_dev, owner_group)
     labels = [labels]
     for i in range(1, n_dom):
@@ -1121,7 +1130,7 @@
     high = lax.ppermute(source[:, :, :HALO], "sub", down)
     edge, pot = inner_kernel(*sizes)(*tables, zone_ids, source, *near_core(low, high))
     fields = prepare_kernel(*sizes, *lists)(*tables, *near_core(*labels, pot))
-    return solve_kernel(*sizes)(*near_core(recv, coef, edge, pot, *fields))
+    return solve_kernel(*sizes)(*near_core(recv, swapped, coef, edge, pot, *fields))
 
 
 def fits_small(mesh, source, owner_dev, owner_group):

time: 50.5 us -> 59.1 us (1.17)
  blocking collectives: 0 us -> 22.7 us
  starting transfers between devices: 26 us -> 15.1 us
  waiting for transfers between devices: 7.86 us -> 4.52 us
    all_to_all x0 -> x1, blocking collectives: none -> 22.7 us  [local_small(): recv = lax.all_to_all(pay, ('dom', 'sub'), 0, 0)]
    all_to_all x1 -> x0, starting transfers between devices: 7.33 us -> none  [local_small(): recv = lax.all_to_all(pay, ('dom', 'sub'), 0, 0)]
    ppermute x7, starting transfers between devices: 15.2 us -> 10.7 us  [local_small(): labels.append(lax.ppermute(labels[0], 'dom', route))]
    ppermute x7, waiting for transfers between devices: 7.85 us -> 4.51 us  [local_small(): labels.append(lax.ppermute(labels[0], 'dom', route))]
    ppermute x1, starting transfers between devices: 2.17 us -> 3.05 us  [local_small(): low = lax.ppermute(source[:, :, planes - HALO:], 'sub', up)]
  transfers between devices with their start and end apart: 10 -> 10, of which waited for: 2 -> 3; matrix products, arithmetic and copies ran while one was open for 0% -> 0% of each run, Pallas kernels for 13% -> 11%
where the time goes in v4:
time: 59.1 us; the launch traced here: 58.8 us
  blocking collectives  22.7 us (38%)
  Pallas kernels  15.5 us (26%)
  starting transfers between devices  15.1 us (26%)
  waiting for transfers between devices  4.52 us (8%)
  between operations  0.79 us (1%)
    all_to_all x1, blocking collectives, local_small(): recv = lax.all_to_all(pay, ('dom', 'sub'), 0, 0)  22.7 us
    ppermute x7, starting transfers between devices, local_small(): labels.append(lax.ppermute(labels[0], 'dom', route))  10.7 us
    pallas_call x1, Pallas kernels, local_small(): pay, coef = first_kernel(*sizes)(*far)  4.76 us
    ppermute x7, waiting for transfers between devices, local_small(): labels.append(lax.ppermute(labels[0], 'dom', route))  4.51 us
    pallas_call x1, Pallas kernels, local_small(): solve_kernel(*sizes)(*near_core(recv, swapped, coef, edge, pot, *fields))  4.23 us
    pallas_call x1, Pallas kernels, local_small(): inner_kernel(*sizes)(*tables, zone_ids, source, *near_core(low, high))  3.57 us
    ppermute x1, starting transfers between devices, local_small(): low = lax.ppermute(source[:, :, planes - HALO:], 'sub', up)  3.05 us
    pallas_call x1, Pallas kernels, local_small(): fields = prepare_kernel(*sizes, *lists)(*tables, *near_core(*labels, pot))  2.72 us
  transfers between devices with their start and end apart: 10, of which 3 were waited for; matrix products, arithmetic and copies ran while one was open for 0% of the time, Pallas kernels for 11%

profile of v4, /device:TPU:0, one launch (start us, length us, event | category | flops | bytes accessed | tf_op | source)
XLA Modules:
  0.0 58.8 jit_solution(4972300784132808254)
XLA Ops:
  0.6 4.8 %first.1 = (f32[32,32,128]{2,1,0:T(8,128)S(1)}, f32[31,8,128]{2,1,0:T(8,128)S(1)}) custom-call(f32[7,16]{1,0:T(8,128)} %bitcast.2, f32[8,16]{1,0:T(8,128)} %bitcast.5, s32[4,1024]{1,0:T(4,128)} %zone_ref.5, f32[4,7,4,1024]{3,2,1,0:T(4,128)} %source_ref.3), custom_call_target="tpu_custom_call" | custom-call | tf_op jit(solution)/shard_map/first/pallas_call | solution.py:1121
  5.4 0.0 copy-start
  5.4 22.7 %all_to_all.5.recv_ref = f32[32,32,128]{2,1,0:T(8,128)S(1)} all-to-all(f32[32,32,128]{2,1,0:T(8,128)S(1)} %get-tuple-element.9), channel_id=1, replica_groups=mesh['dom'=8,'sub'=4] {'dom','sub'}, dimensions={0} | all-to-all | bytes 1048576 | tf_op jit(solution)/shard_map/all_to_all | solution.py:1122
  28.2 0.0 copy-start.1
  28.2 0.0 collective-permute-start
  28.2 0.0 copy-done
  28.2 0.2 fusion
  28.4 0.0 copy-start.4
  28.4 0.0 copy-start.5
  28.4 1.3 %collective-permute-start.2 = (f32[4,7,2,1024]{3,2,1,0:T(2,128)S(1)}, f32[4,7,2,1024]{3,2,1,0:T(2,128)S(1)}, u32[]{:S(2)}, u32[]{:S(2)}) collective-permute-start(f32[4,7,2,1024]{3,2,1,0:T(2,128)S(1)} %get-tuple-element.16), channel_id=1, source_target_pairs={{1,0},{2,1},{3,2},{5,4},{6,5},{7,6},{9,8},{10,9},{11,10},{13,12},{... | collective-permute-start | bytes 688136 | tf_op jit(solution)/shard_map/ppermute | solution.py:1130
  29.7 0.0 copy-start.2
  29.7 0.0 copy-start.3
  29.7 3.0 %collective-permute-start.1 = (f32[4,7,2,1024]{3,2,1,0:T(2,128)S(1)}, f32[4,7,2,1024]{3,2,1,0:T(2,128)S(1)}, u32[]{:S(2)}, u32[]{:S(2)}) collective-permute-start(f32[4,7,2,1024]{3,2,1,0:T(2,128)S(1)} %get-tuple-element.17), channel_id=1, source_target_pairs={{0,1},{1,2},{2,3},{4,5},{5,6},{6,7},{8,9},{9,10},{10,11},{12,13},{... | collective-permute-start | bytes 688136 | tf_op jit(solution)/shard_map/ppermute | solution.py:1129
  32.8 0.0 copy-done.1
  32.8 0.0 copy-done.4
  32.8 0.0 copy-done.5
  32.8 0.2 label.1.refs_0_
  33.0 1.8 %collective-permute-start.9 = (f32[8,128]{1,0:T(8,128)S(1)}, f32[8,128]{1,0:T(8,128)S(1)}, u32[]{:S(2)}, u32[]{:S(2)}) collective-permute-start(f32[8,128]{1,0:T(8,128)S(1)} %label.1.refs_0_), channel_id=1, source_target_pairs={{0,28},{4,24},{8,20},{12,16},{16,12},{20,8},{24,4},{28,0},{1,29},{... | collective-permute-start | bytes 12296 | tf_op jit(solution)/shard_map/ppermute | solution.py:1128
  34.7 2.7 %collective-permute-start.8 = (f32[8,128]{1,0:T(8,128)S(1)}, f32[8,128]{1,0:T(8,128)S(1)}, u32[]{:S(2)}, u32[]{:S(2)}) collective-permute-start(f32[8,128]{1,0:T(8,128)S(1)} %label.1.refs_0_), channel_id=1, source_target_pairs={{0,24},{4,28},{8,16},{12,20},{16,8},{20,12},{24,0},{28,4},{1,25},{... | collective-permute-start | bytes 12296 | tf_op jit(solution)/shard_map/ppermute | solution.py:1128
  37.5 1.8 %collective-permute-done.9.refs_7_ = f32[8,128]{1,0:T(8,128)S(1)} collective-permute-done((f32[8,128]{1,0:T(8,128)S(1)}, f32[8,128]{1,0:T(8,128)S(1)}, u32[]{:S(2)}, u32[]{:S(2)}) %collective-permute-start.9) | collective-permute-done | bytes 4128 | tf_op jit(solution)/shard_map/ppermute | solution.py:1128
  39.3 0.0 collective-permute-start.7
  39.3 0.8 %collective-permute-done.8.refs_6_ = f32[8,128]{1,0:T(8,128)S(1)} collective-permute-done((f32[8,128]{1,0:T(8,128)S(1)}, f32[8,128]{1,0:T(8,128)S(1)}, u32[]{:S(2)}, u32[]{:S(2)}) %collective-permute-start.8) | collective-permute-done | bytes 4128 | tf_op jit(solution)/shard_map/ppermute | solution.py:1128
  40.1 2.7 %collective-permute-start.6 = (f32[8,128]{1,0:T(8,128)S(1)}, f32[8,128]{1,0:T(8,128)S(1)}, u32[]{:S(2)}, u32[]{:S(2)}) collective-permute-start(f32[8,128]{1,0:T(8,128)S(1)} %label.1.refs_0_), channel_id=1, source_target_pairs={{0,16},{4,20},{8,24},{12,28},{16,0},{20,4},{24,8},{28,12},{1,17},{... | collective-permute-start | bytes 12296 | tf_op jit(solution)/shard_map/ppermute | solution.py:1128
  42.9 1.8 %collective-permute-done.7.refs_5_ = f32[8,128]{1,0:T(8,128)S(1)} collective-permute-done((f32[8,128]{1,0:T(8,128)S(1)}, f32[8,128]{1,0:T(8,128)S(1)}, u32[]{:S(2)}, u32[]{:S(2)}) %collective-permute-start.7) | collective-permute-done | bytes 4128 | tf_op jit(solution)/shard_map/ppermute | solution.py:1128
  44.7 0.0 collective-permute-start.5
  44.7 0.0 collective-permute-done.2.high_ref
  44.7 2.7 %collective-permute-start.4 = (f32[8,128]{1,0:T(8,128)S(1)}, f32[8,128]{1,0:T(8,128)S(1)}, u32[]{:S(2)}, u32[]{:S(2)}) collective-permute-start(f32[8,128]{1,0:T(8,128)S(1)} %label.1.refs_0_), channel_id=1, source_target_pairs={{0,8},{4,12},{8,0},{12,4},{16,24},{20,28},{24,16},{28,20},{1,9},{5... | collective-permute-start | bytes 12296 | tf_op jit(solution)/shard_map/ppermute | solution.py:1128
  47.4 0.0 collective-permute-done.1.low_ref
  47.4 0.8 %collective-permute-start.3 = (f32[8,128]{1,0:T(8,128)S(1)}, f32[8,128]{1,0:T(8,128)S(1)}, u32[]{:S(2)}, u32[]{:S(2)}) collective-permute-start(f32[8,128]{1,0:T(8,128)S(1)} %label.1.refs_0_), channel_id=1, source_target_pairs={{0,4},{4,0},{8,12},{12,8},{16,20},{20,16},{24,28},{28,24},{1,5},{5... | collective-permute-start | bytes 12296 | tf_op jit(solution)/shard_map/ppermute | solution.py:1128
  48.2 0.0 copy-done.2
  48.2 0.0 copy-done.3
  48.2 3.6 %inner.1 = (f32[4,7,4,1024]{3,2,1,0:T(4,128)S(1)}, f32[4,4,1024]{2,1,0:T(4,128)S(1)}) custom-call(f32[7,16]{1,0:T(8,128)S(1)} %bitcast.3, f32[8,16]{1,0:T(8,128)S(1)} %bitcast.6, s32[4,1024]{1,0:T(4,128)S(1)} %copy-done.1, f32[4,7,4,1024]{3,2,1,0:T(4,128)S(1)} %copy-done, f32[4,7,2,1024]{3,2,1,0:T(2,128)S(1)} %collective-permute-done.1.low_ref, ...), custom_call_target="tpu_custom_call" | custom-call | tf_op jit(solution)/shard_map/inner/pallas_call | solution.py:1131
  51.8 0.0 collective-permute-done.6.refs_4_
  51.8 0.0 collective-permute-done.5.refs_3_
  51.8 0.0 collective-permute-done.4.refs_2_
  51.9 0.0 collective-permute-done.3.refs_1_
  51.9 2.7 %prepare.1 = (bf16[256,256]{1,0:T(8,128)(2,1)S(1)}, f32[4,256,128]{2,1,0:T(8,128)S(1)}, f32[16,64,128]{2,1,0:T(8,128)S(1)}) custom-call(f32[7,16]{1,0:T(8,128)S(1)} %bitcast.4, f32[8,16]{1,0:T(8,128)S(1)} %bitcast.7, f32[8,128]{1,0:T(8,128)S(1)} %label.1.refs_0_, f32[8,128]{1,0:T(8,128)S(1)} %collective-permute-done.3.refs_1_, ...), custom_call_target="tpu_custom_call" | custom-call | tf_op jit(solution)/shard_map/prepare/pallas_call | solution.py:1132
  54.6 0.0 collective-permute-done.swap_ref
  54.6 4.2 %solve.1 = (f32[4,7,4,1024]{3,2,1,0:T(4,128)}, f32[4,4,1024]{2,1,0:T(4,128)}) custom-call(f32[32,32,128]{2,1,0:T(8,128)S(1)} %all_to_all.5.recv_ref, f32[32,32,128]{2,1,0:T(8,128)S(1)} %collective-permute-done.swap_ref, f32[31,8,128]{2,1,0:T(8,128)S(1)} %get-tuple-element.10.coef_ref, f32[4,7,4,1024]{3,2,1,0:T(4,128)S(1)} %get-tuple-element.11.edge_in, ...), custom_call_target="tpu_custom_call" | custom-call | tf_op jit(solution)/shard_map/solve/pallas_call | solution.py:1133
Async XLA Ops:
  5.4 22.8 %copy-start = (f32[4,7,4,1024]{3,2,1,0:T(4,128)S(1)}, f32[4,7,4,1024]{3,2,1,0:T(4,128)}, u32[]{:S(2)}) copy-start(f32[4,7,4,1024]{3,2,1,0:T(4,128)} %source_ref.3) | copy-start | bytes 1376260
  28.2 4.6 %copy-start.1 = (s32[4,1024]{1,0:T(4,128)S(1)}, s32[4,1024]{1,0:T(4,128)}, u32[]{:S(2)}) copy-start(s32[4,1024]{1,0:T(4,128)} %zone_ref.5) | copy-start | bytes 49156
  28.2 26.4 %collective-permute-start = (f32[32,32,128]{2,1,0:T(8,128)S(1)}, f32[32,32,128]{2,1,0:T(8,128)S(1)}, u32[]{:S(2)}, u32[]{:S(2)}) collective-permute-start(f32[32,32,128]{2,1,0:T(8,128)S(1)} %all_to_all.5.recv_ref), channel_id=1, source_target_pairs={{0,1},{1,0},{2,3},{3,2},{4,5},{5,4},{6,7},{7,6},{8,9},{9,8},{10,11... | collective-permute-start | bytes 1572872 | tf_op jit(solution)/shard_map/ppermute | solution.py:1123
  28.4 4.4 %copy-start.4 = (s32[1,32]{1,0:T(1,128)S(1)}, s32[1,32]{1,0:T(1,128)}, u32[]{:S(2)}) copy-start(s32[1,32]{1,0:T(1,128)} %owner_ref.1) | copy-start | bytes 388
  28.4 4.4 %copy-start.5 = (s32[1,32]{1,0:T(1,128)S(1)}, s32[1,32]{1,0:T(1,128)}, u32[]{:S(2)}) copy-start(s32[1,32]{1,0:T(1,128)} %group_ref.1) | copy-start | bytes 388
  28.4 16.4 %collective-permute-start.2 = (f32[4,7,2,1024]{3,2,1,0:T(2,128)S(1)}, f32[4,7,2,1024]{3,2,1,0:T(2,128)S(1)}, u32[]{:S(2)}, u32[]{:S(2)}) collective-permute-start(f32[4,7,2,1024]{3,2,1,0:T(2,128)S(1)} %get-tuple-element.16), channel_id=1, source_target_pairs={{1,0},{2,1},{3,2},{5,4},{6,5},{7,6},{9,8},{10,9},{11,10},{13,12},{... | collective-permute-start | bytes 688136 | tf_op jit(solution)/shard_map/ppermute | solution.py:1130
  29.7 18.6 %copy-start.2 = (f32[16,7]{0,1:T(8,128)S(1)}, f32[16,7]{0,1:T(8,128)}, u32[]{:S(2)}) copy-start(f32[16,7]{0,1:T(8,128)} %param.8) | copy-start | bytes 1348
  29.7 18.6 %copy-start.3 = (f32[16,8]{0,1:T(8,128)S(1)}, f32[16,8]{0,1:T(8,128)}, u32[]{:S(2)}) copy-start(f32[16,8]{0,1:T(8,128)} %param.9) | copy-start | bytes 1540
  29.7 17.7 %collective-permute-start.1 = (f32[4,7,2,1024]{3,2,1,0:T(2,128)S(1)}, f32[4,7,2,1024]{3,2,1,0:T(2,128)S(1)}, u32[]{:S(2)}, u32[]{:S(2)}) collective-permute-start(f32[4,7,2,1024]{3,2,1,0:T(2,128)S(1)} %get-tuple-element.17), channel_id=1, source_target_pairs={{0,1},{1,2},{2,3},{4,5},{5,6},{6,7},{8,9},{9,10},{10,11},{12,13},{... | collective-permute-start | bytes 688136 | tf_op jit(solution)/shard_map/ppermute | solution.py:1129
  33.0 6.3 %collective-permute-start.9 = (f32[8,128]{1,0:T(8,128)S(1)}, f32[8,128]{1,0:T(8,128)S(1)}, u32[]{:S(2)}, u32[]{:S(2)}) collective-permute-start(f32[8,128]{1,0:T(8,128)S(1)} %label.1.refs_0_), channel_id=1, source_target_pairs={{0,28},{4,24},{8,20},{12,16},{16,12},{20,8},{24,4},{28,0},{1,29},{... | collective-permute-start | bytes 12296 | tf_op jit(solution)/shard_map/ppermute | solution.py:1128
  34.7 5.4 %collective-permute-start.8 = (f32[8,128]{1,0:T(8,128)S(1)}, f32[8,128]{1,0:T(8,128)S(1)}, u32[]{:S(2)}, u32[]{:S(2)}) collective-permute-start(f32[8,128]{1,0:T(8,128)S(1)} %label.1.refs_0_), channel_id=1, source_target_pairs={{0,24},{4,28},{8,16},{12,20},{16,8},{20,12},{24,0},{28,4},{1,25},{... | collective-permute-start | bytes 12296 | tf_op jit(solution)/shard_map/ppermute | solution.py:1128
  39.3 5.4 %collective-permute-start.7 = (f32[8,128]{1,0:T(8,128)S(1)}, f32[8,128]{1,0:T(8,128)S(1)}, u32[]{:S(2)}, u32[]{:S(2)}) collective-permute-start(f32[8,128]{1,0:T(8,128)S(1)} %label.1.refs_0_), channel_id=1, source_target_pairs={{0,20},{4,16},{8,28},{12,24},{16,4},{20,0},{24,12},{28,8},{1,21},{... | collective-permute-start | bytes 12296 | tf_op jit(solution)/shard_map/ppermute | solution.py:1128
  40.1 11.7 %collective-permute-start.6 = (f32[8,128]{1,0:T(8,128)S(1)}, f32[8,128]{1,0:T(8,128)S(1)}, u32[]{:S(2)}, u32[]{:S(2)}) collective-permute-start(f32[8,128]{1,0:T(8,128)S(1)} %label.1.refs_0_), channel_id=1, source_target_pairs={{0,16},{4,20},{8,24},{12,28},{16,0},{20,4},{24,8},{28,12},{1,17},{... | collective-permute-start | bytes 12296 | tf_op jit(solution)/shard_map/ppermute | solution.py:1128
  44.7 7.1 %collective-permute-start.5 = (f32[8,128]{1,0:T(8,128)S(1)}, f32[8,128]{1,0:T(8,128)S(1)}, u32[]{:S(2)}, u32[]{:S(2)}) collective-permute-start(f32[8,128]{1,0:T(8,128)S(1)} %label.1.refs_0_), channel_id=1, source_target_pairs={{0,12},{4,8},{8,4},{12,0},{16,28},{20,24},{24,20},{28,16},{1,13},{... | collective-permute-start | bytes 12296 | tf_op jit(solution)/shard_map/ppermute | solution.py:1128
  44.7 7.1 %collective-permute-start.4 = (f32[8,128]{1,0:T(8,128)S(1)}, f32[8,128]{1,0:T(8,128)S(1)}, u32[]{:S(2)}, u32[]{:S(2)}) collective-permute-start(f32[8,128]{1,0:T(8,128)S(1)} %label.1.refs_0_), channel_id=1, source_target_pairs={{0,8},{4,12},{8,0},{12,4},{16,24},{20,28},{24,16},{28,20},{1,9},{5... | collective-permute-start | bytes 12296 | tf_op jit(solution)/shard_map/ppermute | solution.py:1128
  47.4 4.5 %collective-permute-start.3 = (f32[8,128]{1,0:T(8,128)S(1)}, f32[8,128]{1,0:T(8,128)S(1)}, u32[]{:S(2)}, u32[]{:S(2)}) collective-permute-start(f32[8,128]{1,0:T(8,128)S(1)} %label.1.refs_0_), channel_id=1, source_target_pairs={{0,4},{4,0},{8,12},{12,8},{16,20},{20,16},{24,28},{28,24},{1,5},{5... | collective-permute-start | bytes 12296 | tf_op jit(solution)/shard_map/ppermute | solution.py:1128

commit v5 on v4

--- a/solution.py
+++ b/solution.py
@@ -4,7 +4,6 @@
 from jax.experimental import pallas as pl
 from jax.experimental.pallas import tpu as pltpu
 from jax.sharding import PartitionSpec as P
-
 
 LAT = 32
 SWEEPS = 2
@@ -448,13 +447,14 @@
 NONE7 = [None] * 7
 
 
-def first_kernel(n_dom, n_sub, macros, planes, cells):
+def first_kernel(n_dom, n_sub, macros, planes, cells, slots, recv_rows):
     sides = 2 * macros
-    blocks = 2 * planes
-    half = planes * sides
-
-    def body(kappa_ref, mu_ref, zone_ref, source_ref, pay_ref, coef_ref, hold_ref, sems):
+    capacity = recv_rows // n_dom
+    half = (planes + 1) * sides
+
+    def body(kappa_ref, mu_ref, zone_ref, source_ref, owner_ref, group_ref, pay_ref, coef_ref, hold_ref, sems):
         k = lax.axis_index("sub")
+        d = lax.axis_index("dom")
         shape = (sides, LANES)
         sh = Strip(shape)
         row = iota(shape, 0)
@@ -545,13 +545,33 @@
         high = jnp.where(row < macros, row_roll(n2[planes + 1], macros), n1[planes])
         spare = [flagged(-1, res[-1][2]), high, n2[-1], n2[planes]]
         for p in range(planes):
-            hold_ref[p * sides : (p + 1) * sides, :] = merge(src[p][1], src[p][2], src[p][5], n1[p])
-            at = planes + p
-            hold_ref[at * sides : (at + 1) * sides, :] = merge(res[p][1], res[p][2], spare[p], n2[p])
+            rows = slice(p * sides, (p + 1) * sides)
+            hold_ref[0, rows, :] = merge(src[p][1], src[p][2], src[p][5], n1[p])
+            hold_ref[1, rows, :] = merge(res[p][1], res[p][2], spare[p], n2[p])
+        owner = owner_ref[...].astype(jnp.float32)
+        si, sj = iota((slots, slots), 0), iota((slots, slots), 1)
+        column = jnp.sum(jnp.where(si == sj, owner, 0.0), axis=1, keepdims=True)
+        lower = jnp.where((column == owner) & (si < sj), 1.0, 0.0)
+        position = jnp.sum(lower, axis=0, keepdims=True)
+        flat_index = owner * recv_rows + (d * capacity).astype(jnp.float32) + position
+        keyed = group_ref[...].astype(jnp.float32) + (d * recv_rows).astype(jnp.float32)
+
+        def spread_lanes(values):
+            count = values.shape[1]
+            place = iota((count, LANES), 0)
+            place = 32 * (place >> 3) + 4 * (place & 7) + 3
+            hot = jnp.where(place == iota((count, LANES), 1), 1.0, 0.0)
+            rows = jnp.broadcast_to(values, (sides, count))
+            return jnp.dot(rows, hot, precision=lax.Precision.HIGHEST)
+
+        index = jnp.where(row < macros, spread_lanes(flat_index), spread_lanes(keyed))
+        zone_f = zone.astype(jnp.float32)
+        label = jnp.where(group == 2, lane_roll(zone_f, -1), lane_roll(zone_f, 1))
+        label = jnp.where(group == 3, index, label)
+        for i in range(2):
+            hold_ref[i, planes * sides :, :] = label
         copies = [
-            pltpu.make_async_copy(
-                hold_ref.at[pl.ds(dest % 2 * half, half)], pay_ref.at[dest], sems.at[dest]
-            )
+            pltpu.make_async_copy(hold_ref.at[dest % 2], pay_ref.at[dest], sems.at[dest])
             for dest in range(n_dom * n_sub)
         ]
         for copy in copies:
@@ -566,55 +586,16 @@
         body,
         compiler_params=pltpu.CompilerParams(vmem_limit_bytes=VMEM_BYTES),
         name="first",
-        in_specs=[smem, smem, vmem, vmem],
+        in_specs=[smem, smem, vmem, vmem, vmem, vmem],
         out_shape=(
             jax.ShapeDtypeStruct((n_dom * n_sub, half, LANES), f32),
             pltpu.VMEM((31, sides, LANES), f32),
         ),
         out_specs=(pl.BlockSpec(memory_space=pltpu.HBM), vmem),
         scratch_shapes=[
-            pltpu.VMEM((blocks * sides, LANES), f32),
+            pltpu.VMEM((2, half, LANES), f32),
             pltpu.SemaphoreType.DMA((n_dom * n_sub,)),
         ],
-    )
-
-
-def label_kernel(n_dom, n_sub, macros, planes, cells, slots, recv_rows):
-    sides = 2 * macros
-    capacity = recv_rows // n_dom
-
-    def body(zone_ref, owner_ref, group_ref, pay_ref):
-        d = lax.axis_index("dom")
-        shape = (sides, LANES)
-        row = iota(shape, 0)
-        group = iota(shape, 1) & 3
-        owner = owner_ref[...].astype(jnp.float32)
-        si, sj = iota((slots, slots), 0), iota((slots, slots), 1)
-        column = jnp.sum(jnp.where(si == sj, owner, 0.0), axis=1, keepdims=True)
-        lower = jnp.where((column == owner) & (si < sj), 1.0, 0.0)
-        position = jnp.sum(lower, axis=0, keepdims=True)
-        flat_index = owner * recv_rows + (d * capacity).astype(jnp.float32) + position
-        keyed = group_ref[...].astype(jnp.float32) + (d * recv_rows).astype(jnp.float32)
-
-        def spread_lanes(values):
-            count = values.shape[1]
-            place = iota((count, LANES), 0)
-            place = 32 * (place >> 3) + 4 * (place & 7) + 3
-            hot = jnp.where(place == iota((count, LANES), 1), 1.0, 0.0)
-            rows = jnp.broadcast_to(values, (sides, count))
-            return jnp.dot(rows, hot, precision=lax.Precision.HIGHEST)
-
-        index = jnp.where(row < macros, spread_lanes(flat_index), spread_lanes(keyed))
-        zone = to_strip(zone_ref[...]).astype(jnp.float32)
-        block = jnp.where(group == 2, lane_roll(zone, -1), lane_roll(zone, 1))
-        block = jnp.where(group == 3, index, block)
-        pay_ref[...] = block
-
-    return pl.pallas_call(
-        body,
-        compiler_params=pltpu.CompilerParams(vmem_limit_bytes=VMEM_BYTES),
-        name="label",
-        out_shape=pltpu.VMEM((sides, LANES), jnp.float32),
     )
 
 
@@ -741,11 +722,9 @@
     n = n_dom * sides
     total = n * planes
 
-    def body(kappa_ref, mu_ref, *refs):
-        same_ref, weight_ref, field_ref, recv_ref = refs[n_dom + 1 :]
-        d = lax.axis_index("dom")
-        for i in range(n_dom):
-            recv_ref[d ^ i] = refs[i][...]
+    def body(kappa_ref, mu_ref, wide_ref, same_ref, weight_ref, field_ref, recv_ref):
+        for e in range(n_dom):
+            recv_ref[e] = wide_ref[e * lax.axis_size("sub"), planes * sides :, :]
         shape = (n, LANES)
         group = iota(shape, 1) & 3
         index = jnp.concatenate([recv_ref[e] for e in range(n_dom)], axis=0)
@@ -863,7 +842,7 @@
         body,
         compiler_params=pltpu.CompilerParams(vmem_limit_bytes=VMEM_BYTES),
         name="prepare",
-        in_specs=[smem, smem] + [vmem] * (n_dom + 1),
+        in_specs=[smem, smem, vmem],
         out_shape=(
             pltpu.VMEM((total, total), jnp.bfloat16),
             pltpu.VMEM((4, total, LANES), f32),
@@ -1117,19 +1096,14 @@
     up = [(i, i + 1) for i in range(n_sub - 1)]
     down = [(i + 1, i) for i in range(n_sub - 1)]
     tables = (kappa_table.T, mu_table.T)
-    far = [pltpu.with_memory_space_constraint(v, pltpu.HBM) for v in (*tables, zone_ids, source)]
-    pay, coef = first_kernel(*sizes)(*far)
+    far = [pltpu.with_memory_space_constraint(v, pltpu.HBM) for v in (*tables, zone_ids, source, owner_dev, owner_group)]
+    pay, coef = first_kernel(*sizes, *lists)(*far)
     recv = lax.all_to_all(pay, ("dom", "sub"), 0, 0)
     swapped = lax.ppermute(recv, "sub", [(i, i ^ 1) for i in range(n_sub)])
-    labels = label_kernel(*sizes, *lists)(zone_ids, owner_dev, owner_group)
-    labels = [labels]
-    for i in range(1, n_dom):
-        route = [(e, e ^ i) for e in range(n_dom)]
-        labels.append(lax.ppermute(labels[0], "dom", route))
     low = lax.ppermute(source[:, :, planes - HALO :], "sub", up)
     high = lax.ppermute(source[:, :, :HALO], "sub", down)
     edge, pot = inner_kernel(*sizes)(*tables, zone_ids, source, *near_core(low, high))
-    fields = prepare_kernel(*sizes, *lists)(*tables, *near_core(*labels, pot))
+    fields = prepare_kernel(*sizes, *lists)(*tables, *near_core(recv))
     return solve_kernel(*sizes)(*near_core(recv, swapped, coef, edge, pot, *fields))
 
 

time: 59.1 us -> 50.5 us (0.85)
  the two profiles are of different devices: /device:TPU:0 before, /device:TPU:1 now
where the time goes in v5:
time: 50.5 us; the launch traced here: 50.2 us
  blocking collectives  24.7 us (49%)
  Pallas kernels  15.7 us (31%)
  starting transfers between devices  6 us (12%)
  waiting for transfers between devices  2.95 us (6%)
  between operations  0.69 us (1%)
    all_to_all x1, blocking collectives, local_small(): recv = lax.all_to_all(pay, ('dom', 'sub'), 0, 0)  24.7 us
    pallas_call x1, Pallas kernels, local_small(): pay, coef = first_kernel(*sizes, *lists)(*far)  5.22 us
    pallas_call x1, Pallas kernels, local_small(): solve_kernel(*sizes)(*near_core(recv, swapped, coef, edge, pot, *fields))  4.21 us
    ppermute x1, starting transfers between devices, local_small(): low = lax.ppermute(source[:, :, planes - HALO:], 'sub', up)  3.58 us
    pallas_call x1, Pallas kernels, local_small(): inner_kernel(*sizes)(*tables, zone_ids, source, *near_core(low, high))  3.57 us
    pallas_call x1, Pallas kernels, local_small(): fields = prepare_kernel(*sizes, *lists)(*tables, *near_core(recv))  2.71 us
    ppermute x1, starting transfers between devices, local_small(): high = lax.ppermute(source[:, :, :HALO], 'sub', down)  1.99 us
    ppermute x1, waiting for transfers between devices, local_small(): high = lax.ppermute(source[:, :, :HALO], 'sub', down)  1.76 us
  transfers between devices with their start and end apart: 3, of which 2 were waited for; matrix products, arithmetic and copies ran while one was open for 0% of the time, Pallas kernels for 13%

profile of v5, /device:TPU:1, one launch (start us, length us, event | category | flops | bytes accessed | tf_op | source)
XLA Modules:
  0.0 50.2 jit_solution(1360629031744715903)
XLA Ops:
  0.6 5.2 %first.1 = (f32[32,40,128]{2,1,0:T(8,128)S(1)}, f32[31,8,128]{2,1,0:T(8,128)S(1)}) custom-call(f32[7,16]{1,0:T(8,128)} %bitcast.2, f32[8,16]{1,0:T(8,128)} %bitcast.5, s32[4,1024]{1,0:T(4,128)} %zone_ref.3, f32[4,7,4,1024]{3,2,1,0:T(4,128)} %source_ref.3, s32[1,32]{1,0:T(1,128)} %owner_ref.1, s32[1,32]{1,0:T(1,128)} %group_ref.1), custom_call_target="tpu_custom_call" | custom-call | tf_op jit(solution)/shard_map/first/pallas_call | solution.py:1100
  5.9 0.0 copy-start
  5.9 24.7 %all_to_all.5.wide_ref.recv_ref = f32[32,40,128]{2,1,0:T(8,128)S(1)} all-to-all(f32[32,40,128]{2,1,0:T(8,128)S(1)} %get-tuple-element.9), channel_id=1, replica_groups=mesh['dom'=8,'sub'=4] {'dom','sub'}, dimensions={0} | all-to-all | bytes 1310720 | tf_op jit(solution)/shard_map/all_to_all | solution.py:1101
  30.6 0.0 copy-start.1
  30.6 0.4 collective-permute-start
  31.0 0.0 copy-done
  31.0 0.0 copy-start.2
  31.0 0.0 copy-start.3
  31.0 0.2 fusion
  31.2 2.0 %collective-permute-start.2 = (f32[4,7,2,1024]{3,2,1,0:T(2,128)S(1)}, f32[4,7,2,1024]{3,2,1,0:T(2,128)S(1)}, u32[]{:S(2)}, u32[]{:S(2)}) collective-permute-start(f32[4,7,2,1024]{3,2,1,0:T(2,128)S(1)} %get-tuple-element.16), channel_id=1, source_target_pairs={{1,0},{2,1},{3,2},{5,4},{6,5},{7,6},{9,8},{10,9},{11,10},{13,12},{... | collective-permute-start | bytes 688136 | tf_op jit(solution)/shard_map/ppermute | solution.py:1104
  33.2 3.6 %collective-permute-start.1 = (f32[4,7,2,1024]{3,2,1,0:T(2,128)S(1)}, f32[4,7,2,1024]{3,2,1,0:T(2,128)S(1)}, u32[]{:S(2)}, u32[]{:S(2)}) collective-permute-start(f32[4,7,2,1024]{3,2,1,0:T(2,128)S(1)} %get-tuple-element.17), channel_id=1, source_target_pairs={{0,1},{1,2},{2,3},{4,5},{5,6},{6,7},{8,9},{9,10},{10,11},{12,13},{... | collective-permute-start | bytes 688136 | tf_op jit(solution)/shard_map/ppermute | solution.py:1103
  36.8 1.8 %collective-permute-done.2.high_ref = f32[4,7,2,1024]{3,2,1,0:T(2,128)S(1)} collective-permute-done((f32[4,7,2,1024]{3,2,1,0:T(2,128)S(1)}, f32[4,7,2,1024]{3,2,1,0:T(2,128)S(1)}, u32[]{:S(2)}, u32[]{:S(2)}) %collective-permute-start.2) | collective-permute-done | bytes 229408 | tf_op jit(solution)/shard_map/ppermute | solution.py:1104
  38.5 1.2 %collective-permute-done.1.low_ref = f32[4,7,2,1024]{3,2,1,0:T(2,128)S(1)} collective-permute-done((f32[4,7,2,1024]{3,2,1,0:T(2,128)S(1)}, f32[4,7,2,1024]{3,2,1,0:T(2,128)S(1)}, u32[]{:S(2)}, u32[]{:S(2)}) %collective-permute-start.1) | collective-permute-done | bytes 229408 | tf_op jit(solution)/shard_map/ppermute | solution.py:1103
  39.7 0.0 copy-done.1
  39.7 0.0 copy-done.2
  39.7 0.0 copy-done.3
  39.7 3.6 %inner.1 = (f32[4,7,4,1024]{3,2,1,0:T(4,128)S(1)}, f32[4,4,1024]{2,1,0:T(4,128)S(1)}) custom-call(f32[7,16]{1,0:T(8,128)S(1)} %bitcast.3, f32[8,16]{1,0:T(8,128)S(1)} %bitcast.6, s32[4,1024]{1,0:T(4,128)S(1)} %copy-done.1, f32[4,7,4,1024]{3,2,1,0:T(4,128)S(1)} %copy-done, f32[4,7,2,1024]{3,2,1,0:T(2,128)S(1)} %collective-permute-done.1.low_ref, ...), custom_call_target="tpu_custom_call" | custom-call | tf_op jit(solution)/shard_map/inner/pallas_call | solution.py:1105
  43.3 2.7 %prepare.1 = (bf16[256,256]{1,0:T(8,128)(2,1)S(1)}, f32[4,256,128]{2,1,0:T(8,128)S(1)}, f32[16,64,128]{2,1,0:T(8,128)S(1)}) custom-call(f32[7,16]{1,0:T(8,128)S(1)} %bitcast.4, f32[8,16]{1,0:T(8,128)S(1)} %bitcast.7, f32[32,40,128]{2,1,0:T(8,128)S(1)} %all_to_all.5.wide_ref.recv_ref), custom_call_target="tpu_custom_call" | custom-call | tf_op jit(solution)/shard_map/prepare/pallas_call | solution.py:1106
  46.0 0.0 collective-permute-done.swap_ref
  46.0 4.2 %solve.1 = (f32[4,7,4,1024]{3,2,1,0:T(4,128)}, f32[4,4,1024]{2,1,0:T(4,128)}) custom-call(f32[32,40,128]{2,1,0:T(8,128)S(1)} %all_to_all.5.wide_ref.recv_ref, f32[32,40,128]{2,1,0:T(8,128)S(1)} %collective-permute-done.swap_ref, f32[31,8,128]{2,1,0:T(8,128)S(1)} %get-tuple-element.10.coef_ref, f32[4,7,4,1024]{3,2,1,0:T(4,128)S(1)} %get-tuple-element.11.edge_in, ...), custom_call_target="tpu_custom_call" | custom-call | tf_op jit(solution)/shard_map/solve/pallas_call | solution.py:1107
Async XLA Ops:
  5.9 25.2 %copy-start = (f32[4,7,4,1024]{3,2,1,0:T(4,128)S(1)}, f32[4,7,4,1024]{3,2,1,0:T(4,128)}, u32[]{:S(2)}) copy-start(f32[4,7,4,1024]{3,2,1,0:T(4,128)} %source_ref.3) | copy-start | bytes 1376260
  30.6 9.1 %copy-start.1 = (s32[4,1024]{1,0:T(4,128)S(1)}, s32[4,1024]{1,0:T(4,128)}, u32[]{:S(2)}) copy-start(s32[4,1024]{1,0:T(4,128)} %zone_ref.3) | copy-start | bytes 49156
  30.6 15.4 %collective-permute-start = (f32[32,40,128]{2,1,0:T(8,128)S(1)}, f32[32,40,128]{2,1,0:T(8,128)S(1)}, u32[]{:S(2)}, u32[]{:S(2)}) collective-permute-start(f32[32,40,128]{2,1,0:T(8,128)S(1)} %all_to_all.5.wide_ref.recv_ref), channel_id=1, source_target_pairs={{0,1},{1,0},{2,3},{3,2},{4,5},{5,4},{6,7},{7,6},{8,9},{9,8},{10,11... | collective-permute-start | bytes 1966088 | tf_op jit(solution)/shard_map/ppermute | solution.py:1102
  31.0 8.7 %copy-start.2 = (f32[16,7]{0,1:T(8,128)S(1)}, f32[16,7]{0,1:T(8,128)}, u32[]{:S(2)}) copy-start(f32[16,7]{0,1:T(8,128)} %param.8) | copy-start | bytes 1348
  31.0 8.7 %copy-start.3 = (f32[16,8]{0,1:T(8,128)S(1)}, f32[16,8]{0,1:T(8,128)}, u32[]{:S(2)}) copy-start(f32[16,8]{0,1:T(8,128)} %param.9) | copy-start | bytes 1540
  31.2 7.3 %collective-permute-start.2 = (f32[4,7,2,1024]{3,2,1,0:T(2,128)S(1)}, f32[4,7,2,1024]{3,2,1,0:T(2,128)S(1)}, u32[]{:S(2)}, u32[]{:S(2)}) collective-permute-start(f32[4,7,2,1024]{3,2,1,0:T(2,128)S(1)} %get-tuple-element.16), channel_id=1, source_target_pairs={{1,0},{2,1},{3,2},{5,4},{6,5},{7,6},{9,8},{10,9},{11,10},{13,12},{... | collective-permute-start | bytes 688136 | tf_op jit(solution)/shard_map/ppermute | solution.py:1104
  33.2 6.5 %collective-permute-start.1 = (f32[4,7,2,1024]{3,2,1,0:T(2,128)S(1)}, f32[4,7,2,1024]{3,2,1,0:T(2,128)S(1)}, u32[]{:S(2)}, u32[]{:S(2)}) collective-permute-start(f32[4,7,2,1024]{3,2,1,0:T(2,128)S(1)} %get-tuple-element.17), channel_id=1, source_target_pairs={{0,1},{1,2},{2,3},{4,5},{5,6},{6,7},{8,9},{9,10},{10,11},{12,13},{... | collective-permute-start | bytes 688136 | tf_op jit(solution)/shard_map/ppermute | solution.py:1103
